TPU v7x, 32 devices: a whole 2x2x4 slice. The times are simulated.
32 devices in a mesh: dp: 8 (over z, y), fsdp: 4 (over x, core).
Axes of the slice: x: 2, y: 2, z: 4, core: 2. Of those that a mesh axis runs over, the one named last changes fastest.
Arguments:
- tokens: bfloat16 [8192, 768], P(('dp', 'fsdp')), may hold values from -6 to 6
- out_grad: bfloat16 [8192, 768], P(('dp', 'fsdp')), may hold values from -6 to 6
- mlm_mask: int32 [8192], P(('dp', 'fsdp')), may hold values 0 or 1
- live_mask: int32 [8192], P(('dp', 'fsdp')), may hold values 0 or 1
- doc_lengths: int32 [64, 4], P(('dp', 'fsdp')), may hold values from 1 to 64, 128 in all within a row
- layout_buckets: int32 [2, 8192, 128], P(None, ('dp', 'fsdp')), may hold values from 0 to 31
- attn_in: bfloat16 [2, 768, 2304], P(None, 'fsdp'), may hold values from -0.21875 to 0.21875
- attn_out: bfloat16 [2, 768, 768], P(None, 'fsdp'), may hold values from -0.875 to 0.875
- ffn_in: bfloat16 [2, 768, 3072], P(None, 'fsdp'), may hold values from -0.21875 to 0.21875
- ffn_out: bfloat16 [2, 3072, 768], P(None, 'fsdp'), may hold values from -0.109375 to 0.109375
- biases: bfloat16 [2, 6, 768], P(None, None, 'fsdp'), may hold values from -1 to 1
- ffn_in_bias: bfloat16 [2, 3072], P(None, 'fsdp'), may hold values from -1 to 1
- gains: bfloat16 [2, 2, 768], P(None, None, 'fsdp'), may hold values from 0.5 to 1.5
- tables: bfloat16 [2, 3, 32, 12], P(None, None, 'fsdp'), may hold values from -4 to 4
Outputs:
- layer_out: bfloat16 [2, 8192, 768], P(None, ('dp', 'fsdp'))
- input_grad: float32 [8192, 768], P(('dp', 'fsdp'))
- grad_attn_in: float32 [2, 768, 2304], P(None, 'fsdp')
- grad_attn_out: float32 [2, 768, 768], P(None, 'fsdp')
- grad_ffn_in: float32 [2, 768, 3072], P(None, 'fsdp')
- grad_ffn_out: float32 [2, 3072, 768], P(None, 'fsdp')
- grad_biases: float32 [2, 6, 768], P(None, None, 'fsdp')
- grad_ffn_in_bias: float32 [2, 3072], P(None, 'fsdp')
- grad_gains: float32 [2, 2, 768], P(None, None, 'fsdp')
- grad_tables: float32 [2, 3, 32, 12], P(None, None, 'fsdp')
Inputs may be any that keep to these rules, and one draw needn't show every extreme that they name: `doc_lengths`: the 4 lengths of each window sum to 128. `live_mask`: 1 marks a real token, 0 padding. `mlm_mask`: 1 marks a position whose output receives a gradient.
All inputs are finite; a program needn't handle non-finite values. No bound on the sum of `mlm_mask` or of `live_mask` on one device may be relied on, other than what follows from the above.
Results may differ from a plain program's by a relative error of at most 0.025.
Values may be sent and summed in bfloat16 or wider, within the bound.
A program may use at most 256 MiB of HBM per device.

v0:
```python
import jax
import jax.numpy as jnp
from jax import lax
from jax.sharding import PartitionSpec as P

H = 12
DH = 64
NB = 32
WIN = 128


EPSILON = 1e-05


def exact_gelu(values):
    return jax.nn.gelu(values, approximate=False)


def norm_forward(values, gain_row, shift_row):
    centre = values - jnp.mean(values, axis=-1, keepdims=True)
    spread = jnp.mean(centre * centre, axis=-1, keepdims=True)
    inverse = lax.rsqrt(spread + EPSILON)
    normed = centre * inverse
    return (normed * gain_row + shift_row, normed, inverse)


def norm_backward(incoming, normed, inverse, gain_row):
    scaled = incoming * gain_row
    centred = (
        scaled
        - jnp.mean(scaled, axis=-1, keepdims=True)
        - normed * jnp.mean(scaled * normed, axis=-1, keepdims=True)
    )
    return (centred * inverse, jnp.sum(incoming * normed, axis=0), jnp.sum(incoming, axis=0))


def geometry(doc_lengths, live_mask, layout_buckets):
    windows = doc_lengths.shape[0]
    positions = jnp.arange(WIN, dtype=jnp.int32)
    doc_ends = jnp.cumsum(doc_lengths, axis=1)
    document = jnp.sum((positions[None, :, None] >= doc_ends[:, None, :]).astype(jnp.int32), axis=2)
    live_rows = live_mask.reshape(windows, WIN) == 1
    diagonal = positions[:, None] == positions[None, :]
    pair_mask = (document[:, :, None] == document[:, None, :]) & (
        live_rows[:, None, :] | diagonal[None]
    )
    offset = jnp.clip(positions[None, :] - positions[:, None], -(NB // 2), NB // 2 - 1) + NB // 2
    buckets = jnp.arange(NB, dtype=jnp.int32)
    linear = (offset[None] == buckets[:, None, None]).astype(jnp.bfloat16)
    layout_rows = layout_buckets.reshape(2, windows, WIN, WIN)
    across = (layout_rows[:, :, None] == buckets[None, None, :, None, None]).astype(jnp.bfloat16)
    return (pair_mask, linear, across)


def pair_terms_of(bias_table, linear, across):
    terms = jnp.einsum("bij,bh->hij", linear, bias_table[0], preferred_element_type=jnp.float32)[
        None
    ]
    terms = terms + jnp.einsum(
        "wbij,bh->whij", across[0], bias_table[1], preferred_element_type=jnp.float32
    )
    return terms + jnp.einsum(
        "wbij,bh->whij", across[1], bias_table[2], preferred_element_type=jnp.float32
    )


def masked_scores(query_rows, key_rows, pair_terms, pair_mask):
    scores = (
        jnp.einsum("wihd,wjhd->whij", query_rows, key_rows, preferred_element_type=jnp.float32)
        + pair_terms
    )
    return jnp.where(pair_mask[:, None], scores, -1e30)


def fetch_forward(w_in, w_out, w_up, w_down, shifts, up_shift, gain_rows, bias_table):
    return (
        lax.all_gather(w_in, "fsdp", axis=0, tiled=True),
        lax.all_gather(w_out, "fsdp", axis=0, tiled=True),
        lax.all_gather(w_up, "fsdp", axis=0, tiled=True),
        lax.all_gather(w_down, "fsdp", axis=0, tiled=True),
        lax.all_gather(shifts, "fsdp", axis=1, tiled=True),
        lax.all_gather(up_shift, "fsdp", axis=0, tiled=True),
        lax.all_gather(gain_rows, "fsdp", axis=1, tiled=True),
        lax.all_gather(bias_table, "fsdp", axis=1, tiled=True),
    )


def fetch_backward(w_in, w_out, w_up, w_down, shifts, up_shift, gain_rows, bias_table):
    return (
        lax.all_gather(w_in, "fsdp", axis=0, tiled=True),
        lax.all_gather(w_out, "fsdp", axis=0, tiled=True),
        lax.all_gather(w_up, "fsdp", axis=0, tiled=True),
        lax.all_gather(w_down, "fsdp", axis=0, tiled=True),
        lax.all_gather(shifts, "fsdp", axis=1, tiled=True),
        lax.all_gather(up_shift, "fsdp", axis=0, tiled=True),
        lax.all_gather(gain_rows, "fsdp", axis=1, tiled=True),
        lax.all_gather(bias_table, "fsdp", axis=1, tiled=True),
    )


def layer_forward(inputs, weights, pair_mask, linear, across):
    w_in, w_out, w_up, w_down, shifts, up_shift, gain_rows, bias_table = weights
    shifts = shifts.astype(jnp.float32)
    gain_rows = gain_rows.astype(jnp.float32)
    rows = inputs.shape[0]
    windows = rows // WIN
    width = w_out.shape[0]
    scaling = DH ** (-0.5)
    projected = jnp.dot(inputs, w_in, preferred_element_type=jnp.float32)
    query_rows = (
        ((projected[:, :width] + shifts[0]) * scaling)
        .astype(jnp.bfloat16)
        .reshape(windows, WIN, H, DH)
    )
    key_rows = projected[:, width : 2 * width].astype(jnp.bfloat16).reshape(windows, WIN, H, DH)
    value_rows = (
        (projected[:, 2 * width :] + shifts[1]).astype(jnp.bfloat16).reshape(windows, WIN, H, DH)
    )
    pair_terms = pair_terms_of(bias_table, linear, across)
    scores = masked_scores(query_rows, key_rows, pair_terms, pair_mask)
    highest = jnp.max(scores, axis=-1, keepdims=True)
    exponent = jnp.exp(scores - highest)
    denominator = jnp.sum(exponent, axis=-1, keepdims=True)
    probs = exponent / denominator
    log_total = highest + jnp.log(denominator)
    mixed_rows = jnp.einsum(
        "whij,wjhd->wihd",
        probs.astype(jnp.bfloat16),
        value_rows,
        preferred_element_type=jnp.float32,
    )
    mixed_rows = mixed_rows.reshape(rows, width).astype(jnp.bfloat16)
    attended = jnp.dot(mixed_rows, w_out, preferred_element_type=jnp.float32) + shifts[2]
    first_norm, normed_first, inverse_first = norm_forward(
        inputs.astype(jnp.float32) + attended, gain_rows[0], shifts[3]
    )
    first_low = first_norm.astype(jnp.bfloat16)
    hidden = jnp.dot(first_low, w_up, preferred_element_type=jnp.float32) + up_shift.astype(
        jnp.float32
    )
    active = exact_gelu(hidden).astype(jnp.bfloat16)
    branch = jnp.dot(active, w_down, preferred_element_type=jnp.float32) + shifts[4]
    result, normed_second, inverse_second = norm_forward(
        first_norm + branch, gain_rows[1], shifts[5]
    )
    kept = (
        query_rows,
        key_rows,
        value_rows,
        pair_terms,
        log_total,
        mixed_rows,
        normed_first,
        inverse_first,
        first_low,
        hidden,
        active,
        normed_second,
        inverse_second,
    )
    return (result, kept)


def layer_backward(incoming, inputs, weights, kept, pair_mask, linear, across):
    w_in, w_out, w_up, w_down, shifts, up_shift, gain_rows, bias_table = weights
    gain_rows = gain_rows.astype(jnp.float32)
    (
        query_rows,
        key_rows,
        value_rows,
        pair_terms,
        log_total,
        mixed_rows,
        normed_first,
        inverse_first,
        first_low,
        hidden,
        active,
        normed_second,
        inverse_second,
    ) = kept
    rows = inputs.shape[0]
    width = w_out.shape[0]
    windows = rows // WIN
    scaling = DH ** (-0.5)
    grad_second, grad_gain_second, grad_shift_second = norm_backward(
        incoming, normed_second, inverse_second, gain_rows[1]
    )
    branch_low = grad_second.astype(jnp.bfloat16)
    grad_down = jnp.einsum("nf,nd->fd", active, branch_low, preferred_element_type=jnp.float32)
    grad_branch_shift = jnp.sum(branch_low.astype(jnp.float32), axis=0)
    grad_active = jnp.einsum("nd,fd->nf", branch_low, w_down, preferred_element_type=jnp.float32)
    hidden_low = jax.vjp(exact_gelu, hidden)[1](grad_active)[0].astype(jnp.bfloat16)
    grad_up = jnp.einsum("nd,nf->df", first_low, hidden_low, preferred_element_type=jnp.float32)
    grad_up_shift = jnp.sum(hidden_low.astype(jnp.float32), axis=0)
    grad_first = grad_second + jnp.einsum(
        "nf,df->nd", hidden_low, w_up, preferred_element_type=jnp.float32
    )
    grad_attended, grad_gain_first, grad_shift_first = norm_backward(
        grad_first, normed_first, inverse_first, gain_rows[0]
    )
    attended_low = grad_attended.astype(jnp.bfloat16)
    grad_out_weight = jnp.einsum(
        "nd,ne->de", mixed_rows, attended_low, preferred_element_type=jnp.float32
    )
    grad_attended_shift = jnp.sum(attended_low.astype(jnp.float32), axis=0)
    grad_mixed = jnp.einsum("ne,de->nd", attended_low, w_out, preferred_element_type=jnp.float32)
    grad_mixed = grad_mixed.astype(jnp.bfloat16).reshape(windows, WIN, H, DH)
    scores = masked_scores(query_rows, key_rows, pair_terms, pair_mask)
    probs = jnp.exp(scores - log_total)
    grad_probs = jnp.einsum(
        "wihd,wjhd->whij", grad_mixed, value_rows, preferred_element_type=jnp.float32
    )
    grad_value = jnp.einsum(
        "whij,wihd->wjhd",
        probs.astype(jnp.bfloat16),
        grad_mixed,
        preferred_element_type=jnp.float32,
    ).astype(jnp.bfloat16)
    grad_scores = (
        probs * (grad_probs - jnp.sum(probs * grad_probs, axis=-1, keepdims=True))
    ).astype(jnp.bfloat16)
    grad_query = (
        jnp.einsum(
            "whij,wjhd->wihd", grad_scores, key_rows, preferred_element_type=jnp.float32
        ).astype(jnp.bfloat16)
        * scaling
    )
    grad_key = jnp.einsum(
        "whij,wihd->wjhd", grad_scores, query_rows, preferred_element_type=jnp.float32
    ).astype(jnp.bfloat16)
    grad_qkv = jnp.concatenate(
        [
            grad_query.reshape(rows, width),
            grad_key.reshape(rows, width),
            grad_value.reshape(rows, width),
        ],
        axis=1,
    )
    grad_in_weight = jnp.einsum("nd,ne->de", inputs, grad_qkv, preferred_element_type=jnp.float32)
    grad_linear = jnp.einsum(
        "bij,whij->bh", linear, grad_scores, preferred_element_type=jnp.float32
    )
    grad_across_x = jnp.einsum(
        "wbij,whij->bh", across[0], grad_scores, preferred_element_type=jnp.float32
    )
    grad_across_y = jnp.einsum(
        "wbij,whij->bh", across[1], grad_scores, preferred_element_type=jnp.float32
    )
    grad_table = jnp.stack([grad_linear, grad_across_x, grad_across_y])
    grad_inputs = grad_attended + jnp.einsum(
        "ne,de->nd", grad_qkv, w_in, preferred_element_type=jnp.float32
    )
    grad_query_shift = jnp.sum(grad_query.reshape(rows, width).astype(jnp.float32), axis=0)
    grad_value_shift = jnp.sum(grad_value.reshape(rows, width).astype(jnp.float32), axis=0)
    grad_shifts = jnp.stack(
        [
            grad_query_shift,
            grad_value_shift,
            grad_attended_shift,
            grad_shift_first,
            grad_branch_shift,
            grad_shift_second,
        ]
    )
    grad_gain_rows = jnp.stack([grad_gain_first, grad_gain_second])
    grads = (
        grad_in_weight,
        grad_out_weight,
        grad_up,
        grad_down,
        grad_shifts,
        grad_up_shift,
        grad_gain_rows,
        grad_table,
    )
    return (grad_inputs, grads)


def local(
    tokens,
    out_grad,
    mlm_mask,
    live_mask,
    doc_lengths,
    layout_buckets,
    attn_in,
    attn_out,
    ffn_in,
    ffn_out,
    biases,
    ffn_in_bias,
    gains,
    tables,
):
    pair_mask, linear, across = geometry(doc_lengths, live_mask, layout_buckets)
    layer_total = attn_in.shape[0]
    current = tokens
    layer_inputs = []
    kept_list = []
    fetched_list = []
    outputs = []
    for layer_index in range(layer_total):
        fetched = fetch_forward(
            attn_in[layer_index],
            attn_out[layer_index],
            ffn_in[layer_index],
            ffn_out[layer_index],
            biases[layer_index],
            ffn_in_bias[layer_index],
            gains[layer_index],
            tables[layer_index],
        )
        result, kept = layer_forward(current, fetched, pair_mask, linear, across)
        layer_inputs.append(current)
        kept_list.append(kept)
        fetched_list.append(fetched)
        current = result.astype(jnp.bfloat16)
        outputs.append(current)
    grad_inputs = out_grad.astype(jnp.float32) * mlm_mask.astype(jnp.float32)[:, None]
    shard_list = []
    for layer_index in reversed(range(layer_total)):
        fetched = fetch_backward(
            attn_in[layer_index],
            attn_out[layer_index],
            ffn_in[layer_index],
            ffn_out[layer_index],
            biases[layer_index],
            ffn_in_bias[layer_index],
            gains[layer_index],
            tables[layer_index],
        )
        grad_inputs, grads = layer_backward(
            grad_inputs,
            layer_inputs[layer_index],
            fetched,
            kept_list[layer_index],
            pair_mask,
            linear,
            across,
        )
        parts = (
            lax.psum_scatter(
                grads[0].astype(jnp.bfloat16), "fsdp", scatter_dimension=0, tiled=True
            ).astype(jnp.float32),
            lax.psum_scatter(
                grads[1].astype(jnp.bfloat16), "fsdp", scatter_dimension=0, tiled=True
            ).astype(jnp.float32),
            lax.psum_scatter(
                grads[2].astype(jnp.bfloat16), "fsdp", scatter_dimension=0, tiled=True
            ).astype(jnp.float32),
            lax.psum_scatter(
                grads[3].astype(jnp.bfloat16), "fsdp", scatter_dimension=0, tiled=True
            ).astype(jnp.float32),
            lax.psum_scatter(
                grads[4].astype(jnp.bfloat16), "fsdp", scatter_dimension=1, tiled=True
            ).astype(jnp.float32),
            lax.psum_scatter(
                grads[5].astype(jnp.bfloat16), "fsdp", scatter_dimension=0, tiled=True
            ).astype(jnp.float32),
            lax.psum_scatter(
                grads[6].astype(jnp.bfloat16), "fsdp", scatter_dimension=1, tiled=True
            ).astype(jnp.float32),
            lax.psum_scatter(
                grads[7].astype(jnp.bfloat16), "fsdp", scatter_dimension=1, tiled=True
            ).astype(jnp.float32),
        )
        shard_list.insert(0, parts)
    stacked = [jnp.stack([parts[member] for parts in shard_list]) for member in range(8)]
    stacked = lax.psum(
        (
            stacked[0],
            stacked[1],
            stacked[2],
            stacked[3],
            stacked[4],
            stacked[5],
            stacked[6],
            stacked[7],
        ),
        "dp",
    )
    return (
        jnp.stack(outputs),
        grad_inputs,
        stacked[0],
        stacked[1],
        stacked[2],
        stacked[3],
        stacked[4],
        stacked[5],
        stacked[6],
        stacked[7],
    )


def solution(mesh):
    return jax.shard_map(
        local,
        mesh=mesh,
        in_specs=(
            P(("dp", "fsdp"), None),
            P(("dp", "fsdp"), None),
            P(("dp", "fsdp")),
            P(("dp", "fsdp")),
            P(("dp", "fsdp"), None),
            P(None, ("dp", "fsdp"), None),
            P(None, "fsdp", None),
            P(None, "fsdp", None),
            P(None, "fsdp", None),
            P(None, "fsdp", None),
            P(None, None, "fsdp"),
            P(None, "fsdp"),
            P(None, None, "fsdp"),
            P(None, None, "fsdp", None),
        ),
        out_specs=(
            P(None, ("dp", "fsdp"), None),
            P(("dp", "fsdp"), None),
            P(None, "fsdp", None),
            P(None, "fsdp", None),
            P(None, "fsdp", None),
            P(None, "fsdp", None),
            P(None, None, "fsdp"),
            P(None, "fsdp"),
            P(None, None, "fsdp"),
            P(None, None, "fsdp", None),
        ),
        check_vma=False,
    )
```

profile of v0, /device:TPU:0, one launch (start us, length us, event | category | flops | bytes accessed | tf_op | source)
XLA Modules:
  0.0 1245.4 jit_solution(14112566530570059108)
XLA Ops:
  20.0 6.3 all-gather.2
  41.4 6.9 all-gather.1
  48.7 13.4 %slice_reduce_fusion.8 = (f32[768]{0:T(1024)S(1)}, f32[768]{0:T(1024)}, f32[768]{0:T(1024)}, f32[768]{0:T(1024)}, f32[768]{0:T(1024)}, /*index=5*/f32[768]{0:T(1024)}) fusion(f32[1,6,768]{1,0,2:T(1,128)S(1)} %convert_element_type.318), kind=kLoop, calls=%fused_computation.240 | loop fusion | bytes 36864 | tf_op jit(solution)/shard_map/slice | solution.py:144
  71.5 8.5 all-gather.4
  92.1 9.6 all-gather.9
  102.1 13.4 %slice_reduce_fusion = (f32[768]{0:T(1024)}, f32[768]{0:T(1024)}, f32[768]{0:T(1024)}, f32[768]{0:T(1024)}, f32[768]{0:T(1024)}, /*index=5*/f32[768]{0:T(1024)}) fusion(f32[1,6,768]{1,0,2:T(1,128)S(1)} %convert_element_type.321), kind=kLoop, calls=%fused_computation.232 | loop fusion | bytes 36864 | tf_op jit(solution)/shard_map/slice | solution.py:144
  121.6 9.1 all-gather.12
  155.3 11.9 multiply_convert_fusion.1
  171.9 8.4 all-gather.33.cloned.1.call-done
  191.9 7.2 all-gather.35.cloned.1.call-done
  203.7 34.4 %all-gather.37.cloned.1.call-done = bf16[1,768,3072]{2,1,0:T(8,128)(2,1)} async-done(((bf16[1,192,3072]{2,1,0:T(8,128)(2,1)}), bf16[1,768,3072]{2,1,0:T(8,128)(2,1)}) %all-gather.37.cloned.1.call-update) | async-done | bytes 4718608 | tf_op jit(solution)/shard_map/all_gather | solution.py:79
  238.2 12.2 multiply_convert_fusion
  250.4 26.8 %all-gather.39.cloned.1.call-done = bf16[1,3072,768]{2,1,0:T(8,128)(2,1)} async-done(((bf16[1,768,768]{2,1,0:T(8,128)(2,1)}), bf16[1,3072,768]{2,1,0:T(8,128)(2,1)}) %all-gather.39.cloned.1.call-update) | async-done | bytes 4718608 | tf_op jit(solution)/shard_map/all_gather | solution.py:80
  374.9 38.2 %reduce-scatter.37.cloned.1.call-done = bf16[192,2304]{1,0:T(8,128)(2,1)} async-done(((bf16[768,2304]{1,0:T(8,128)(2,1)}), bf16[192,2304]{1,0:T(8,128)(2,1)}) %reduce-scatter.37.cloned.1.call-update) | async-done | bytes 884752
  414.7 41.9 %reduce-scatter.39.cloned.1.call-done = bf16[192,2304]{1,0:T(8,128)(2,1)} async-done(((bf16[768,2304]{1,0:T(8,128)(2,1)}), bf16[192,2304]{1,0:T(8,128)(2,1)}) %reduce-scatter.39.cloned.1.call-update) | async-done | bytes 884752
  462.9 44.2 %reduce-scatter.29.cloned.1.call-done = bf16[192,3072]{1,0:T(8,128)(2,1)} async-done(((bf16[768,3072]{1,0:T(8,128)(2,1)}), bf16[192,3072]{1,0:T(8,128)(2,1)}) %reduce-scatter.29.cloned.1.call-update) | async-done | bytes 1179664 | tf_op jit(solution)/shard_map/reduce_scatter | solution.py:349
  507.1 51.0 %reduce-scatter.31.cloned.1.call-done = bf16[192,3072]{1,0:T(8,128)(2,1)} async-done(((bf16[768,3072]{1,0:T(8,128)(2,1)}), bf16[192,3072]{1,0:T(8,128)(2,1)}) %reduce-scatter.31.cloned.1.call-update) | async-done | bytes 1179664 | tf_op jit(solution)/shard_map/reduce_scatter | solution.py:349
  562.2 46.3 %reduce-scatter.35.cloned.1.call-done = bf16[768,768]{1,0:T(8,128)(2,1)} async-done(((bf16[3072,768]{1,0:T(8,128)(2,1)}), bf16[768,768]{1,0:T(8,128)(2,1)}) %reduce-scatter.35.cloned.1.call-update) | async-done | bytes 1179664 | tf_op jit(solution)/shard_map/reduce_scatter | solution.py:352
  608.4 50.4 %reduce-scatter.33.cloned.1.call-done = bf16[768,768]{1,0:T(8,128)(2,1)} async-done(((bf16[3072,768]{1,0:T(8,128)(2,1)}), bf16[768,768]{1,0:T(8,128)(2,1)}) %reduce-scatter.33.cloned.1.call-update) | async-done | bytes 1179664 | tf_op jit(solution)/shard_map/reduce_scatter | solution.py:352
  682.7 11.1 all-reduce.6
  704.0 21.3 %reduce-scatter.41.cloned.1.call-done = bf16[192,6]{1,0:T(8,128)(2,1)} async-done(((bf16[768,6]{1,0:T(8,128)(2,1)}), bf16[192,6]{1,0:T(8,128)(2,1)}) %reduce-scatter.41.cloned.1.call-update) | async-done | bytes 2320
  726.2 21.2 %reduce-scatter.43.cloned.1.call-done = bf16[192,6]{1,0:T(8,128)(2,1)} async-done(((bf16[768,6]{1,0:T(8,128)(2,1)}), bf16[192,6]{1,0:T(8,128)(2,1)}) %reduce-scatter.43.cloned.1.call-update) | async-done | bytes 2320
  748.3 40.5 %all-reduce.4 = (f32[2,6,192]{2,1,0:T(8,128)S(1)}, f32[2,768]{1,0:T(2,128)}, f32[2,2,192]{2,1,0:T(2,128)}, f32[2,3,8,12]{3,1,2,0:T(4,128)S(1)}) all-reduce(f32[2,6,192]{2,1,0:T(8,128)S(1)} %maximum_convert_fusion.5, f32[2,768]{1,0:T(2,128)S(1)} %maximum_convert_fusion.6, ...), channel_id=1, replica_groups=mesh['dp'=8,'fsdp'=4] {'dp'}, use_global_device_ids=true, to_apply=%region_50.51 | all-reduce | flops 5184 | bytes 41472 | tf_op jit(solution)/shard_map/psum | solution.py:370
  790.0 433.4 %all-reduce.9.cloned.1.call-done = (f32[2,192,2304]{1,2,0:T(8,128)}, f32[2,192,768]{2,1,0:T(8,128)}, f32[2,192,3072]{2,1,0:T(8,128)}, f32[2,768,768]{2,1,0:T(8,128)}) async-done(((f32[2,192,2304]{1,2,0:T(8,128)}, f32[2,192,768]{2,1,0:T(8,128)}, f32[2,192,3072]{2,1,0:T(8,128)}, f32[2,768,768]{2,1,0:T(8,128)}), (f32[2,192,2304]{1,2,0:T(8,128)}, f32[2,192,768]{2,1,0:T(8,128)}, f32[2,192,3072]{2,1,0:T(8,128)}, ...) | async-done | bytes 14155792 | tf_op jit(solution)/shard_map/psum | solution.py:370
  (501 shorter events, 260.0 us)
Async XLA Ops:
  7.2 136.0 %all-gather.25.cloned.1.call-start = ((), (), s32[]{:S(2)}) async-start(), calls=%async_computation.18 | async-start | bytes 4423680 | tf_op jit(solution)/shard_map/all_gather | solution.py:77
  10.2 142.8 %all-gather.27.cloned.1.call-start = ((), (), s32[]{:S(2)}) async-start(), calls=%async_computation.19 | async-start | bytes 1474560 | tf_op jit(solution)/shard_map/all_gather | solution.py:78
  11.1 144.2 %all-gather.29.cloned.1.call-start = ((), (), s32[]{:S(2)}) async-start(), calls=%async_computation.20 | async-start | bytes 5898240 | tf_op jit(solution)/shard_map/all_gather | solution.py:79
  12.8 154.4 %all-gather.31.cloned.1.call-start = ((), (), s32[]{:S(2)}) async-start(), calls=%async_computation.21 | async-start | bytes 5898240 | tf_op jit(solution)/shard_map/all_gather | solution.py:80
  16.1 164.2 %all-gather.33.cloned.1.call-start = ((), (), s32[]{:S(2)}) async-start(), calls=%async_computation.22 | async-start | bytes 4423680 | tf_op jit(solution)/shard_map/all_gather | solution.py:77
  16.7 182.5 %all-gather.35.cloned.1.call-start = ((), (), s32[]{:S(2)}) async-start(), calls=%async_computation.23 | async-start | bytes 1474560 | tf_op jit(solution)/shard_map/all_gather | solution.py:78
  17.3 220.9 %all-gather.37.cloned.1.call-start = ((), (), s32[]{:S(2)}) async-start(), calls=%async_computation.24 | async-start | bytes 5898240 | tf_op jit(solution)/shard_map/all_gather | solution.py:79
  18.0 259.2 %all-gather.39.cloned.1.call-start = ((), (), s32[]{:S(2)}) async-start(), calls=%async_computation.25 | async-start | bytes 5898240 | tf_op jit(solution)/shard_map/all_gather | solution.py:80
  18.8 353.9 %reduce-scatter.25.cloned.1.call-start = ((), (), s32[]{:S(2)}) async-start(), calls=%async_computation.12 | async-start | bytes 1474560 | tf_op jit(solution)/shard_map/reduce_scatter | solution.py:346
  118.5 24.7 %copy-start.30 = (bf16[256,768]{1,0:T(8,128)(2,1)S(1)}, bf16[256,768]{1,0:T(8,128)(2,1)}, u32[]{:S(2)}) copy-start(bf16[256,768]{1,0:T(8,128)(2,1)} %param.14) | copy-start | bytes 1179652
  120.2 22.3 %copy-start.61 = (pred[128,128]{0,1:T(8,128)(4,1)S(1)}, pred[128,128]{0,1:T(8,128)(4,1)}, u32[]{:S(2)}) copy-start(pred[128,128]{0,1:T(8,128)(4,1)} %iota_compare_fusion.22) | copy-start | bytes 49156
  120.2 22.3 %copy-start.88 = (s32[2,128]{1,0:T(2,128)S(1)}, s32[2,128]{1,0:T(2,128)}, u32[]{:S(2)}) copy-start(s32[2,128]{1,0:T(2,128)} %convert_reduce_fusion.2) | copy-start | bytes 3076
  315.8 56.9 %reduce-scatter.27.cloned.1.call-start = ((), (), s32[]{:S(2)}) async-start(), calls=%async_computation.13 | async-start | bytes 1474560 | tf_op jit(solution)/shard_map/reduce_scatter | solution.py:346
  322.7 90.4 %reduce-scatter.37.cloned.1.call-start = ((), (), s32[]{:S(2)}) async-start(), calls=%async_computation.26 | async-start | bytes 4423680
  338.5 118.0 %reduce-scatter.39.cloned.1.call-start = ((), (), s32[]{:S(2)}) async-start(), calls=%async_computation.27 | async-start | bytes 4423680
  342.9 164.2 %reduce-scatter.29.cloned.1.call-start = ((), (), s32[]{:S(2)}) async-start(), calls=%async_computation.14 | async-start | bytes 5898240 | tf_op jit(solution)/shard_map/reduce_scatter | solution.py:349
  349.2 208.9 %reduce-scatter.31.cloned.1.call-start = ((), (), s32[]{:S(2)}) async-start(), calls=%async_computation.15 | async-start | bytes 5898240 | tf_op jit(solution)/shard_map/reduce_scatter | solution.py:349
  355.6 252.8 %reduce-scatter.35.cloned.1.call-start = ((), (), s32[]{:S(2)}) async-start(), calls=%async_computation.17 | async-start | bytes 5898240 | tf_op jit(solution)/shard_map/reduce_scatter | solution.py:352
  361.8 297.0 %reduce-scatter.33.cloned.1.call-start = ((), (), s32[]{:S(2)}) async-start(), calls=%async_computation.16 | async-start | bytes 5898240 | tf_op jit(solution)/shard_map/reduce_scatter | solution.py:352
  368.0 331.2 %reduce-scatter.45.cloned.1.call-start = ((), (), s32[]{:S(2)}) async-start(), calls=%async_computation.30 | async-start | bytes 245760
  369.0 334.1 %reduce-scatter.47.cloned.1.call-start = ((), (), s32[]{:S(2)}) async-start(), calls=%async_computation.31 | async-start | bytes 245760
  370.0 355.4 %reduce-scatter.41.cloned.1.call-start = ((), (), s32[]{:S(2)}) async-start(), calls=%async_computation.28 | async-start | bytes 245760
  371.2 376.3 %reduce-scatter.43.cloned.1.call-start = ((), (), s32[]{:S(2)}) async-start(), calls=%async_computation.29 | async-start | bytes 245760
  372.4 851.1 %all-reduce.9.cloned.1.call-start = ((), (), s32[]{:S(2)}) async-start(), calls=%async_computation.32 | async-start | bytes 30670848 | tf_op jit(solution)/shard_map/psum | solution.py:370
  (115 other events, 554.2 us)
Sparse Core Ops, SparseCore 0:
  10.3 33.7 all-gather.24
  45.6 17.4 all-gather.26
  65.2 41.0 all-gather.28
  107.7 40.3 all-gather.30
  149.5 30.7 all-gather.32
  181.7 17.4 all-gather.34
  200.7 37.4 all-gather.36
  239.7 37.4 all-gather.38
  315.9 25.6 reduce-scatter.24
  344.0 25.6 reduce-scatter.26
  372.8 40.3 reduce-scatter.36
  416.1 40.3 reduce-scatter.38
  459.1 47.9 reduce-scatter.28
  510.0 47.9 reduce-scatter.30
  560.4 47.9 reduce-scatter.34
  610.8 47.9 reduce-scatter.32
  661.1 19.7 reduce-scatter.44
  683.2 19.8 reduce-scatter.46
  705.6 19.7 reduce-scatter.40
  727.6 19.7 reduce-scatter.42
  752.8 470.5 all-reduce.8
where the time goes:
time: 1250 us
  waiting for transfers between devices  830 us (66%)
  local copies, waits for them, and re-layouts  129 us (10%)
  matrix products  125 us (10%)
  blocking collectives  109 us (9%)
  other arithmetic  32.7 us (3%)
  between operations  17.8 us (1%)
    psum x1, waiting for transfers between devices, local(): lax.psum((stacked[0], stacked[1], stacked[2], stacked[3], stacked[4], sta...  433 us
    unnamed x27, waiting for transfers between devices  128 us
    reduce_scatter x2, waiting for transfers between devices, local(): lax.psum_scatter(grads[3].astype(jnp.bfloat16), 'fsdp', scatter_dimension...  96.7 us
    reduce_scatter x2, waiting for transfers between devices, local(): lax.psum_scatter(grads[2].astype(jnp.bfloat16), 'fsdp', scatter_dimension...  95.1 us
    unnamed x264, local copies, waits for them, and re-layouts  46.8 us
    psum x1, blocking collectives, local(): lax.psum((stacked[0], stacked[1], stacked[2], stacked[3], stacked[4], sta...  40.5 us
    all_gather x2, waiting for transfers between devices, fetch_forward(): lax.all_gather(w_up, 'fsdp', axis=0, tiled=True)  34.5 us
    slice x2, local copies, waits for them, and re-layouts, layer_forward(): shifts[5]  26.8 us
  transfers between devices with their start and end apart: 21, of which 14 were waited for; matrix products, arithmetic and copies ran while one was open for 18% of the time, Pallas kernels for 0%

commit v1 on v0

--- a/solution.py
+++ b/solution.py
@@ -1,6 +1,10 @@
+import functools
+
 import jax
 import jax.numpy as jnp
 from jax import lax
+from jax.experimental import pallas as pl
+from jax.experimental.pallas import tpu as pltpu
 from jax.sharding import PartitionSpec as P
 
 H = 12
@@ -10,6 +14,7 @@
 
 
 EPSILON = 1e-05
+LAG = 2
 
 
 def exact_gelu(values):
@@ -73,19 +78,6 @@
 
 
 def fetch_forward(w_in, w_out, w_up, w_down, shifts, up_shift, gain_rows, bias_table):
-    return (
-        lax.all_gather(w_in, "fsdp", axis=0, tiled=True),
-        lax.all_gather(w_out, "fsdp", axis=0, tiled=True),
-        lax.all_gather(w_up, "fsdp", axis=0, tiled=True),
-        lax.all_gather(w_down, "fsdp", axis=0, tiled=True),
-        lax.all_gather(shifts, "fsdp", axis=1, tiled=True),
-        lax.all_gather(up_shift, "fsdp", axis=0, tiled=True),
-        lax.all_gather(gain_rows, "fsdp", axis=1, tiled=True),
-        lax.all_gather(bias_table, "fsdp", axis=1, tiled=True),
-    )
-
-
-def fetch_backward(w_in, w_out, w_up, w_down, shifts, up_shift, gain_rows, bias_table):
     return (
         lax.all_gather(w_in, "fsdp", axis=0, tiled=True),
         lax.all_gather(w_out, "fsdp", axis=0, tiled=True),
@@ -275,6 +267,242 @@
         grad_table,
     )
     return (grad_inputs, grads)
+
+
+MESH = pl.DeviceIdType.MESH
+CHUNK_TILES = 1
+
+
+def add_rows(target, other):
+    target[...] = (target[...].astype(jnp.float32) + other[...].astype(jnp.float32)).astype(
+        jnp.bfloat16
+    )
+
+
+def reduce_kernel(
+    high, count, grads, out, own, core_in, x_in, y_in, z_in, full, load_sem, core_sem,
+    x_sem, y_sem, z_sem, zg_sem, yg_sem, sent, out_sem,
+):
+    dp = lax.axis_index("dp")
+    shard = lax.axis_index("fsdp")
+    y_at, z_at = lax.rem(dp, 2), lax.div(dp, 2)
+    x_at, core = lax.div(shard, 2), lax.rem(shard, 2)
+    core_peer = (dp, x_at * 2 + 1 - core)
+    x_peer = (dp, (1 - x_at) * 2 + core)
+    y_peer = (z_at * 2 + 1 - y_at, shard)
+    z_of = [lax.rem(z_at + step, high) for step in range(high)]
+    z_from = [lax.rem(z_at + high - step, high) for step in range(high)]
+    z_peers = [(z_of[step] * 2 + y_at, shard) for step in range(high)]
+    chunk = own.shape[2]
+    half = chunk // 2
+    piece = half // high
+
+    barrier = pltpu.get_barrier_semaphore()
+    peers = [core_peer, x_peer, y_peer] + z_peers[1:]
+    for peer in peers:
+        pl.semaphore_signal(barrier, inc=1, device_id=peer, device_id_type=MESH)
+    pl.semaphore_wait(barrier, len(peers))
+
+    def remote(source, target, send_at, receive, peer):
+        return pltpu.make_async_remote_copy(
+            src_ref=source, dst_ref=target, send_sem=sent.at[send_at], recv_sem=receive,
+            device_id=peer, device_id_type=MESH,
+        )
+
+    def rows_of(k, wanted):
+        return grads.at[wanted, pl.ds(pl.multiple_of(k * chunk, chunk), chunk), :]
+
+    def load(k, j):
+        wanted = (x_at if j == 0 else 1 - x_at) * 2 + core
+        return pltpu.make_async_copy(rows_of(k, wanted), own.at[k, j], load_sem.at[k, j])
+
+    def core_send(k, j):
+        wanted = (x_at if j == 0 else 1 - x_at) * 2 + 1 - core
+        return remote(rows_of(k, wanted), core_in.at[k, j], 0, core_sem.at[k, j], core_peer)
+
+    def x_send(k):
+        return remote(own.at[k, 1], x_in.at[k], 1, x_sem.at[k], x_peer)
+
+    def y_rows(side):
+        return pl.ds(pl.multiple_of(side * half, half), half)
+
+    def y_send(k):
+        return remote(own.at[k, 0, y_rows(1 - y_at)], y_in.at[k], 2, y_sem.at[k], y_peer)
+
+    def z_rows(at):
+        return pl.ds(pl.multiple_of(y_at * half + at * piece, piece), piece)
+
+    def z_send(k, step):
+        return remote(
+            own.at[k, 0, z_rows(z_of[step])], z_in.at[k, step - 1], 3,
+            z_sem.at[k, step - 1], z_peers[step],
+        )
+
+    def zg_send(k, step):
+        mine = full.at[k, z_rows(z_at)]
+        return remote(mine, mine, 4, zg_sem.at[k, step - 1], z_peers[step])
+
+    def zg_arrival(k, step):
+        theirs = full.at[k, z_rows(z_from[step])]
+        return remote(theirs, theirs, 4, zg_sem.at[k, step - 1], z_peers[step])
+
+    def yg_send(k):
+        mine = full.at[k, y_rows(y_at)]
+        return remote(mine, mine, 5, yg_sem.at[k], y_peer)
+
+    def store(k):
+        return pltpu.make_async_copy(
+            full.at[k], out.at[pl.ds(pl.multiple_of(k * chunk, chunk), chunk), :], out_sem.at[k]
+        )
+
+    @pl.loop(0, count)
+    def _(k):
+        for j in (1, 0):
+            core_send(k, j).start()
+            load(k, j).start()
+
+    def stage_core(k):
+        for j in (1, 0):
+            load(k, j).wait()
+            core_send(k, j).wait_recv()
+            add_rows(own.at[k, j], core_in.at[k, j])
+            if j == 1:
+                x_send(k).start()
+
+    def stage_x(k):
+        x_send(k).wait_recv()
+        add_rows(own.at[k, 0], x_in.at[k])
+        y_send(k).start()
+
+    def stage_y(k):
+        y_send(k).wait_recv()
+        add_rows(own.at[k, 0, y_rows(y_at)], y_in.at[k])
+        for step in range(1, high):
+            z_send(k, step).start()
+
+    def stage_z(k):
+        total = own[k, 0, z_rows(z_at), :].astype(jnp.float32)
+        for step in range(1, high):
+            z_send(k, step).wait_recv()
+            total = total + z_in[k, step - 1].astype(jnp.float32)
+        full[k, z_rows(z_at), :] = total.astype(jnp.bfloat16)
+        for step in range(1, high):
+            zg_send(k, step).start()
+
+    def stage_spread(k):
+        for step in range(1, high):
+            zg_arrival(k, step).wait_recv()
+        yg_send(k).start()
+
+    def stage_store(k):
+        yg_send(k).wait_recv()
+        store(k).start()
+
+    stages = (stage_core, stage_x, stage_y, stage_z, stage_spread, stage_store)
+    lags = (0, LAG, 2 * LAG, 3 * LAG, 4 * LAG, 5 * LAG)
+
+    @pl.loop(0, count + lags[-1])
+    def _(t):
+        for stage, lag in zip(stages, lags):
+            k = t - lag
+
+            @pl.when((k >= 0) & (k < count))
+            def _():
+                stage(k)
+
+    def all_sent(source, target, send_at, peer):
+        remote(source, target, send_at, x_sem.at[0], peer).wait_send()
+
+    all_sent(own, core_in, 0, core_peer)
+    all_sent(x_in, x_in, 1, x_peer)
+    all_sent(y_in, y_in, 2, y_peer)
+    all_sent(z_in, z_in, 3, z_peers[1])
+    all_sent(z_in, z_in, 4, z_peers[1])
+    all_sent(y_in, y_in, 5, y_peer)
+
+    @pl.loop(0, count)
+    def _(k):
+        store(k).wait()
+
+
+def reduce_gradients(grads, group):
+    shards, rows, width = grads.shape
+    high = group // 2
+    chunk = chunk_rows(group)
+    count = rows // chunk
+    piece = chunk // group
+    buffers = [
+        (count, 2, chunk, width),
+        (count, 2, chunk, width),
+        (count, chunk, width),
+        (count, chunk // 2, width),
+        (count, high - 1, piece, width),
+        (count, chunk, width),
+    ]
+    semaphores = [(count, 2), (count, 2), (count,), (count,), (count, high - 1),
+                  (count, high - 1), (count,), (6,), (count,)]
+    return pl.pallas_call(
+        functools.partial(reduce_kernel, high, count),
+        out_shape=jax.ShapeDtypeStruct((rows, width), jnp.bfloat16),
+        in_specs=[pl.BlockSpec(memory_space=pltpu.MemorySpace.HBM)],
+        out_specs=pl.BlockSpec(memory_space=pltpu.MemorySpace.HBM),
+        scratch_shapes=[pltpu.VMEM(shape, jnp.bfloat16) for shape in buffers]
+        + [pltpu.SemaphoreType.DMA(shape) for shape in semaphores],
+        compiler_params=pltpu.CompilerParams(
+            collective_id=1, has_side_effects=True, vmem_limit_bytes=64 * 1024 * 1024 - 65536
+        ),
+    )(grads)
+
+
+def chunk_rows(group):
+    return 16 * CHUNK_TILES * group
+
+
+def pack_gradients(grad_list, shards, group):
+    blocks, smalls = [], []
+    for grads in grad_list:
+        w_in, w_out, w_up, w_down, shifts, up_shift, gain_rows, bias_table = grads
+        width = w_out.shape[1]
+        for member in (w_in, w_out, w_up, w_down):
+            member = member.astype(jnp.bfloat16)
+            depth = member.shape[0] // shards
+            member = member.reshape(shards, depth, member.shape[1] // width, width)
+            blocks.append(jnp.swapaxes(member, 1, 2).reshape(shards, -1, width))
+        smalls.append(jnp.swapaxes(shifts.reshape(6, shards, -1), 0, 1).reshape(shards, -1))
+        smalls.append(up_shift.reshape(shards, -1))
+        smalls.append(jnp.swapaxes(gain_rows.reshape(2, shards, -1), 0, 1).reshape(shards, -1))
+        smalls.append(jnp.swapaxes(bias_table.reshape(3, shards, -1), 0, 1).reshape(shards, -1))
+    small = jnp.concatenate(smalls, axis=1)
+    rows = sum(block.shape[1] for block in blocks)
+    chunk = chunk_rows(group)
+    total = -(-(rows + -(-small.shape[1] // width)) // chunk) * chunk
+    small = jnp.pad(small, ((0, 0), (0, (total - rows) * width - small.shape[1])))
+    blocks.append(small.reshape(shards, total - rows, width).astype(jnp.bfloat16))
+    return jnp.concatenate(blocks, axis=1), (len(grad_list), rows, shards)
+
+
+def unpack_gradients(reduced, shapes):
+    layers, rows, shards = shapes
+    width = reduced.shape[1]
+    per_layer = rows // layers
+    depth = width // shards
+    body = reduced[:rows].astype(jnp.float32).reshape(layers, per_layer, width)
+    spans = []
+    start = 0
+    for blocks in (3, 1, 4):
+        part = body[:, start : start + blocks * depth].reshape(layers, blocks, depth, width)
+        spans.append(jnp.swapaxes(part, 1, 2).reshape(layers, depth, blocks * width))
+        start += blocks * depth
+    spans.append(body[:, start:])
+    small = reduced[rows:].astype(jnp.float32).reshape(-1)
+    sizes = (6 * depth, width, 2 * depth, 3 * (NB // shards) * H)
+    small = small[: layers * sum(sizes)].reshape(layers, -1)
+    forms = ((6, depth), (width,), (2, depth), (3, NB // shards, H))
+    start = 0
+    for size, form in zip(sizes, forms):
+        spans.append(small[:, start : start + size].reshape((layers,) + form))
+        start += size
+    return tuple(spans)
 
 
 def local(
@@ -320,78 +548,19 @@
     grad_inputs = out_grad.astype(jnp.float32) * mlm_mask.astype(jnp.float32)[:, None]
     shard_list = []
     for layer_index in reversed(range(layer_total)):
-        fetched = fetch_backward(
-            attn_in[layer_index],
-            attn_out[layer_index],
-            ffn_in[layer_index],
-            ffn_out[layer_index],
-            biases[layer_index],
-            ffn_in_bias[layer_index],
-            gains[layer_index],
-            tables[layer_index],
-        )
         grad_inputs, grads = layer_backward(
             grad_inputs,
             layer_inputs[layer_index],
-            fetched,
+            fetched_list[layer_index],
             kept_list[layer_index],
             pair_mask,
             linear,
             across,
         )
-        parts = (
-            lax.psum_scatter(
-                grads[0].astype(jnp.bfloat16), "fsdp", scatter_dimension=0, tiled=True
-            ).astype(jnp.float32),
-            lax.psum_scatter(
-                grads[1].astype(jnp.bfloat16), "fsdp", scatter_dimension=0, tiled=True
-            ).astype(jnp.float32),
-            lax.psum_scatter(
-                grads[2].astype(jnp.bfloat16), "fsdp", scatter_dimension=0, tiled=True
-            ).astype(jnp.float32),
-            lax.psum_scatter(
-                grads[3].astype(jnp.bfloat16), "fsdp", scatter_dimension=0, tiled=True
-            ).astype(jnp.float32),
-            lax.psum_scatter(
-                grads[4].astype(jnp.bfloat16), "fsdp", scatter_dimension=1, tiled=True
-            ).astype(jnp.float32),
-            lax.psum_scatter(
-                grads[5].astype(jnp.bfloat16), "fsdp", scatter_dimension=0, tiled=True
-            ).astype(jnp.float32),
-            lax.psum_scatter(
-                grads[6].astype(jnp.bfloat16), "fsdp", scatter_dimension=1, tiled=True
-            ).astype(jnp.float32),
-            lax.psum_scatter(
-                grads[7].astype(jnp.bfloat16), "fsdp", scatter_dimension=1, tiled=True
-            ).astype(jnp.float32),
-        )
-        shard_list.insert(0, parts)
-    stacked = [jnp.stack([parts[member] for parts in shard_list]) for member in range(8)]
-    stacked = lax.psum(
-        (
-            stacked[0],
-            stacked[1],
-            stacked[2],
-            stacked[3],
-            stacked[4],
-            stacked[5],
-            stacked[6],
-            stacked[7],
-        ),
-        "dp",
-    )
-    return (
-        jnp.stack(outputs),
-        grad_inputs,
-        stacked[0],
-        stacked[1],
-        stacked[2],
-        stacked[3],
-        stacked[4],
-        stacked[5],
-        stacked[6],
-        stacked[7],
-    )
+        shard_list.insert(0, grads)
+    packed, shapes = pack_gradients(shard_list, lax.axis_size("fsdp"), lax.axis_size("dp"))
+    reduced = reduce_gradients(packed, lax.axis_size("dp"))
+    return (jnp.stack(outputs), grad_inputs) + unpack_gradients(reduced, shapes)
 
 
 def solution(mesh):

time: 1250 us -> 728 us (0.58)
  waiting for transfers between devices: 830 us -> 71 us
  Pallas kernels: 0 us -> 191 us
  local copies, waits for them, and re-layouts: 129 us -> 239 us
  blocking collectives: 109 us -> 57.4 us
    psum x1 -> x0, waiting for transfers between devices: 433 us -> none  [local(): lax.psum((stacked[0], stacked[1], stacked[2], stacked[3], stacked[4], sta...]
    reduce_scatter x6 -> x0, waiting for transfers between devices: 192 us -> none  [the longest x2 96.7 us: local(): lax.psum_scatter(grads[3].astype(jnp.bfloat16), 'fsdp', scatter_dimension...]
    pallas_call x0 -> x1, Pallas kernels: none -> 191 us  [reduce_gradients(): pl.pallas_call(functools.partial(reduce_kernel, high, count), out_shape=j...]
    unnamed x27 -> x8, waiting for transfers between devices: 128 us -> 2.51 us
    reshape x0 -> x22, local copies, waits for them, and re-layouts: none -> 70.5 us  [the longest x6 44.8 us: pack_gradients(): member = member.reshape(shards, depth, member.shape[1] // width, width)]
    psum x1 -> x0, blocking collectives: 40.5 us -> none  [local(): lax.psum((stacked[0], stacked[1], stacked[2], stacked[3], stacked[4], sta...]
    another operation x14 -> x2, other arithmetic: 15.7 us -> 1.91 us  [local(): return (jnp.stack(outputs), grad_inputs) + unpack_gradients(reduced, shapes)]
    another operation x14, local copies, waits for them, and re-layouts: 0.47 us -> 13.7 us  [layer_backward(): jnp.stack([grad_query_shift, grad_value_shift, grad_attended_shift, grad_...]
  transfers between devices with their start and end apart: 21 -> 8, of which waited for: 14 -> 4; matrix products, arithmetic and copies ran while one was open for 18% -> 19% of each run, Pallas kernels for 0% -> 0%
where the time goes in v1:
time: 728 us; the launch traced here: 720 us
  local copies, waits for them, and re-layouts  239 us (33%)
  Pallas kernels  191 us (26%)
  matrix products  120 us (16%)
  waiting for transfers between devices  71 us (10%)
  blocking collectives  57.4 us (8%)
  other arithmetic  25.3 us (3%)
  between operations  15.8 us (2%)
    pallas_call x1, Pallas kernels, reduce_gradients(): pl.pallas_call(functools.partial(reduce_kernel, high, count), out_shape=j...  191 us
    reshape x6, local copies, waits for them, and re-layouts, pack_gradients(): member = member.reshape(shards, depth, member.shape[1] // width, width)  44.8 us
    unnamed x289, local copies, waits for them, and re-layouts  34.6 us
    all_gather x2, waiting for transfers between devices, fetch_forward(): lax.all_gather(w_up, 'fsdp', axis=0, tiled=True)  33.5 us
    slice x2, local copies, waits for them, and re-layouts, layer_forward(): shifts[5]  26.8 us
    all_gather x2, waiting for transfers between devices, fetch_forward(): lax.all_gather(w_down, 'fsdp', axis=0, tiled=True)  26.7 us
    dot_general x2, matrix products, layer_forward(): jnp.dot(first_low, w_up, preferred_element_type=jnp.float32)  24.2 us
    all_gather x2, blocking collectives, fetch_forward(): lax.all_gather(gain_rows, 'fsdp', axis=1, tiled=True)  18.4 us
  transfers between devices with their start and end apart: 8, of which 4 were waited for; matrix products, arithmetic and copies ran while one was open for 19% of the time, Pallas kernels for 0%

profile of v1, /device:TPU:0, one launch (start us, length us, event | category | flops | bytes accessed | tf_op | source)
XLA Modules:
  0.0 720.5 jit_solution(2734301977217787375)
XLA Ops:
  18.7 6.2 all-gather.10
  30.0 5.9 all-gather.2
  43.2 7.0 all-gather.9
  50.6 13.4 %slice_reduce_fusion = (f32[768]{0:T(1024)}, f32[768]{0:T(1024)}, f32[768]{0:T(1024)}, f32[768]{0:T(1024)}, f32[768]{0:T(1024)}, /*index=5*/f32[768]{0:T(1024)}) fusion(f32[1,6,768]{1,0,2:T(1,128)S(1)} %convert_element_type.312), kind=kLoop, calls=%fused_computation.224 | loop fusion | bytes 36864 | tf_op jit(solution)/shard_map/slice | solution.py:136
  64.0 5.2 all-gather.14
  78.1 9.7 %all-gather.1 = bf16[1,6,768]{1,0,2:T(2,128)(2,1)S(1)} all-gather(bf16[1,6,192]{1,0,2:T(2,128)(2,1)S(1)} %copy.420), channel_id=3, replica_groups=mesh['dp'=8,'fsdp'=4] {'fsdp'}, dimensions={2}, use_global_device_ids=true | all-gather | bytes 11520 | tf_op jit(solution)/shard_map/all_gather | solution.py:86
  88.2 13.4 %slice_reduce_fusion.8 = (f32[768]{0:T(1024)S(1)}, f32[768]{0:T(1024)}, f32[768]{0:T(1024)}, f32[768]{0:T(1024)}, f32[768]{0:T(1024)}, /*index=5*/f32[768]{0:T(1024)}) fusion(f32[1,6,768]{1,0,2:T(1,128)S(1)} %convert_element_type.309), kind=kLoop, calls=%fused_computation.232 | loop fusion | bytes 36864 | tf_op jit(solution)/shard_map/slice | solution.py:136
  101.6 5.2 all-gather.6
  114.1 9.0 %all-gather.4 = bf16[1,2,768]{1,0,2:T(2,128)(2,1)S(1)} all-gather(bf16[1,2,192]{1,0,2:T(2,128)(2,1)S(1)} %copy.424), channel_id=6, replica_groups=mesh['dp'=8,'fsdp'=4] {'fsdp'}, dimensions={2}, use_global_device_ids=true | all-gather | bytes 3840 | tf_op jit(solution)/shard_map/all_gather | solution.py:88
  128.3 9.3 %all-gather.12 = bf16[1,2,768]{1,0,2:T(2,128)(2,1)S(1)} all-gather(bf16[1,2,192]{1,0,2:T(2,128)(2,1)S(1)} %copy.429), channel_id=14, replica_groups=mesh['dp'=8,'fsdp'=4] {'fsdp'}, dimensions={2}, use_global_device_ids=true | all-gather | bytes 3840 | tf_op jit(solution)/shard_map/all_gather | solution.py:88
  159.9 11.8 %multiply_convert_fusion.1 = (bf16[256,3072]{1,0:T(8,128)(2,1)}, f32[256,3072]{1,0:T(8,128)}, f32[256,3072]{1,0:T(8,128)}) fusion(f32[3072]{0:T(1024)} %bitcast.397, bf16[1,768,3072]{2,1,0:T(8,128)(2,1)} %all-gather.29.cloned.1.call-done, f32[256,768]{1,0:T(8,128)S(1)} %get-tuple-element.126, f32[768]{0:T(1024)} %get-tuple-element.78, ...), kind=kOutput, calls=%fused_computation.64 | convolution fusion | flops 1260847104 | bytes 13389824 | tf_op jit(solution)/shard_map/dot_general | solution.py:130
  204.5 33.5 %all-gather.37.cloned.1.call-done = bf16[1,768,3072]{2,1,0:T(8,128)(2,1)} async-done(((bf16[1,192,3072]{2,1,0:T(8,128)(2,1)}), bf16[1,768,3072]{2,1,0:T(8,128)(2,1)}) %all-gather.37.cloned.1.call-update) | async-done | bytes 4718608 | tf_op jit(solution)/shard_map/all_gather | solution.py:84
  238.0 12.3 %multiply_convert_fusion = (bf16[256,3072]{1,0:T(8,128)(2,1)}, f32[256,3072]{1,0:T(8,128)}, f32[256,3072]{1,0:T(8,128)}) fusion(f32[3072]{0:T(1024)} %bitcast.396, bf16[1,768,3072]{2,1,0:T(8,128)(2,1)} %all-gather.37.cloned.1.call-done, f32[256,768]{1,0:T(8,128)} %copy-done.9, f32[768]{0:T(1024)} %get-tuple-element.70, f32[768]{0:T(1024)S(1)} %get-tuple-element.67, ...), kind=kOutput, calls=%fused_computation.51 | convolution fusion | flops 1260847104 | bytes 13389824 | tf_op jit(solution)/shard_map/dot_general | solution.py:130
  250.3 26.7 %all-gather.39.cloned.1.call-done = bf16[1,3072,768]{2,1,0:T(8,128)(2,1)} async-done(((bf16[1,768,768]{2,1,0:T(8,128)(2,1)}), bf16[1,3072,768]{2,1,0:T(8,128)(2,1)}) %all-gather.39.cloned.1.call-update) | async-done | bytes 4718608 | tf_op jit(solution)/shard_map/all_gather | solution.py:85
  363.8 8.7 %reshape.409 = bf16[4,192,3,768]{3,2,1,0:T(4,128)(2,1)} reshape(bf16[768,2304]{1,0:T(8,128)(2,1)} %copy.374) | data formatting | bytes 7077888 | tf_op jit(solution)/shard_map/reshape | solution.py:469
  377.6 10.1 %reshape.411 = bf16[4,192,4,768]{3,2,1,0:T(4,128)(2,1)} reshape(bf16[768,3072]{1,0:T(8,128)(2,1)} %convolution_convert_fusion.4) | data formatting | bytes 9437184 | tf_op jit(solution)/shard_map/reshape | solution.py:469
  387.8 5.5 copy.376
  393.3 5.3 reshape.413
  401.5 9.7 %reshape.415 = bf16[4,192,4,768]{3,2,1,0:T(4,128)(2,1)} reshape(bf16[768,3072]{1,0:T(8,128)(2,1)} %convolution_convert_fusion.1) | data formatting | bytes 9437184 | tf_op jit(solution)/shard_map/reshape | solution.py:469
  411.3 5.3 copy.378
  484.8 190.9 %shard_map.213 = bf16[4736,768]{1,0:T(8,128)(2,1)} custom-call(bf16[4,4736,768]{2,1,0:T(8,128)(2,1)} %bitcast_dynamic-update-slice_fusion.grads), custom_call_target="tpu_custom_call" | custom-call | tf_op jit(solution)/shard_map/pallas_call | solution.py:444
  687.8 6.6 copy.548
  694.4 6.6 reshape.428
  701.0 5.3 copy.430
  (534 shorter events, 281.9 us)
Async XLA Ops:
  7.2 136.7 %all-gather.25.cloned.1.call-start = ((), (), s32[]{:S(2)}) async-start(), calls=%async_computation | async-start | bytes 4423680 | tf_op jit(solution)/shard_map/all_gather | solution.py:82
  10.2 147.2 %all-gather.27.cloned.1.call-start = ((), (), s32[]{:S(2)}) async-start(), calls=%async_computation.1 | async-start | bytes 1474560 | tf_op jit(solution)/shard_map/all_gather | solution.py:83
  11.1 148.8 %all-gather.29.cloned.1.call-start = ((), (), s32[]{:S(2)}) async-start(), calls=%async_computation.2 | async-start | bytes 5898240 | tf_op jit(solution)/shard_map/all_gather | solution.py:84
  12.8 159.0 %all-gather.31.cloned.1.call-start = ((), (), s32[]{:S(2)}) async-start(), calls=%async_computation.3 | async-start | bytes 5898240 | tf_op jit(solution)/shard_map/all_gather | solution.py:85
  16.0 8.9 %copy-start.64 = (s32[2,256,128]{2,1,0:T(8,128)S(1)}, s32[2,256,128]{2,1,0:T(8,128)}, u32[]{:S(2)}) copy-start(s32[2,256,128]{2,1,0:T(8,128)} %param.19) | copy-start | bytes 786436
  16.0 164.0 %all-gather.33.cloned.1.call-start = ((), (), s32[]{:S(2)}) async-start(), calls=%async_computation.4 | async-start | bytes 4423680 | tf_op jit(solution)/shard_map/all_gather | solution.py:82
  16.6 182.3 %all-gather.35.cloned.1.call-start = ((), (), s32[]{:S(2)}) async-start(), calls=%async_computation.5 | async-start | bytes 1474560 | tf_op jit(solution)/shard_map/all_gather | solution.py:83
  17.2 220.8 %all-gather.37.cloned.1.call-start = ((), (), s32[]{:S(2)}) async-start(), calls=%async_computation.6 | async-start | bytes 5898240 | tf_op jit(solution)/shard_map/all_gather | solution.py:84
  17.9 259.0 %all-gather.39.cloned.1.call-start = ((), (), s32[]{:S(2)}) async-start(), calls=%async_computation.7 | async-start | bytes 5898240 | tf_op jit(solution)/shard_map/all_gather | solution.py:85
  30.0 10.0 %copy-start.60 = (s32[128,128]{1,0:T(8,128)}, s32[128,128]{1,0:T(8,128)S(1)}, u32[]{:S(2)}) copy-start(s32[128,128]{1,0:T(8,128)S(1)} %clamp_add_fusion) | copy-start | bytes 196612
  41.1 22.9 %copy-start.105 = (bf16[2,768]{1,0:T(2,128)(2,1)S(1)}, bf16[2,768]{1,0:T(2,128)(2,1)}, u32[]{:S(2)}) copy-start(bf16[2,768]{1,0:T(2,128)(2,1)} %param.25) | copy-start | bytes 9220
  111.7 30.8 %copy-start.112 = (s32[256]{0:T(256)S(1)}, s32[256]{0:T(256)}, u32[]{:S(2)}) copy-start(s32[256]{0:T(256)} %param.16) | copy-start | bytes 3076
  111.7 31.4 %copy-start.72 = (pred[128,128]{0,1:T(8,128)(4,1)S(1)}, pred[128,128]{0,1:T(8,128)(4,1)}, u32[]{:S(2)}) copy-start(pred[128,128]{0,1:T(8,128)(4,1)} %iota_compare_fusion.18) | copy-start | bytes 49156
  111.7 32.1 %copy-start.38 = (bf16[256,768]{1,0:T(8,128)(2,1)S(1)}, bf16[256,768]{1,0:T(8,128)(2,1)}, u32[]{:S(2)}) copy-start(bf16[256,768]{1,0:T(8,128)(2,1)} %param.14) | copy-start | bytes 1179652
  157.3 14.5 %copy-start.41 = (bf16[2,128,12,64]{1,0,3,2:T(2,128)(2,1)}, bf16[2,128,12,64]{1,0,3,2:T(2,128)(2,1)S(1)}, u32[]{:S(2)}) copy-start(bf16[2,128,12,64]{1,0,3,2:T(2,128)(2,1)S(1)} %copy.332) | copy-start | bytes 1179652
  159.6 12.2 %copy-start.7 = (f32[256,768]{1,0:T(8,128)}, f32[256,768]{1,0:T(8,128)S(1)}, u32[]{:S(2)}) copy-start(f32[256,768]{1,0:T(8,128)S(1)} %get-tuple-element.126) | copy-start | bytes 2359300
  159.7 12.1 %copy-start.84 = (f32[256]{0:T(256)}, f32[256]{0:T(256)S(1)}, u32[]{:S(2)}) copy-start(f32[256]{0:T(256)S(1)} %broadcast_multiply_fusion.11) | copy-start | bytes 3076
  159.9 11.9 %copy-start.99 = (f32[256]{0:T(256)}, f32[256]{0:T(256)S(1)}, u32[]{:S(2)}) copy-start(f32[256]{0:T(256)S(1)} %add_rsqrt_fusion.3) | copy-start | bytes 3076
  277.0 7.8 %slice-start.16 = ((s8[4718592]{0:T(1024)(128)(4,1)}), s8[4194304]{0:T(1024)(128)(4,1)S(1)}, s32[]{:S(2)}) async-start(s8[4718592]{0:T(1024)(128)(4,1)} %bitcast.404), calls=%async_computation.24 | async-start | bytes 8388608
  277.0 7.8 %slice-start.17 = ((s8[4718592]{0:T(1024)(128)(4,1)}), s8[524288]{0:T(1024)(128)(4,1)S(1)}, s32[]{:S(2)}) async-start(s8[4718592]{0:T(1024)(128)(4,1)} %bitcast.404), calls=%async_computation.25 | async-start | bytes 1048576
  277.0 7.8 %copy-start.116 = (f32[256,3072]{1,0:T(8,128)S(1)}, f32[256,3072]{1,0:T(8,128)}, u32[]{:S(2)}) copy-start(f32[256,3072]{1,0:T(8,128)} %get-tuple-element.134) | copy-start | bytes 9437188
  298.5 8.9 %slice-start.12 = ((s8[4718592]{0:T(1024)(128)(4,1)}), s8[4194304]{0:T(1024)(128)(4,1)S(1)}, s32[]{:S(2)}) async-start(s8[4718592]{0:T(1024)(128)(4,1)} %bitcast.400), calls=%async_computation.20 | async-start | bytes 8388608
  701.0 8.4 %copy-start.15 = (f32[256,768]{1,0:T(8,128)S(1)}, f32[256,768]{1,0:T(8,128)}, u32[]{:S(2)}) copy-start(f32[256,768]{1,0:T(8,128)} %copy-done.13) | copy-start | bytes 2359300
  701.0 8.4 %copy-start.22 = (bf16[256,2304]{0,1:T(8,128)(2,1)S(1)}, bf16[256,2304]{0,1:T(8,128)(2,1)}, u32[]{:S(2)}) copy-start(bf16[256,2304]{0,1:T(8,128)(2,1)} %copy-done.21) | copy-start | bytes 3538948
  (119 other events, 420.9 us)
Sparse Core Ops, SparseCore 0:
  10.3 33.7 all-gather.24
  45.6 17.4 all-gather.26
  65.2 39.5 all-gather.28
  106.2 41.6 all-gather.30
  149.3 30.7 all-gather.32
  181.5 17.4 all-gather.34
  200.5 37.4 all-gather.36
  239.5 37.4 all-gather.38

commit v2 on v1

--- a/solution.py
+++ b/solution.py
@@ -1,4 +1,5 @@
 import functools
+from typing import NamedTuple
 
 import jax
 import jax.numpy as jnp
@@ -75,19 +76,6 @@
         + pair_terms
     )
     return jnp.where(pair_mask[:, None], scores, -1e30)
-
-
-def fetch_forward(w_in, w_out, w_up, w_down, shifts, up_shift, gain_rows, bias_table):
-    return (
-        lax.all_gather(w_in, "fsdp", axis=0, tiled=True),
-        lax.all_gather(w_out, "fsdp", axis=0, tiled=True),
-        lax.all_gather(w_up, "fsdp", axis=0, tiled=True),
-        lax.all_gather(w_down, "fsdp", axis=0, tiled=True),
-        lax.all_gather(shifts, "fsdp", axis=1, tiled=True),
-        lax.all_gather(up_shift, "fsdp", axis=0, tiled=True),
-        lax.all_gather(gain_rows, "fsdp", axis=1, tiled=True),
-        lax.all_gather(bias_table, "fsdp", axis=1, tiled=True),
-    )
 
 
 def layer_forward(inputs, weights, pair_mask, linear, across):
@@ -279,10 +267,10 @@
     )
 
 
-def reduce_kernel(
-    high, count, grads, out, own, core_in, x_in, y_in, z_in, full, load_sem, core_sem,
-    x_sem, y_sem, z_sem, zg_sem, yg_sem, sent, out_sem,
-):
+def reduce_kernel(high, count, segments, members, *refs):
+    sources, targets = refs[:members], refs[members : 2 * members]
+    (own, core_in, x_in, y_in, z_in, full, load_sem, core_sem, x_sem, y_sem, z_sem, zg_sem,
+     yg_sem, sent, out_sem) = refs[2 * members :]
     dp = lax.axis_index("dp")
     shard = lax.axis_index("fsdp")
     y_at, z_at = lax.rem(dp, 2), lax.div(dp, 2)
@@ -309,16 +297,20 @@
             device_id=peer, device_id_type=MESH,
         )
 
-    def rows_of(k, wanted):
-        return grads.at[wanted, pl.ds(pl.multiple_of(k * chunk, chunk), chunk), :]
-
-    def load(k, j):
-        wanted = (x_at if j == 0 else 1 - x_at) * 2 + core
-        return pltpu.make_async_copy(rows_of(k, wanted), own.at[k, j], load_sem.at[k, j])
-
-    def core_send(k, j):
-        wanted = (x_at if j == 0 else 1 - x_at) * 2 + 1 - core
-        return remote(rows_of(k, wanted), core_in.at[k, j], 0, core_sem.at[k, j], core_peer)
+    def source_of(segment, wanted):
+        ref = sources[segment.member]
+        start = pl.multiple_of(wanted * segment.depth + segment.row, 16)
+        return ref.at[pl.ds(start, segment.rows), pl.ds(segment.column, own.shape[3])]
+
+    def slot_of(buffer, k, j, segment):
+        return buffer.at[k, j, pl.ds(segment.at, segment.rows)]
+
+    def load_arrival(k, j):
+        slot = own.at[k, j]
+        return pltpu.make_async_copy(slot, slot, load_sem.at[k, j])
+
+    def core_arrival(k, j):
+        return remote(core_in.at[k, j], core_in.at[k, j], 0, core_sem.at[k, j], core_peer)
 
     def x_send(k):
         return remote(own.at[k, 1], x_in.at[k], 1, x_sem.at[k], x_peer)
@@ -350,21 +342,26 @@
         mine = full.at[k, y_rows(y_at)]
         return remote(mine, mine, 5, yg_sem.at[k], y_peer)
 
-    def store(k):
-        return pltpu.make_async_copy(
-            full.at[k], out.at[pl.ds(pl.multiple_of(k * chunk, chunk), chunk), :], out_sem.at[k]
-        )
-
-    @pl.loop(0, count)
-    def _(k):
+    def store_end(k):
+        return pltpu.make_async_copy(full.at[k], full.at[k], out_sem.at[k])
+
+    for segment in segments:
+        k = segment.chunk
         for j in (1, 0):
-            core_send(k, j).start()
-            load(k, j).start()
+            x_wanted = x_at if j == 0 else 1 - x_at
+            remote(
+                source_of(segment, x_wanted * 2 + 1 - core), slot_of(core_in, k, j, segment),
+                0, core_sem.at[k, j], core_peer,
+            ).start()
+            pltpu.make_async_copy(
+                source_of(segment, x_wanted * 2 + core), slot_of(own, k, j, segment),
+                load_sem.at[k, j],
+            ).start()
 
     def stage_core(k):
         for j in (1, 0):
-            load(k, j).wait()
-            core_send(k, j).wait_recv()
+            load_arrival(k, j).wait()
+            core_arrival(k, j).wait_recv()
             add_rows(own.at[k, j], core_in.at[k, j])
             if j == 1:
                 x_send(k).start()
@@ -396,7 +393,17 @@
 
     def stage_store(k):
         yg_send(k).wait_recv()
-        store(k).start()
+        for segment in segments:
+
+            @pl.when(k == segment.chunk)
+            def _(segment=segment):
+                target = targets[segment.member].at[
+                    pl.ds(segment.row, segment.rows), pl.ds(segment.column, own.shape[3])
+                ]
+                pltpu.make_async_copy(
+                    full.at[segment.chunk, pl.ds(segment.at, segment.rows)], target,
+                    out_sem.at[segment.chunk],
+                ).start()
 
     stages = (stage_core, stage_x, stage_y, stage_z, stage_spread, stage_store)
     lags = (0, LAG, 2 * LAG, 3 * LAG, 4 * LAG, 5 * LAG)
@@ -422,13 +429,38 @@
 
     @pl.loop(0, count)
     def _(k):
-        store(k).wait()
-
-
-def reduce_gradients(grads, group):
-    shards, rows, width = grads.shape
+        store_end(k).wait()
+
+
+class Segment(NamedTuple):
+    member: int
+    depth: int
+    row: int
+    column: int
+    rows: int
+    chunk: int
+    at: int
+
+
+def plan_segments(members, shards, width, chunk):
+    segments, place = [], 0
+    for member, array in enumerate(members):
+        depth = array.shape[0] // shards
+        for column in range(0, array.shape[1], width):
+            row = 0
+            while row < depth:
+                rows = min(depth - row, chunk - place % chunk)
+                segments.append(
+                    Segment(member, depth, row, column, rows, place // chunk, place % chunk)
+                )
+                row, place = row + rows, place + rows
+    return tuple(segments), place
+
+
+def reduce_gradients(members, shards, group, width):
     high = group // 2
     chunk = chunk_rows(group)
+    segments, rows = plan_segments(members, shards, width, chunk)
     count = rows // chunk
     piece = chunk // group
     buffers = [
@@ -441,68 +473,247 @@
     ]
     semaphores = [(count, 2), (count, 2), (count,), (count,), (count, high - 1),
                   (count, high - 1), (count,), (6,), (count,)]
+    hbm = pl.BlockSpec(memory_space=pltpu.MemorySpace.HBM)
     return pl.pallas_call(
-        functools.partial(reduce_kernel, high, count),
-        out_shape=jax.ShapeDtypeStruct((rows, width), jnp.bfloat16),
-        in_specs=[pl.BlockSpec(memory_space=pltpu.MemorySpace.HBM)],
-        out_specs=pl.BlockSpec(memory_space=pltpu.MemorySpace.HBM),
+        functools.partial(reduce_kernel, high, count, segments, len(members)),
+        out_shape=[
+            jax.ShapeDtypeStruct((array.shape[0] // shards, array.shape[1]), jnp.bfloat16)
+            for array in members
+        ],
+        in_specs=[hbm] * len(members),
+        out_specs=[hbm] * len(members),
         scratch_shapes=[pltpu.VMEM(shape, jnp.bfloat16) for shape in buffers]
         + [pltpu.SemaphoreType.DMA(shape) for shape in semaphores],
         compiler_params=pltpu.CompilerParams(
             collective_id=1, has_side_effects=True, vmem_limit_bytes=64 * 1024 * 1024 - 65536
         ),
-    )(grads)
+    )(*members)
 
 
 def chunk_rows(group):
     return 16 * CHUNK_TILES * group
 
 
-def pack_gradients(grad_list, shards, group):
-    blocks, smalls = [], []
+def sum_gradients(grad_list, shards, group):
+    members, smalls = [], []
     for grads in grad_list:
         w_in, w_out, w_up, w_down, shifts, up_shift, gain_rows, bias_table = grads
         width = w_out.shape[1]
-        for member in (w_in, w_out, w_up, w_down):
-            member = member.astype(jnp.bfloat16)
-            depth = member.shape[0] // shards
-            member = member.reshape(shards, depth, member.shape[1] // width, width)
-            blocks.append(jnp.swapaxes(member, 1, 2).reshape(shards, -1, width))
+        members += [member.astype(jnp.bfloat16) for member in (w_in, w_out, w_up, w_down)]
         smalls.append(jnp.swapaxes(shifts.reshape(6, shards, -1), 0, 1).reshape(shards, -1))
         smalls.append(up_shift.reshape(shards, -1))
         smalls.append(jnp.swapaxes(gain_rows.reshape(2, shards, -1), 0, 1).reshape(shards, -1))
         smalls.append(jnp.swapaxes(bias_table.reshape(3, shards, -1), 0, 1).reshape(shards, -1))
-    small = jnp.concatenate(smalls, axis=1)
-    rows = sum(block.shape[1] for block in blocks)
+    small = jnp.concatenate(smalls, axis=1).astype(jnp.bfloat16)
+    layers = len(grad_list)
+    rows = sum(member.size // (shards * width) for member in members)
     chunk = chunk_rows(group)
     total = -(-(rows + -(-small.shape[1] // width)) // chunk) * chunk
     small = jnp.pad(small, ((0, 0), (0, (total - rows) * width - small.shape[1])))
-    blocks.append(small.reshape(shards, total - rows, width).astype(jnp.bfloat16))
-    return jnp.concatenate(blocks, axis=1), (len(grad_list), rows, shards)
-
-
-def unpack_gradients(reduced, shapes):
-    layers, rows, shards = shapes
-    width = reduced.shape[1]
-    per_layer = rows // layers
+    members.append(small.reshape(shards * (total - rows), width))
+    reduced = reduce_gradients(members, shards, group, width)
+    spans = [
+        jnp.stack([reduced[4 * layer + member] for layer in range(layers)]).astype(jnp.float32)
+        for member in range(4)
+    ]
     depth = width // shards
-    body = reduced[:rows].astype(jnp.float32).reshape(layers, per_layer, width)
-    spans = []
-    start = 0
-    for blocks in (3, 1, 4):
-        part = body[:, start : start + blocks * depth].reshape(layers, blocks, depth, width)
-        spans.append(jnp.swapaxes(part, 1, 2).reshape(layers, depth, blocks * width))
-        start += blocks * depth
-    spans.append(body[:, start:])
-    small = reduced[rows:].astype(jnp.float32).reshape(-1)
     sizes = (6 * depth, width, 2 * depth, 3 * (NB // shards) * H)
-    small = small[: layers * sum(sizes)].reshape(layers, -1)
+    used = layers * sum(sizes)
+    small = reduced[-1][: -(-used // width)].astype(jnp.float32).reshape(-1)
+    small = small[:used].reshape(layers, -1)
     forms = ((6, depth), (width,), (2, depth), (3, NB // shards, H))
     start = 0
     for size, form in zip(sizes, forms):
         spans.append(small[:, start : start + size].reshape((layers,) + form))
         start += size
     return tuple(spans)
+
+
+def gather_kernel(items, *refs):
+    total = len(items)
+    sources, targets = refs[:5], refs[5 : 5 + total]
+    stages = refs[5 + total : 5 + 2 * total]
+    load_sem, store_sem, send_sem, arrive = refs[5 + 2 * total :]
+    dp = lax.axis_index("dp")
+    shard = lax.axis_index("fsdp")
+    x_at, core = lax.div(shard, 2), lax.rem(shard, 2)
+    bits = (lax.rem(dp, 2), lax.rem(lax.div(dp, 2), 2))
+    core_peer = (dp, x_at * 2 + 1 - core)
+    other = (1 - x_at) * 2 + core
+    x_peer = (dp, other)
+    dp_peers = [
+        (dp + 1 - 2 * bits[0], shard),
+        (dp + 2 - 4 * bits[1], shard),
+    ]
+    barrier = pltpu.get_barrier_semaphore()
+    for peer in [core_peer, x_peer] + dp_peers:
+        pl.semaphore_signal(barrier, inc=1, device_id=peer, device_id_type=MESH)
+    pl.semaphore_wait(barrier, 4)
+
+    def copy(source, target, item, kind, peer):
+        return pltpu.make_async_remote_copy(
+            src_ref=source, dst_ref=target, send_sem=send_sem.at[item, kind],
+            recv_sem=arrive.at[item, kind], device_id=peer, device_id_type=MESH,
+        )
+
+    def shard_of(i):
+        member, layer = items[i]
+        return sources[member] if layer is None else sources[member].at[layer]
+
+    def depth_of(i):
+        return stages[i].shape[0]
+
+    def parts_of(i):
+        return 4 if depth_of(i) % 64 == 0 else 1
+
+    def mine_out(i):
+        n = depth_of(i)
+        return targets[i].at[pl.ds(pl.multiple_of(shard * n, 16), n)]
+
+    def other_out(i, quarter):
+        n = depth_of(i)
+        part = n // parts_of(i)
+        return targets[i].at[pl.ds(pl.multiple_of(other * n + quarter * part, 16), part)]
+
+    def other_whole(i):
+        n = depth_of(i)
+        return targets[i].at[pl.ds(pl.multiple_of(other * n, 16), n)]
+
+    def order_of(i):
+        return (0, 1) if i % 2 == 0 else (1, 0)
+
+    def quarter_of(i, flips):
+        if parts_of(i) == 1:
+            return 0
+        now = [bits[axis] if axis not in flips else 1 - bits[axis] for axis in (0, 1)]
+        return now[1] * 2 + now[0]
+
+    def x_send(i):
+        n = depth_of(i)
+        part = n // parts_of(i)
+        start = pl.multiple_of(quarter_of(i, ()) * part, 16)
+        rows = pl.ds(start, part)
+        landing = targets[i].at[pl.ds(pl.multiple_of(shard * n + start, 16), part)]
+        return copy(shard_of(i).at[rows], landing, i, 0, x_peer)
+
+    def first_send(i):
+        mine = other_out(i, quarter_of(i, ()))
+        return copy(mine, mine, i, 1, dp_peers[order_of(i)[0]])
+
+    def second_send(i):
+        mine = other_out(i, quarter_of(i, ()))
+        return copy(mine, mine, i, 2, dp_peers[order_of(i)[1]])
+
+    def relay_send(i):
+        mine = other_out(i, quarter_of(i, (order_of(i)[0],)))
+        return copy(mine, mine, i, 3, dp_peers[order_of(i)[1]])
+
+    def own_share(i):
+        return copy(shard_of(i), mine_out(i), i, 4, core_peer)
+
+    def far_share(i):
+        return copy(other_whole(i), other_whole(i), i, 5, core_peer)
+
+    def load(i):
+        return pltpu.make_async_copy(shard_of(i), stages[i], load_sem.at[i])
+
+    def store(i):
+        return pltpu.make_async_copy(stages[i], mine_out(i), store_sem.at[i])
+
+    for i in range(total):
+        x_send(i).start()
+    for i in range(total):
+        own_share(i).start()
+        load(i).start()
+
+    def spread(i):
+        x_send(i).wait_recv()
+        if parts_of(i) == 4:
+            first_send(i).start()
+            second_send(i).start()
+        load(i).wait()
+        store(i).start()
+
+    def relay(i):
+        if parts_of(i) == 4:
+            first_send(i).wait_recv()
+            relay_send(i).start()
+
+    def share(i):
+        if parts_of(i) == 4:
+            second_send(i).wait_recv()
+            relay_send(i).wait_recv()
+        far_share(i).start()
+
+    for step in range(total + 4):
+        if step < total:
+            spread(step)
+        if 0 <= step - 1 < total:
+            relay(step - 1)
+        if 0 <= step - 3 < total:
+            share(step - 3)
+    for i in range(total):
+        own_share(i).wait()
+        far_share(i).wait()
+        x_send(i).wait_send()
+        if parts_of(i) == 4:
+            first_send(i).wait_send()
+            second_send(i).wait_send()
+            relay_send(i).wait_send()
+        store(i).wait()
+
+
+def gather_weights(sources, small, shards):
+    layers = sources[0].shape[0]
+    items = [(4, None)]
+    forms = [small.shape]
+    for layer in range(layers):
+        for member in range(4):
+            items.append((member, layer))
+            forms.append(sources[member].shape[1:])
+    hbm = pl.BlockSpec(memory_space=pltpu.MemorySpace.HBM)
+    total = len(items)
+    return pl.pallas_call(
+        functools.partial(gather_kernel, tuple(items)),
+        out_shape=[
+            jax.ShapeDtypeStruct((form[0] * shards, form[1]), jnp.bfloat16) for form in forms
+        ],
+        in_specs=[hbm] * 5,
+        out_specs=[hbm] * total,
+        scratch_shapes=[pltpu.VMEM(form, jnp.bfloat16) for form in forms]
+        + [
+            pltpu.SemaphoreType.DMA((total,)),
+            pltpu.SemaphoreType.DMA((total,)),
+            pltpu.SemaphoreType.DMA((total, 6)),
+            pltpu.SemaphoreType.DMA((total, 6)),
+        ],
+        compiler_params=pltpu.CompilerParams(collective_id=0, has_side_effects=True),
+    )(*sources, small)
+
+
+def fetch_all(attn_in, attn_out, ffn_in, ffn_out, biases, ffn_in_bias, gains, tables, shards):
+    layers, depth = attn_in.shape[0], attn_in.shape[1]
+    width = depth * shards
+    flat = jnp.concatenate(
+        [member.reshape(-1) for member in (biases, ffn_in_bias, gains, tables)]
+    )
+    rows = -(-flat.shape[0] // (16 * width)) * 16
+    small = jnp.pad(flat, (0, rows * width - flat.shape[0])).reshape(rows, width)
+    gathered = gather_weights((attn_in, attn_out, ffn_in, ffn_out), small, shards)
+    small = gathered[0].reshape(shards, -1)
+    pieces = []
+    start = 0
+    for member, axis in ((biases, 2), (ffn_in_bias, 1), (gains, 2), (tables, 2)):
+        piece = small[:, start : start + member.size].reshape((shards,) + member.shape)
+        start += member.size
+        piece = jnp.moveaxis(piece, 0, axis)
+        pieces.append(
+            piece.reshape(member.shape[:axis] + (-1,) + member.shape[axis + 1 :])
+        )
+    return [
+        tuple(gathered[1 + 4 * layer : 5 + 4 * layer]) + tuple(piece[layer] for piece in pieces)
+        for layer in range(layers)
+    ]
 
 
 def local(
@@ -526,23 +737,16 @@
     current = tokens
     layer_inputs = []
     kept_list = []
-    fetched_list = []
+    shards = lax.axis_size("fsdp")
+    fetched_list = fetch_all(
+        attn_in, attn_out, ffn_in, ffn_out, biases, ffn_in_bias, gains, tables, shards
+    )
     outputs = []
     for layer_index in range(layer_total):
-        fetched = fetch_forward(
-            attn_in[layer_index],
-            attn_out[layer_index],
-            ffn_in[layer_index],
-            ffn_out[layer_index],
-            biases[layer_index],
-            ffn_in_bias[layer_index],
-            gains[layer_index],
-            tables[layer_index],
-        )
+        fetched = fetched_list[layer_index]
         result, kept = layer_forward(current, fetched, pair_mask, linear, across)
         layer_inputs.append(current)
         kept_list.append(kept)
-        fetched_list.append(fetched)
         current = result.astype(jnp.bfloat16)
         outputs.append(current)
     grad_inputs = out_grad.astype(jnp.float32) * mlm_mask.astype(jnp.float32)[:, None]
@@ -558,9 +762,8 @@
             across,
         )
         shard_list.insert(0, grads)
-    packed, shapes = pack_gradients(shard_list, lax.axis_size("fsdp"), lax.axis_size("dp"))
-    reduced = reduce_gradients(packed, lax.axis_size("dp"))
-    return (jnp.stack(outputs), grad_inputs) + unpack_gradients(reduced, shapes)
+    summed = sum_gradients(shard_list, shards, lax.axis_size("dp"))
+    return (jnp.stack(outputs), grad_inputs) + summed
 
 
 def solution(mesh):

time: 728 us -> 594 us (0.82)
  local copies, waits for them, and re-layouts: 239 us -> 135 us
  Pallas kernels: 191 us -> 268 us
  waiting for transfers between devices: 71 us -> 0 us
  blocking collectives: 57.4 us -> 0 us
  matrix products: 120 us -> 144 us
  between operations: 15.8 us -> 2.45 us
  other arithmetic: 25.3 us -> 36.7 us
    pallas_call x1 -> x2, Pallas kernels: 191 us -> 268 us  [the longest x1 190 us: reduce_gradients(): pl.pallas_call(functools.partial(reduce_kernel, high, count, segments, le...]
    all_gather x8 -> x0, waiting for transfers between devices: 68.5 us -> none  [the longest x2 33.5 us: fetch_forward(): lax.all_gather(w_up, 'fsdp', axis=0, tiled=True)]
    all_gather x8 -> x0, blocking collectives: 57.4 us -> none  [the longest x2 18.4 us: fetch_forward(): lax.all_gather(gain_rows, 'fsdp', axis=1, tiled=True)]
    reshape x22 -> x24, local copies, waits for them, and re-layouts: 70.5 us -> 18.6 us  [the longest x2 2.71 us: sum_gradients(): jnp.swapaxes(bias_table.reshape(3, shards, -1), 0, 1).reshape(shards, -1)]
    slice x2 -> x1, local copies, waits for them, and re-layouts: 26.8 us -> 0.74 us  [layer_forward(): shifts[5]]
    slice x21 -> x10, local copies, waits for them, and re-layouts: 20.3 us -> 2.04 us  [the longest x5 0.73 us: fetch_all(): small[:, start:start + member.size].reshape((shards,) + member.shape)]
    unnamed x289 -> x233, local copies, waits for them, and re-layouts: 34.6 us -> 17.1 us
    convert_element_type x0 -> x5, other arithmetic: none -> 10 us  [the longest x4 9.88 us: sum_gradients(): jnp.stack([reduced[4 * layer + member] for layer in range(layers)])]
  transfers between devices with their start and end apart: 8 -> 0, of which waited for: 4 -> 0; matrix products, arithmetic and copies ran while one was open for 19% -> 0% of each run, Pallas kernels for 0% -> 0%
where the time goes in v2:
time: 594 us; the launch traced here: 587 us
  Pallas kernels  268 us (45%)
  matrix products  144 us (24%)
  local copies, waits for them, and re-layouts  135 us (23%)
  other arithmetic  36.7 us (6%)
    pallas_call x1, Pallas kernels, reduce_gradients(): pl.pallas_call(functools.partial(reduce_kernel, high, count, segments, le...  190 us
    pallas_call x1, Pallas kernels, gather_weights(): pl.pallas_call(functools.partial(gather_kernel, tuple(items)), out_shape=...  78.3 us
    dot_general x2, matrix products, layer_forward(): jnp.dot(first_low, w_up, preferred_element_type=jnp.float32)  24.1 us
    unnamed x233, local copies, waits for them, and re-layouts  17.1 us
    another operation x14, local copies, waits for them, and re-layouts, layer_backward(): jnp.stack([grad_query_shift, grad_value_shift, grad_attended_shift, grad_...  13.1 us
    dot_general x2, matrix products, layer_backward(): jnp.einsum('nd,fd->nf', branch_low, w_down, preferred_element_type=jnp.fl...  12 us

profile of v2, /device:TPU:0, one launch (start us, length us, event | category | flops | bytes accessed | tf_op | source)
XLA Modules:
  0.0 586.5 jit_solution(1302845874524614241)
XLA Ops:
  4.4 78.3 %shard_map.213 = (bf16[64,768]{1,0:T(8,128)(2,1)}, bf16[768,2304]{1,0:T(8,128)(2,1)}, bf16[768,768]{1,0:T(8,128)(2,1)}, bf16[768,3072]{1,0:T(8,128)(2,1)}, bf16[...) custom-call(bf16[2,192,2304]{2,1,0:T(8,128)(2,1)} %refs_0_.1, ...), custom_call_target="tpu_custom_call" | custom-call | tf_op jit(solution)/shard_map/pallas_call | solution.py:676
  84.7 3.2 convolution_bitcast_fusion
  116.3 11.8 %multiply_convert_fusion.1 = (bf16[256,3072]{1,0:T(8,128)(2,1)}, f32[256,3072]{1,0:T(8,128)}, f32[256,3072]{1,0:T(8,128)}) fusion(f32[3072]{0:T(1024)S(1)} %bitcast.277, bf16[768,3072]{1,0:T(8,128)(2,1)} %get-tuple-element.31, f32[256,768]{1,0:T(8,128)S(1)} %get-tuple-element.150, f32[768]{0:T(1024)S(1)} %add.284, f32[768]{0:T(1024)S(1)} %mul.288, ...), kind=kOutput, calls=%fused_computation.40 | convolution fusion | flops 1260847104 | bytes 13389824 | tf_op jit(solution)/shard_map/dot_general | solution.py:118
  128.2 4.3 fusion.150
  133.7 4.6 fusion.160
  144.8 3.1 fusion.125
  150.6 3.2 fusion.124
  176.3 12.3 %multiply_convert_fusion = (bf16[256,3072]{1,0:T(8,128)(2,1)}, f32[256,3072]{1,0:T(8,128)}, f32[256,3072]{1,0:T(8,128)}) fusion(f32[3072]{0:T(1024)} %bitcast.276, bf16[768,3072]{1,0:T(8,128)(2,1)} %get-tuple-element.35, f32[256,768]{1,0:T(8,128)} %copy-done.8, f32[768]{0:T(1024)} %add.313, f32[768]{0:T(1024)S(1)} %mul.304, f32[256]{0:T(256)} %add_rsqrt_fusion.1, ...), kind=kOutput, calls=%fused_computation.27 | convolution fusion | flops 1260847104 | bytes 13389824 | tf_op jit(solution)/shard_map/dot_general | solution.py:118
  189.9 4.6 fusion.153
  199.7 3.2 multiply_reduce_fusion.2
  205.1 6.4 %fusion.159 = (bf16[3072]{0:T(1024)(128)(2,1)}, bf16[256,3072]{1,0:T(8,128)(2,1)S(1)}) fusion(f32[256,3072]{1,0:T(8,128)S(1)} %copy-done.103, f32[256,3072]{1,0:T(8,128)} %get-tuple-element.158, bf16[3072,768]{1,0:T(8,128)(2,1)} %get-tuple-element.36, f32[256,768]{1,0:T(8,128)S(1)} %get-tuple-element.121), kind=kOutput, calls=%fused_computation.319 | convolution fusion | flops 1219949568 | bytes 13375488 | tf_op jit(solution)/shard_map/nd,fd->nf/dot_general | solution.py:172
  227.7 3.1 slice_bitcast_fusion.1
  256.3 3.0 fusion.158
  274.1 5.6 fusion.156
  316.1 3.0 fusion.155
  348.8 4.9 convolution_convert_fusion.refs_7_
  353.7 3.7 convolution_convert_fusion.1.refs_6_
  359.0 3.1 convolution_convert_fusion.2.refs_4_
  362.1 3.6 convolution_convert_fusion.3.refs_3_
  365.8 4.0 convolution_convert_fusion.4.refs_2_
  374.5 2.9 fusion.refs_0_
  377.4 189.8 %shard_map.214 = (bf16[192,2304]{1,0:T(8,128)(2,1)}, bf16[192,768]{1,0:T(8,128)(2,1)}, bf16[192,3072]{1,0:T(8,128)(2,1)}, bf16[768,768]{1,0:T(8,128)(2,1)}, bf16...) custom-call(bf16[768,2304]{1,0:T(8,128)(2,1)} %fusion.refs_0_, ...), custom_call_target="tpu_custom_call" | custom-call | tf_op jit(solution)/shard_map/pallas_call | solution.py:477
  567.3 4.3 maximum_convert_fusion.1
  580.8 4.1 convolution_add_fusion.4
  (443 shorter events, 214.1 us)
Async XLA Ops:
  4.4 80.3 %copy-start.30 = (bf16[256,768]{1,0:T(8,128)(2,1)S(1)}, bf16[256,768]{1,0:T(8,128)(2,1)}, u32[]{:S(2)}) copy-start(bf16[256,768]{1,0:T(8,128)(2,1)} %param.14) | copy-start | bytes 1179652
  83.6 6.7 %copy-start.65 = (bf16[4,12288]{1,0:T(4,128)(2,1)}, bf16[4,12288]{1,0:T(4,128)(2,1)S(1)}, u32[]{:S(2)}) copy-start(bf16[4,12288]{1,0:T(4,128)(2,1)S(1)} %reshape.469) | copy-start | bytes 294916
  90.5 6.1 %copy-start.66 = (bf16[4,2,3,8,12]{4,3,2,1,0:T(8,128)(2,1)}, bf16[4,2,3,8,12]{4,3,2,1,0:T(8,128)(2,1)S(1)}, u32[]{:S(2)}) copy-start(bf16[4,2,3,8,12]{4,3,2,1,0:T(8,128)(2,1)S(1)} %reshape.474) | copy-start | bytes 13828
  111.7 16.4 %copy-start.33 = (bf16[2,128,12,64]{1,0,3,2:T(2,128)(2,1)}, bf16[2,128,12,64]{1,0,3,2:T(2,128)(2,1)S(1)}, u32[]{:S(2)}) copy-start(bf16[2,128,12,64]{1,0,3,2:T(2,128)(2,1)S(1)} %copy.294) | copy-start | bytes 1179652
  113.7 14.5 %copy-start.5 = (f32[256,768]{1,0:T(8,128)}, f32[256,768]{1,0:T(8,128)S(1)}, u32[]{:S(2)}) copy-start(f32[256,768]{1,0:T(8,128)S(1)} %get-tuple-element.150) | copy-start | bytes 2359300
  113.7 14.3 %copy-start.82 = (f32[256]{0:T(256)}, f32[256]{0:T(256)S(1)}, u32[]{:S(2)}) copy-start(f32[256]{0:T(256)S(1)} %broadcast_multiply_fusion.11) | copy-start | bytes 3076
  114.0 14.1 %copy-start.94 = (f32[256]{0:T(256)}, f32[256]{0:T(256)S(1)}, u32[]{:S(2)}) copy-start(f32[256]{0:T(256)S(1)} %add_rsqrt_fusion.3) | copy-start | bytes 3076
  114.1 14.1 %copy-start.70 = (f32[768]{0:T(1024)}, f32[768]{0:T(1024)S(1)}, u32[]{:S(2)}) copy-start(f32[768]{0:T(1024)S(1)} %add.284) | copy-start | bytes 9220
  116.3 11.8 %copy-start.90 = (f32[4,192]{1,0:T(4,128)S(1)}, f32[4,192]{1,0:T(4,128)}, u32[]{:S(2)}) copy-start(f32[4,192]{1,0:T(4,128)} %get-tuple-element.184) | copy-start | bytes 9220
  132.5 5.7 copy-start.1
  132.5 37.7 %copy-start.74 = (f32[256]{0:T(256)}, f32[256]{0:T(256)S(1)}, u32[]{:S(2)}) copy-start(f32[256]{0:T(256)S(1)} %broadcast_multiply_fusion.10) | copy-start | bytes 3076
  132.9 226.1 %copy-start.63 = (f32[768]{0:T(1024)}, f32[768]{0:T(1024)S(1)}, u32[]{:S(2)}) copy-start(f32[768]{0:T(1024)S(1)} %add.294) | copy-start | bytes 9220
  133.6 225.3 %copy-start.58 = (f32[768]{0:T(1024)}, f32[768]{0:T(1024)S(1)}, u32[]{:S(2)}) copy-start(f32[768]{0:T(1024)S(1)} %mul.297) | copy-start | bytes 9220
  150.6 5.9 %copy-start.54 = (s32[128,128]{1,0:T(8,128)S(1)}, s32[128,128]{1,0:T(8,128)}, u32[]{:S(2)}) copy-start(s32[128,128]{1,0:T(8,128)} %copy-done.53) | copy-start | bytes 196612
  198.8 6.3 %copy-start.103 = (f32[256,3072]{1,0:T(8,128)S(1)}, f32[256,3072]{1,0:T(8,128)}, u32[]{:S(2)}) copy-start(f32[256,3072]{1,0:T(8,128)} %get-tuple-element.131) | copy-start | bytes 9437188
  199.7 11.8 %slice-start.3 = ((s8[4718592]{0:T(1024)(128)(4,1)}), s8[4194304]{0:T(1024)(128)(4,1)S(1)}, s32[]{:S(2)}) async-start(s8[4718592]{0:T(1024)(128)(4,1)} %bitcast.280), calls=%async_computation.3 | async-start | bytes 8388608
  205.1 6.4 %copy-start.25 = (f32[256,768]{1,0:T(8,128)}, f32[256,768]{1,0:T(8,128)S(1)}, u32[]{:S(2)}) copy-start(f32[256,768]{1,0:T(8,128)S(1)} %get-tuple-element.121) | copy-start | bytes 2359300
  205.1 6.4 %copy-start.9 = (f32[256,768]{1,0:T(8,128)S(1)}, f32[256,768]{1,0:T(8,128)}, u32[]{:S(2)}) copy-start(f32[256,768]{1,0:T(8,128)} %copy-done.8) | copy-start | bytes 2359300
  205.1 6.4 %copy-start.86 = (f32[256]{0:T(256)S(1)}, f32[256]{0:T(256)}, u32[]{:S(2)}) copy-start(f32[256]{0:T(256)} %copy-done.85) | copy-start | bytes 3076
  205.1 6.4 %copy-start.97 = (f32[256]{0:T(256)S(1)}, f32[256]{0:T(256)}, u32[]{:S(2)}) copy-start(f32[256]{0:T(256)} %add_rsqrt_fusion.1) | copy-start | bytes 3076
  205.1 6.4 %slice-start.4 = ((s8[4718592]{0:T(1024)(128)(4,1)}), s8[524288]{0:T(1024)(128)(4,1)S(1)}, s32[]{:S(2)}) async-start(s8[4718592]{0:T(1024)(128)(4,1)} %bitcast.280), calls=%async_computation.4 | async-start | bytes 1048576
  271.0 8.8 %slice-start.1 = ((s8[4718592]{0:T(1024)(128)(4,1)}), s8[4194304]{0:T(1024)(128)(4,1)S(1)}, s32[]{:S(2)}) async-start(s8[4718592]{0:T(1024)(128)(4,1)} %bitcast.278), calls=%async_computation.1 | async-start | bytes 8388608
  273.8 6.0 %copy-start.26 = (f32[256,768]{1,0:T(8,128)}, f32[256,768]{1,0:T(8,128)S(1)}, u32[]{:S(2)}) copy-start(f32[256,768]{1,0:T(8,128)S(1)} %get-tuple-element.127) | copy-start | bytes 2359300
  319.1 29.6 %copy-start.22 = (bf16[256,3072]{1,0:T(8,128)(2,1)S(1)}, bf16[256,3072]{1,0:T(8,128)(2,1)}, u32[]{:S(2)}) copy-start(bf16[256,3072]{1,0:T(8,128)(2,1)} %get-tuple-element.130) | copy-start | bytes 4718596
  (85 other events, 297.8 us)

commit v3 on v2

--- a/solution.py
+++ b/solution.py
@@ -1,4 +1,5 @@
 import functools
+import math
 from typing import NamedTuple
 
 import jax
@@ -18,243 +19,12 @@
 LAG = 2
 
 
-def exact_gelu(values):
-    return jax.nn.gelu(values, approximate=False)
-
-
 def norm_forward(values, gain_row, shift_row):
     centre = values - jnp.mean(values, axis=-1, keepdims=True)
     spread = jnp.mean(centre * centre, axis=-1, keepdims=True)
     inverse = lax.rsqrt(spread + EPSILON)
     normed = centre * inverse
     return (normed * gain_row + shift_row, normed, inverse)
-
-
-def norm_backward(incoming, normed, inverse, gain_row):
-    scaled = incoming * gain_row
-    centred = (
-        scaled
-        - jnp.mean(scaled, axis=-1, keepdims=True)
-        - normed * jnp.mean(scaled * normed, axis=-1, keepdims=True)
-    )
-    return (centred * inverse, jnp.sum(incoming * normed, axis=0), jnp.sum(incoming, axis=0))
-
-
-def geometry(doc_lengths, live_mask, layout_buckets):
-    windows = doc_lengths.shape[0]
-    positions = jnp.arange(WIN, dtype=jnp.int32)
-    doc_ends = jnp.cumsum(doc_lengths, axis=1)
-    document = jnp.sum((positions[None, :, None] >= doc_ends[:, None, :]).astype(jnp.int32), axis=2)
-    live_rows = live_mask.reshape(windows, WIN) == 1
-    diagonal = positions[:, None] == positions[None, :]
-    pair_mask = (document[:, :, None] == document[:, None, :]) & (
-        live_rows[:, None, :] | diagonal[None]
-    )
-    offset = jnp.clip(positions[None, :] - positions[:, None], -(NB // 2), NB // 2 - 1) + NB // 2
-    buckets = jnp.arange(NB, dtype=jnp.int32)
-    linear = (offset[None] == buckets[:, None, None]).astype(jnp.bfloat16)
-    layout_rows = layout_buckets.reshape(2, windows, WIN, WIN)
-    across = (layout_rows[:, :, None] == buckets[None, None, :, None, None]).astype(jnp.bfloat16)
-    return (pair_mask, linear, across)
-
-
-def pair_terms_of(bias_table, linear, across):
-    terms = jnp.einsum("bij,bh->hij", linear, bias_table[0], preferred_element_type=jnp.float32)[
-        None
-    ]
-    terms = terms + jnp.einsum(
-        "wbij,bh->whij", across[0], bias_table[1], preferred_element_type=jnp.float32
-    )
-    return terms + jnp.einsum(
-        "wbij,bh->whij", across[1], bias_table[2], preferred_element_type=jnp.float32
-    )
-
-
-def masked_scores(query_rows, key_rows, pair_terms, pair_mask):
-    scores = (
-        jnp.einsum("wihd,wjhd->whij", query_rows, key_rows, preferred_element_type=jnp.float32)
-        + pair_terms
-    )
-    return jnp.where(pair_mask[:, None], scores, -1e30)
-
-
-def layer_forward(inputs, weights, pair_mask, linear, across):
-    w_in, w_out, w_up, w_down, shifts, up_shift, gain_rows, bias_table = weights
-    shifts = shifts.astype(jnp.float32)
-    gain_rows = gain_rows.astype(jnp.float32)
-    rows = inputs.shape[0]
-    windows = rows // WIN
-    width = w_out.shape[0]
-    scaling = DH ** (-0.5)
-    projected = jnp.dot(inputs, w_in, preferred_element_type=jnp.float32)
-    query_rows = (
-        ((projected[:, :width] + shifts[0]) * scaling)
-        .astype(jnp.bfloat16)
-        .reshape(windows, WIN, H, DH)
-    )
-    key_rows = projected[:, width : 2 * width].astype(jnp.bfloat16).reshape(windows, WIN, H, DH)
-    value_rows = (
-        (projected[:, 2 * width :] + shifts[1]).astype(jnp.bfloat16).reshape(windows, WIN, H, DH)
-    )
-    pair_terms = pair_terms_of(bias_table, linear, across)
-    scores = masked_scores(query_rows, key_rows, pair_terms, pair_mask)
-    highest = jnp.max(scores, axis=-1, keepdims=True)
-    exponent = jnp.exp(scores - highest)
-    denominator = jnp.sum(exponent, axis=-1, keepdims=True)
-    probs = exponent / denominator
-    log_total = highest + jnp.log(denominator)
-    mixed_rows = jnp.einsum(
-        "whij,wjhd->wihd",
-        probs.astype(jnp.bfloat16),
-        value_rows,
-        preferred_element_type=jnp.float32,
-    )
-    mixed_rows = mixed_rows.reshape(rows, width).astype(jnp.bfloat16)
-    attended = jnp.dot(mixed_rows, w_out, preferred_element_type=jnp.float32) + shifts[2]
-    first_norm, normed_first, inverse_first = norm_forward(
-        inputs.astype(jnp.float32) + attended, gain_rows[0], shifts[3]
-    )
-    first_low = first_norm.astype(jnp.bfloat16)
-    hidden = jnp.dot(first_low, w_up, preferred_element_type=jnp.float32) + up_shift.astype(
-        jnp.float32
-    )
-    active = exact_gelu(hidden).astype(jnp.bfloat16)
-    branch = jnp.dot(active, w_down, preferred_element_type=jnp.float32) + shifts[4]
-    result, normed_second, inverse_second = norm_forward(
-        first_norm + branch, gain_rows[1], shifts[5]
-    )
-    kept = (
-        query_rows,
-        key_rows,
-        value_rows,
-        pair_terms,
-        log_total,
-        mixed_rows,
-        normed_first,
-        inverse_first,
-        first_low,
-        hidden,
-        active,
-        normed_second,
-        inverse_second,
-    )
-    return (result, kept)
-
-
-def layer_backward(incoming, inputs, weights, kept, pair_mask, linear, across):
-    w_in, w_out, w_up, w_down, shifts, up_shift, gain_rows, bias_table = weights
-    gain_rows = gain_rows.astype(jnp.float32)
-    (
-        query_rows,
-        key_rows,
-        value_rows,
-        pair_terms,
-        log_total,
-        mixed_rows,
-        normed_first,
-        inverse_first,
-        first_low,
-        hidden,
-        active,
-        normed_second,
-        inverse_second,
-    ) = kept
-    rows = inputs.shape[0]
-    width = w_out.shape[0]
-    windows = rows // WIN
-    scaling = DH ** (-0.5)
-    grad_second, grad_gain_second, grad_shift_second = norm_backward(
-        incoming, normed_second, inverse_second, gain_rows[1]
-    )
-    branch_low = grad_second.astype(jnp.bfloat16)
-    grad_down = jnp.einsum("nf,nd->fd", active, branch_low, preferred_element_type=jnp.float32)
-    grad_branch_shift = jnp.sum(branch_low.astype(jnp.float32), axis=0)
-    grad_active = jnp.einsum("nd,fd->nf", branch_low, w_down, preferred_element_type=jnp.float32)
-    hidden_low = jax.vjp(exact_gelu, hidden)[1](grad_active)[0].astype(jnp.bfloat16)
-    grad_up = jnp.einsum("nd,nf->df", first_low, hidden_low, preferred_element_type=jnp.float32)
-    grad_up_shift = jnp.sum(hidden_low.astype(jnp.float32), axis=0)
-    grad_first = grad_second + jnp.einsum(
-        "nf,df->nd", hidden_low, w_up, preferred_element_type=jnp.float32
-    )
-    grad_attended, grad_gain_first, grad_shift_first = norm_backward(
-        grad_first, normed_first, inverse_first, gain_rows[0]
-    )
-    attended_low = grad_attended.astype(jnp.bfloat16)
-    grad_out_weight = jnp.einsum(
-        "nd,ne->de", mixed_rows, attended_low, preferred_element_type=jnp.float32
-    )
-    grad_attended_shift = jnp.sum(attended_low.astype(jnp.float32), axis=0)
-    grad_mixed = jnp.einsum("ne,de->nd", attended_low, w_out, preferred_element_type=jnp.float32)
-    grad_mixed = grad_mixed.astype(jnp.bfloat16).reshape(windows, WIN, H, DH)
-    scores = masked_scores(query_rows, key_rows, pair_terms, pair_mask)
-    probs = jnp.exp(scores - log_total)
-    grad_probs = jnp.einsum(
-        "wihd,wjhd->whij", grad_mixed, value_rows, preferred_element_type=jnp.float32
-    )
-    grad_value = jnp.einsum(
-        "whij,wihd->wjhd",
-        probs.astype(jnp.bfloat16),
-        grad_mixed,
-        preferred_element_type=jnp.float32,
-    ).astype(jnp.bfloat16)
-    grad_scores = (
-        probs * (grad_probs - jnp.sum(probs * grad_probs, axis=-1, keepdims=True))
-    ).astype(jnp.bfloat16)
-    grad_query = (
-        jnp.einsum(
-            "whij,wjhd->wihd", grad_scores, key_rows, preferred_element_type=jnp.float32
-        ).astype(jnp.bfloat16)
-        * scaling
-    )
-    grad_key = jnp.einsum(
-        "whij,wihd->wjhd", grad_scores, query_rows, preferred_element_type=jnp.float32
-    ).astype(jnp.bfloat16)
-    grad_qkv = jnp.concatenate(
-        [
-            grad_query.reshape(rows, width),
-            grad_key.reshape(rows, width),
-            grad_value.reshape(rows, width),
-        ],
-        axis=1,
-    )
-    grad_in_weight = jnp.einsum("nd,ne->de", inputs, grad_qkv, preferred_element_type=jnp.float32)
-    grad_linear = jnp.einsum(
-        "bij,whij->bh", linear, grad_scores, preferred_element_type=jnp.float32
-    )
-    grad_across_x = jnp.einsum(
-        "wbij,whij->bh", across[0], grad_scores, preferred_element_type=jnp.float32
-    )
-    grad_across_y = jnp.einsum(
-        "wbij,whij->bh", across[1], grad_scores, preferred_element_type=jnp.float32
-    )
-    grad_table = jnp.stack([grad_linear, grad_across_x, grad_across_y])
-    grad_inputs = grad_attended + jnp.einsum(
-        "ne,de->nd", grad_qkv, w_in, preferred_element_type=jnp.float32
-    )
-    grad_query_shift = jnp.sum(grad_query.reshape(rows, width).astype(jnp.float32), axis=0)
-    grad_value_shift = jnp.sum(grad_value.reshape(rows, width).astype(jnp.float32), axis=0)
-    grad_shifts = jnp.stack(
-        [
-            grad_query_shift,
-            grad_value_shift,
-            grad_attended_shift,
-            grad_shift_first,
-            grad_branch_shift,
-            grad_shift_second,
-        ]
-    )
-    grad_gain_rows = jnp.stack([grad_gain_first, grad_gain_second])
-    grads = (
-        grad_in_weight,
-        grad_out_weight,
-        grad_up,
-        grad_down,
-        grad_shifts,
-        grad_up_shift,
-        grad_gain_rows,
-        grad_table,
-    )
-    return (grad_inputs, grads)
 
 
 MESH = pl.DeviceIdType.MESH
@@ -442,25 +212,39 @@
     at: int
 
 
-def plan_segments(members, shards, width, chunk):
+def plan_segments(members, depths, strides, width, chunk):
     segments, place = [], 0
     for member, array in enumerate(members):
-        depth = array.shape[0] // shards
+        depth = depths[member]
         for column in range(0, array.shape[1], width):
             row = 0
             while row < depth:
                 rows = min(depth - row, chunk - place % chunk)
                 segments.append(
-                    Segment(member, depth, row, column, rows, place // chunk, place % chunk)
+                    Segment(
+                        member, strides[member], row, column, rows, place // chunk, place % chunk
+                    )
                 )
                 row, place = row + rows, place + rows
     return tuple(segments), place
 
 
-def reduce_gradients(members, shards, group, width):
+def reduce_gradients(members, smalls, shards, group, width):
     high = group // 2
     chunk = chunk_rows(group)
-    segments, rows = plan_segments(members, shards, width, chunk)
+    depths = [array.shape[0] // shards for array in members]
+    strides = depths + [0] * len(smalls)
+    depths += [array.shape[0] for array in smalls]
+    filled = sum(
+        array.shape[1] // width * depth for array, depth in zip(members + smalls, depths)
+    )
+    rest = -filled % chunk
+    members = members + smalls
+    if rest:
+        members = members + [jnp.zeros((rest, width), jnp.bfloat16)]
+        depths.append(rest)
+        strides.append(0)
+    segments, rows = plan_segments(members, depths, strides, width, chunk)
     count = rows // chunk
     piece = chunk // group
     buffers = [
@@ -477,8 +261,8 @@
     return pl.pallas_call(
         functools.partial(reduce_kernel, high, count, segments, len(members)),
         out_shape=[
-            jax.ShapeDtypeStruct((array.shape[0] // shards, array.shape[1]), jnp.bfloat16)
-            for array in members
+            jax.ShapeDtypeStruct((depth, array.shape[1]), jnp.bfloat16)
+            for array, depth in zip(members, depths)
         ],
         in_specs=[hbm] * len(members),
         out_specs=[hbm] * len(members),
@@ -494,39 +278,24 @@
     return 16 * CHUNK_TILES * group
 
 
-def sum_gradients(grad_list, shards, group):
-    members, smalls = [], []
-    for grads in grad_list:
-        w_in, w_out, w_up, w_down, shifts, up_shift, gain_rows, bias_table = grads
-        width = w_out.shape[1]
-        members += [member.astype(jnp.bfloat16) for member in (w_in, w_out, w_up, w_down)]
-        smalls.append(jnp.swapaxes(shifts.reshape(6, shards, -1), 0, 1).reshape(shards, -1))
-        smalls.append(up_shift.reshape(shards, -1))
-        smalls.append(jnp.swapaxes(gain_rows.reshape(2, shards, -1), 0, 1).reshape(shards, -1))
-        smalls.append(jnp.swapaxes(bias_table.reshape(3, shards, -1), 0, 1).reshape(shards, -1))
-    small = jnp.concatenate(smalls, axis=1).astype(jnp.bfloat16)
-    layers = len(grad_list)
-    rows = sum(member.size // (shards * width) for member in members)
-    chunk = chunk_rows(group)
-    total = -(-(rows + -(-small.shape[1] // width)) // chunk) * chunk
-    small = jnp.pad(small, ((0, 0), (0, (total - rows) * width - small.shape[1])))
-    members.append(small.reshape(shards * (total - rows), width))
-    reduced = reduce_gradients(members, shards, group, width)
+def sum_gradients(members, smalls, shards, group):
+    width = smalls[0].shape[1]
+    layers = len(smalls)
+    reduced = reduce_gradients(members, smalls, shards, group, width)
     spans = [
         jnp.stack([reduced[4 * layer + member] for layer in range(layers)]).astype(jnp.float32)
         for member in range(4)
     ]
+    small = jnp.stack(reduced[4 * layers : 5 * layers]).astype(jnp.float32)
     depth = width // shards
-    sizes = (6 * depth, width, 2 * depth, 3 * (NB // shards) * H)
-    used = layers * sum(sizes)
-    small = reduced[-1][: -(-used // width)].astype(jnp.float32).reshape(-1)
-    small = small[:used].reshape(layers, -1)
-    forms = ((6, depth), (width,), (2, depth), (3, NB // shards, H))
-    start = 0
-    for size, form in zip(sizes, forms):
-        spans.append(small[:, start : start + size].reshape((layers,) + form))
-        start += size
-    return tuple(spans)
+    shard = lax.axis_index("fsdp")
+    rows = lax.dynamic_slice_in_dim(small[:, :8], shard * depth, depth, axis=2)
+    up_shift = lax.dynamic_slice_in_dim(small, 8 + shard, 1, axis=1)[:, 0]
+    table = small[:, 16 : 16 + H, : 3 * NB].reshape(layers, H, 3, NB)
+    table = lax.dynamic_slice_in_dim(table, shard * (NB // shards), NB // shards, axis=3)
+    return tuple(spans) + (
+        rows[:, :6], up_shift, rows[:, 6:], jnp.transpose(table, (0, 2, 3, 1)),
+    )
 
 
 def gather_kernel(items, *refs):
@@ -710,10 +479,345 @@
         pieces.append(
             piece.reshape(member.shape[:axis] + (-1,) + member.shape[axis + 1 :])
         )
+    shifts, up_shift, gain_rows, table = [piece.astype(jnp.float32) for piece in pieces]
+    vectors = jnp.concatenate([shifts, gain_rows], axis=1)
+    table = jnp.pad(
+        jnp.swapaxes(table, 2, 3), ((0, 0), (0, 0), (0, 16 - H), (0, WIN - NB))
+    )
     return [
-        tuple(gathered[1 + 4 * layer : 5 + 4 * layer]) + tuple(piece[layer] for piece in pieces)
+        tuple(gathered[1 + 4 * layer : 5 + 4 * layer])
+        + (vectors[layer], up_shift[layer : layer + 1], table[layer])
         for layer in range(layers)
     ]
+
+
+def contract(left, right, left_axis, right_axis):
+    return lax.dot_general(
+        left, right, (((left_axis,), (right_axis,)), ((), ())),
+        preferred_element_type=jnp.float32,
+    )
+
+
+def positions_of(axis):
+    return lax.broadcasted_iota(jnp.int32, (WIN, WIN), axis)
+
+
+def linear_bucket(offset):
+    return jnp.clip(offset, -(NB // 2), NB // 2 - 1) + NB // 2
+
+
+def lane_halves():
+    lane = lax.broadcasted_iota(jnp.int32, (1, 2 * DH), 1)
+    first = (lane < DH).astype(jnp.float32)
+    return first.astype(jnp.bfloat16), (1.0 - first).astype(jnp.bfloat16)
+
+
+def forward_kernel(
+    x_ref, buckets, live, lengths, vectors, up_shift, table, w_in_hbm, w_out_hbm, w_up_hbm,
+    w_down_hbm, out_ref, q_ref, k_ref, v_ref, o_ref, p_ref, low_ref, n1_ref, r1_ref, slope_ref,
+    g_ref, n2_ref, r2_ref, w_in, w_out, w_up, w_down, allowed, y1, total, sem,
+):
+    loads = [
+        pltpu.make_async_copy(source, target, sem.at[at])
+        for at, (source, target) in enumerate(
+            ((w_in_hbm, w_in), (w_out_hbm, w_out), (w_up_hbm, w_up), (w_down_hbm, w_down))
+        )
+    ]
+    for load in loads:
+        load.start()
+    rows, width = x_ref.shape
+    windows = rows // WIN
+    row, column = positions_of(0), positions_of(1)
+    offset = linear_bucket(column - row)
+    first, second = lane_halves()
+    for w in range(windows):
+        row_doc, column_doc = jnp.zeros_like(row), jnp.zeros_like(column)
+        end = 0
+        for k in range(lengths.shape[1]):
+            end = end + lengths[w, k]
+            row_doc = row_doc + (row >= end).astype(jnp.int32)
+            column_doc = column_doc + (column >= end).astype(jnp.int32)
+        alive = jnp.broadcast_to(live[w : w + 1, :], (WIN, WIN))
+        seen = (row_doc == column_doc) & ((alive == 1) | (row == column))
+        allowed[w] = seen.astype(jnp.int32)
+
+    loads[0].wait()
+    inputs = x_ref[...]
+    q_ref[...] = (
+        (jnp.dot(inputs, w_in[:, :width], preferred_element_type=jnp.float32) + vectors[0:1, :])
+        * DH ** (-0.5)
+    ).astype(jnp.bfloat16)
+    k_ref[...] = jnp.dot(
+        inputs, w_in[:, width : 2 * width], preferred_element_type=jnp.float32
+    ).astype(jnp.bfloat16)
+    v_ref[...] = (
+        jnp.dot(inputs, w_in[:, 2 * width :], preferred_element_type=jnp.float32)
+        + vectors[1:2, :]
+    ).astype(jnp.bfloat16)
+
+    def attend(w, pair):
+        span = pl.ds(w * WIN, WIN)
+        lanes = pl.ds(pl.multiple_of(pair * 2 * DH, 2 * DH), 2 * DH)
+        queries, keys, values = q_ref[span, lanes], k_ref[span, lanes], v_ref[span, lanes]
+        mixed = []
+        for side, half in enumerate((first, second)):
+            head = pair * 2 + side
+            scores = contract(queries * half, keys, 1, 1)
+            bias = 0.0
+            for kind, index in enumerate((offset, buckets[0, span, :], buckets[1, span, :])):
+                entries = jnp.broadcast_to(table[kind, pl.ds(head, 1), :], (WIN, WIN))
+                bias = bias + jnp.take_along_axis(
+                    entries, index, axis=1, mode="promise_in_bounds"
+                )
+            scores = jnp.where(allowed[w] == 1, scores + bias, -1e30)
+            exponent = jnp.exp(scores - jnp.max(scores, axis=-1, keepdims=True))
+            probs = exponent / jnp.sum(exponent, axis=-1, keepdims=True)
+            p_ref[w * H + head] = probs
+            mixed.append(
+                jnp.dot(
+                    probs.astype(jnp.bfloat16), values * half, preferred_element_type=jnp.float32
+                )
+            )
+        o_ref[span, lanes] = (mixed[0] + mixed[1]).astype(jnp.bfloat16)
+
+    for w in range(windows):
+
+        @pl.loop(0, H // 4)
+        def _(quad, w=w):
+            attend(w, quad * 2)
+            attend(w, quad * 2 + 1)
+
+    loads[1].wait()
+    attended = (
+        jnp.dot(o_ref[...], w_out[...], preferred_element_type=jnp.float32) + vectors[2:3, :]
+    )
+    first_norm, normed, inverse = norm_forward(
+        inputs.astype(jnp.float32) + attended, vectors[6:7, :], vectors[3:4, :]
+    )
+    n1_ref[...] = normed
+    r1_ref[...] = jnp.broadcast_to(inverse, r1_ref.shape)
+    y1[...] = first_norm
+    low_ref[...] = first_norm.astype(jnp.bfloat16)
+    total[...] = jnp.zeros_like(total)
+    loads[2].wait()
+    loads[3].wait()
+
+    @pl.loop(0, w_up.shape[1] // width)
+    def _(at):
+        lanes = pl.ds(pl.multiple_of(at * width, width), width)
+        hidden = (
+            jnp.dot(low_ref[...], w_up[:, lanes], preferred_element_type=jnp.float32)
+            + up_shift[:, lanes]
+        )
+        mass = 0.5 + 0.5 * lax.erf(hidden * 0.5**0.5)
+        slope_ref[:, lanes] = mass + hidden * jnp.exp(-0.5 * hidden * hidden) * (
+            0.5 / math.pi
+        ) ** 0.5
+        active = (hidden * mass).astype(jnp.bfloat16)
+        g_ref[:, lanes] = active
+        total[...] += jnp.dot(active, w_down[lanes, :], preferred_element_type=jnp.float32)
+
+    result, normed, inverse = norm_forward(
+        y1[...] + (total[...] + vectors[4:5, :]), vectors[7:8, :], vectors[5:6, :]
+    )
+    n2_ref[...] = normed
+    r2_ref[...] = jnp.broadcast_to(inverse, r2_ref.shape)
+    out_ref[...] = result.astype(jnp.bfloat16)
+
+
+def forward_layer(inputs, weights, buckets, live, lengths):
+    w_in, w_out, w_up, w_down, vectors, up_shift, table = weights
+    rows, width = inputs.shape
+    hidden = w_up.shape[1]
+    low, full = jnp.bfloat16, jnp.float32
+    narrow = jax.ShapeDtypeStruct((rows, width), low)
+    wide = jax.ShapeDtypeStruct((rows, width), full)
+    column = jax.ShapeDtypeStruct((rows, WIN), full)
+    vmem = pl.BlockSpec(memory_space=pltpu.MemorySpace.VMEM)
+    hbm = pl.BlockSpec(memory_space=pltpu.MemorySpace.HBM)
+    smem = pl.BlockSpec(memory_space=pltpu.MemorySpace.SMEM)
+    return pl.pallas_call(
+        forward_kernel,
+        out_shape=[
+            narrow, narrow, narrow, narrow, narrow,
+            jax.ShapeDtypeStruct((rows // WIN * H, WIN, WIN), full),
+            narrow, wide, column,
+            jax.ShapeDtypeStruct((rows, hidden), full),
+            jax.ShapeDtypeStruct((rows, hidden), low),
+            wide, column,
+        ],
+        in_specs=[vmem, vmem, vmem, smem, vmem, vmem, vmem, hbm, hbm, hbm, hbm],
+        out_specs=[vmem] * 13,
+        scratch_shapes=[
+            pltpu.VMEM(w_in.shape, low), pltpu.VMEM(w_out.shape, low),
+            pltpu.VMEM(w_up.shape, low), pltpu.VMEM(w_down.shape, low),
+            pltpu.VMEM((rows // WIN, WIN, WIN), jnp.int32),
+            pltpu.VMEM((rows, width), full), pltpu.VMEM((rows, width), full),
+            pltpu.SemaphoreType.DMA((4,)),
+        ],
+        compiler_params=pltpu.CompilerParams(vmem_limit_bytes=56 * 1024 * 1024),
+    )(inputs, buckets, live, lengths, vectors, up_shift, table, w_in, w_out, w_up, w_down)
+
+
+def backward_kernel(
+    dz_ref, n2_ref, r2_ref, slope_ref, n1_ref, r1_ref, p_ref, q_ref, k_ref, v_ref, buckets,
+    vectors, w_down_hbm, w_up_hbm, w_out_hbm, w_in_hbm, dx_ref, df_ref, du_ref, da_ref, dqkv_ref,
+    small_ref, w_down, w_up, w_out, w_in, small, grad, mixed, spread, sem,
+):
+    loads = [
+        pltpu.make_async_copy(source, target, sem.at[at])
+        for at, (source, target) in enumerate(
+            ((w_down_hbm, w_down), (w_up_hbm, w_up), (w_out_hbm, w_out), (w_in_hbm, w_in))
+        )
+    ]
+    for load in loads:
+        load.start()
+    rows, width = dz_ref.shape
+    windows = rows // WIN
+    first, second = lane_halves()
+    small[...] = jnp.zeros_like(small)
+    spread[...] = jnp.zeros_like(spread)
+
+    def add_row(at, values):
+        small[pl.ds(at, 1), :] = jnp.sum(values, axis=0, keepdims=True)
+
+    def norm_back(incoming, normed, inverse, gain_row):
+        scaled = incoming * gain_row
+        centred = (
+            scaled
+            - jnp.mean(scaled, axis=-1, keepdims=True)
+            - normed * jnp.mean(scaled * normed, axis=-1, keepdims=True)
+        )
+        return centred * inverse
+
+    incoming, normed = dz_ref[...], n2_ref[...]
+    add_row(7, incoming * normed)
+    add_row(5, incoming)
+    grad_second = norm_back(incoming, normed, r2_ref[:, 0:1], vectors[7:8, :])
+    grad[...] = grad_second
+    branch_low = grad_second.astype(jnp.bfloat16)
+    df_ref[...] = branch_low
+    add_row(4, branch_low.astype(jnp.float32))
+    loads[0].wait()
+    loads[1].wait()
+
+    @pl.loop(0, w_up.shape[1] // width)
+    def _(at):
+        lanes = pl.ds(pl.multiple_of(at * width, width), width)
+        grad_active = contract(df_ref[...], w_down[lanes, :], 1, 1)
+        hidden_low = (grad_active * slope_ref[:, lanes]).astype(jnp.bfloat16)
+        du_ref[:, lanes] = hidden_low
+        add_row(8 + at, hidden_low.astype(jnp.float32))
+        grad[...] += contract(hidden_low, w_up[:, lanes], 1, 1)
+
+    incoming, normed = grad[...], n1_ref[...]
+    add_row(6, incoming * normed)
+    add_row(3, incoming)
+    grad_attended = norm_back(incoming, normed, r1_ref[:, 0:1], vectors[6:7, :])
+    grad[...] = grad_attended
+    attended_low = grad_attended.astype(jnp.bfloat16)
+    da_ref[...] = attended_low
+    add_row(2, attended_low.astype(jnp.float32))
+    loads[2].wait()
+    mixed[...] = contract(attended_low, w_out[...], 1, 1).astype(jnp.bfloat16)
+
+    def attend(w, pair):
+        span = pl.ds(w * WIN, WIN)
+        start = pl.multiple_of(pair * 2 * DH, 2 * DH)
+        lanes = pl.ds(start, 2 * DH)
+        queries, keys, values = q_ref[span, lanes], k_ref[span, lanes], v_ref[span, lanes]
+        outgoing = mixed[span, lanes]
+        sums = [0.0, 0.0, 0.0]
+        for side, half in enumerate((first, second)):
+            head = pair * 2 + side
+            probs = p_ref[w * H + head]
+            own = outgoing * half
+            grad_probs = contract(own, values, 1, 1)
+            centred = grad_probs - jnp.sum(probs * grad_probs, axis=-1, keepdims=True)
+            grad_scores = (probs * centred).astype(jnp.bfloat16)
+            spread[pl.ds(head, WIN, stride=16), :] = grad_scores.astype(jnp.float32)
+            sums[0] += jnp.dot(grad_scores, keys * half, preferred_element_type=jnp.float32)
+            sums[1] += contract(grad_scores, queries * half, 0, 0)
+            sums[2] += contract(probs.astype(jnp.bfloat16), own, 0, 0)
+        scaled = sums[0].astype(jnp.bfloat16).astype(jnp.float32) * DH ** (-0.5)
+        dqkv_ref[span, lanes] = scaled.astype(jnp.bfloat16)
+        dqkv_ref[span, pl.ds(pl.multiple_of(start + width, 2 * DH), 2 * DH)] = sums[1].astype(
+            jnp.bfloat16
+        )
+        dqkv_ref[span, pl.ds(pl.multiple_of(start + 2 * width, 2 * DH), 2 * DH)] = sums[2].astype(
+            jnp.bfloat16
+        )
+
+    bucket = lax.broadcasted_iota(jnp.int32, (NB, WIN), 0)
+    column = lax.broadcasted_iota(jnp.int32, (1, WIN), 1)
+    group = 8
+    for w in range(windows):
+
+        @pl.loop(0, H // 4)
+        def _(quad, w=w):
+            attend(w, quad * 2)
+            attend(w, quad * 2 + 1)
+
+        def count_group(at, w=w):
+            hits, terms = [], []
+            for step in range(group):
+                i = at * group + step
+                indices = (
+                    linear_bucket(column - i),
+                    buckets[0, pl.ds(w * WIN + i, 1), :],
+                    buckets[1, pl.ds(w * WIN + i, 1), :],
+                )
+                hits.append(
+                    jnp.concatenate(
+                        [(index == bucket).astype(jnp.float32) for index in indices], axis=0
+                    ).astype(jnp.bfloat16)
+                )
+                terms.append(
+                    spread[pl.ds(pl.multiple_of(i * 16, 16), 16), :].astype(jnp.bfloat16)
+                )
+            return contract(jnp.concatenate(terms, axis=1), jnp.concatenate(hits, axis=1), 1, 1)
+
+        @pl.loop(0, WIN // group)
+        def _(at):
+            small[16:32, 0 : 3 * NB] += count_group(at)
+
+    loads[3].wait()
+    add_row(0, dqkv_ref[:, :width].astype(jnp.float32))
+    add_row(1, dqkv_ref[:, 2 * width :].astype(jnp.float32))
+    dx_ref[...] = grad[...] + contract(dqkv_ref[...], w_in[...], 1, 1)
+    small_ref[...] = small[...].astype(jnp.bfloat16)
+
+
+def backward_layer(incoming, weights, kept, buckets):
+    w_in, w_out, w_up, w_down, vectors, _, _ = weights
+    rows, width = incoming.shape
+    hidden = w_up.shape[1]
+    low, full = jnp.bfloat16, jnp.float32
+    narrow = jax.ShapeDtypeStruct((rows, width), low)
+    vmem = pl.BlockSpec(memory_space=pltpu.MemorySpace.VMEM)
+    hbm = pl.BlockSpec(memory_space=pltpu.MemorySpace.HBM)
+    q, k, v, _, p, _, n1, r1, slope, _, n2, r2 = kept
+    return pl.pallas_call(
+        backward_kernel,
+        out_shape=[
+            jax.ShapeDtypeStruct((rows, width), full),
+            narrow,
+            jax.ShapeDtypeStruct((rows, hidden), low),
+            narrow,
+            jax.ShapeDtypeStruct((rows, 3 * width), low),
+            jax.ShapeDtypeStruct((64, width), low),
+        ],
+        in_specs=[vmem] * 12 + [hbm] * 4,
+        out_specs=[vmem] * 6,
+        scratch_shapes=[
+            pltpu.VMEM(w_down.shape, low), pltpu.VMEM(w_up.shape, low),
+            pltpu.VMEM(w_out.shape, low), pltpu.VMEM(w_in.shape, low),
+            pltpu.VMEM((64, width), full), pltpu.VMEM((rows, width), full),
+            pltpu.VMEM((rows, width), low), pltpu.VMEM((WIN * 16, WIN), full),
+            pltpu.SemaphoreType.DMA((4,)),
+        ],
+        compiler_params=pltpu.CompilerParams(vmem_limit_bytes=56 * 1024 * 1024),
+    )(incoming, n2, r2, slope, n1, r1, p, q, k, v, buckets, vectors, w_down, w_up, w_out, w_in)
 
 
 def local(
@@ -732,38 +836,35 @@
     gains,
     tables,
 ):
-    pair_mask, linear, across = geometry(doc_lengths, live_mask, layout_buckets)
-    layer_total = attn_in.shape[0]
+    shards = lax.axis_size("fsdp")
+    weights_list = fetch_all(
+        attn_in, attn_out, ffn_in, ffn_out, biases, ffn_in_bias, gains, tables, shards
+    )
+    live = live_mask.reshape(-1, WIN)
     current = tokens
-    layer_inputs = []
-    kept_list = []
-    shards = lax.axis_size("fsdp")
-    fetched_list = fetch_all(
-        attn_in, attn_out, ffn_in, ffn_out, biases, ffn_in_bias, gains, tables, shards
-    )
-    outputs = []
-    for layer_index in range(layer_total):
-        fetched = fetched_list[layer_index]
-        result, kept = layer_forward(current, fetched, pair_mask, linear, across)
+    layer_inputs, kept_list, outputs = [], [], []
+    for weights in weights_list:
         layer_inputs.append(current)
+        current, *kept = forward_layer(current, weights, layout_buckets, live, doc_lengths)
         kept_list.append(kept)
-        current = result.astype(jnp.bfloat16)
         outputs.append(current)
-    grad_inputs = out_grad.astype(jnp.float32) * mlm_mask.astype(jnp.float32)[:, None]
-    shard_list = []
-    for layer_index in reversed(range(layer_total)):
-        grad_inputs, grads = layer_backward(
-            grad_inputs,
-            layer_inputs[layer_index],
-            fetched_list[layer_index],
-            kept_list[layer_index],
-            pair_mask,
-            linear,
-            across,
-        )
-        shard_list.insert(0, grads)
-    summed = sum_gradients(shard_list, shards, lax.axis_size("dp"))
-    return (jnp.stack(outputs), grad_inputs) + summed
+    incoming = out_grad.astype(jnp.float32) * mlm_mask.astype(jnp.float32)[:, None]
+    members, smalls = [], []
+    for layer in reversed(range(len(weights_list))):
+        kept = kept_list[layer]
+        incoming, df, du, da, dqkv, small = backward_layer(
+            incoming, weights_list[layer], kept, layout_buckets
+        )
+        pairs = ((layer_inputs[layer], dqkv), (kept[3], da), (kept[5], du), (kept[9], df))
+        members = [
+            jnp.einsum("nd,ne->de", left, right, preferred_element_type=jnp.float32).astype(
+                jnp.bfloat16
+            )
+            for left, right in pairs
+        ] + members
+        smalls = [small] + smalls
+    summed = sum_gradients(members, smalls, shards, lax.axis_size("dp"))
+    return (jnp.stack(outputs), incoming) + summed
 
 
 def solution(mesh):

time: 594 us -> 408 us (0.69); the launches traced: 587 us -> 408 us
  local copies, waits for them, and re-layouts: 135 us -> 11.5 us
  matrix products: 144 us -> 25.7 us
  Pallas kernels: 268 us -> 357 us
  other arithmetic: 36.7 us -> 12.9 us
    dot_general x48 -> x8, matrix products: 144 us -> 25.7 us  [local(): jnp.einsum('nd,ne->de', left, right, preferred_element_type=jnp.float32)]
    pallas_call x0 -> x4, Pallas kernels: none -> 88.8 us  [the longest x2 49.8 us: backward_layer(): pl.pallas_call(backward_kernel, out_shape=[jax.ShapeDtypeStruct((rows, wi...]
    another operation x30 -> x0, local copies, waits for them, and re-layouts: 34.8 us -> none  [the longest x14 13.1 us: layer_backward(): jnp.stack([grad_query_shift, grad_value_shift, grad_attended_shift, grad_...]
    reshape x26 -> x1, local copies, waits for them, and re-layouts: 22.2 us -> 0.1 us  [sum_gradients(): table = small[:, 16:16 + H, :3 * NB].reshape(layers, H, 3, NB)]
    reduce_sum x14 -> x0, other arithmetic: 13.7 us -> none  [the longest x2 3.64 us: layer_backward(): jnp.einsum('bij,whij->bh', linear, grad_scores, preferred_element_type=jn...]
    dot_general x6 -> x0, local copies, waits for them, and re-layouts: 13.5 us -> none  [the longest x2 5.63 us: pair_terms_of(): jnp.einsum('wbij,bh->whij', across[0], bias_table[1], preferred_element_t...]
    unnamed x233 -> x55, local copies, waits for them, and re-layouts: 17.1 us -> 4.7 us
    convert_element_type x11 -> x9, local copies, waits for them, and re-layouts: 12.6 us -> 0.63 us  [fetch_all(): piece.astype(jnp.float32)]
where the time goes in v3:
time: 408 us
  Pallas kernels  357 us (88%)
  matrix products  25.7 us (6%)
  other arithmetic  12.9 us (3%)
  local copies, waits for them, and re-layouts  11.5 us (3%)
    pallas_call x1, Pallas kernels, reduce_gradients(): pl.pallas_call(functools.partial(reduce_kernel, high, count, segments, le...  190 us
    pallas_call x1, Pallas kernels, gather_weights(): pl.pallas_call(functools.partial(gather_kernel, tuple(items)), out_shape=...  78.3 us
    pallas_call x2, Pallas kernels, backward_layer(): pl.pallas_call(backward_kernel, out_shape=[jax.ShapeDtypeStruct((rows, wi...  49.8 us
    pallas_call x2, Pallas kernels, forward_layer(): pl.pallas_call(forward_kernel, out_shape=[narrow, narrow, narrow, narrow,...  39.1 us
    dot_general x8, matrix products, local(): jnp.einsum('nd,ne->de', left, right, preferred_element_type=jnp.float32)  25.7 us
    convert_element_type x4, other arithmetic, sum_gradients(): jnp.stack([reduced[4 * layer + member] for layer in range(layers)])  9.87 us

profile of v3, /device:TPU:0, one launch (start us, length us, event | category | flops | bytes accessed | tf_op | source)
XLA Modules:
  0.0 408.1 jit_solution(7511159412173609466)
XLA Ops:
  2.1 0.8 reshape.73
  2.9 0.8 reshape.74
  4.4 78.3 %shard_map.213 = (bf16[64,768]{1,0:T(8,128)(2,1)}, bf16[768,2304]{1,0:T(8,128)(2,1)}, bf16[768,768]{1,0:T(8,128)(2,1)}, bf16[768,3072]{1,0:T(8,128)(2,1)}, bf16[...) custom-call(bf16[2,192,2304]{2,1,0:T(8,128)(2,1)} %refs_0_.1, ...), custom_call_target="tpu_custom_call" | custom-call | tf_op jit(solution)/shard_map/pallas_call | solution.py:445
  82.7 0.9 reshape.76
  86.3 19.6 %shard_map.214 = (bf16[256,768]{1,0:T(8,128)(2,1)}, bf16[256,768]{1,0:T(8,128)(2,1)}, bf16[256,768]{1,0:T(8,128)(2,1)}, bf16[256,768]{1,0:T(8,128)(2,1)}, bf16[2...) custom-call(bf16[256,768]{1,0:T(8,128)(2,1)} %x_ref.1, ...), custom_call_target="tpu_custom_call" | custom-call | tf_op jit(solution)/shard_map/pallas_call | solution.py:639
  106.5 19.5 %shard_map.215 = (bf16[256,768]{1,0:T(8,128)(2,1)}, bf16[256,768]{1,0:T(8,128)(2,1)}, bf16[256,768]{1,0:T(8,128)(2,1)}, bf16[256,768]{1,0:T(8,128)(2,1)}, bf16[2...) custom-call(bf16[256,768]{1,0:T(8,128)(2,1)} %get-tuple-element.72.x, ...), custom_call_target="tpu_custom_call" | custom-call | tf_op jit(solution)/shard_map/pallas_call | solution.py:639
  126.0 1.0 convert_multiply_fusion.dz_ref
  127.0 24.9 %shard_map.216 = (f32[256,768]{1,0:T(8,128)}, bf16[256,768]{1,0:T(8,128)(2,1)}, bf16[256,3072]{1,0:T(8,128)(2,1)}, bf16[256,768]{1,0:T(8,128)(2,1)}, bf16[256,2304]{1,0:T(8,128)(2,1)}, /*index=5*/bf16[64,768]{1,0:T(8,128)(2,1)}) custom-call(f32[256,768]{1,0:T(8,128)} %convert_multiply_fusion.dz_ref, f32[256,768]{1,0:T(8,128)} %get-tuple-element.78.n2_ref, ...), custom_call_target="tpu_custom_call" | custom-call | tf_op jit(solution)/shard_map/pallas_call | solution.py:800
  151.9 4.8 %convolution_convert_fusion.refs_7_ = bf16[3072,768]{1,0:T(8,128)(2,1)} fusion(bf16[256,3072]{1,0:T(8,128)(2,1)S(1)} %copy-done.3, bf16[256,768]{1,0:T(8,128)(2,1)} %get-tuple-element.111), kind=kOutput, calls=%fused_computation | convolution fusion | flops 1210318848 | bytes 6684672 | tf_op jit(solution)/shard_map/nd,ne->de/dot_general | solution.py:860
  156.8 3.6 convolution_convert_fusion.1.refs_6_
  160.4 1.5 convolution_convert_fusion.6.refs_5_
  161.9 3.0 convolution_convert_fusion.2.refs_4_
  164.9 24.9 %shard_map.217 = (f32[256,768]{1,0:T(8,128)}, bf16[256,768]{1,0:T(8,128)(2,1)}, bf16[256,3072]{1,0:T(8,128)(2,1)}, bf16[256,768]{1,0:T(8,128)(2,1)}, bf16[256,2304]{1,0:T(8,128)(2,1)}, /*index=5*/bf16[64,768]{1,0:T(8,128)(2,1)}) custom-call(f32[256,768]{1,0:T(8,128)} %get-tuple-element.87.dz_ref, f32[256,768]{1,0:T(8,128)} %get-tuple-element.88.n2_ref, ...), custom_call_target="tpu_custom_call" | custom-call | tf_op jit(solution)/shard_map/pallas_call | solution.py:800
  189.8 4.8 %convolution_convert_fusion.3.refs_3_ = bf16[3072,768]{1,0:T(8,128)(2,1)} fusion(bf16[256,3072]{1,0:T(8,128)(2,1)S(1)} %copy-done.2, bf16[256,768]{1,0:T(8,128)(2,1)} %get-tuple-element.104), kind=kOutput, calls=%fused_computation.3 | convolution fusion | flops 1210318848 | bytes 6684672 | tf_op jit(solution)/shard_map/nd,ne->de/dot_general | solution.py:860
  194.6 3.6 convolution_convert_fusion.4.refs_2_
  198.2 1.5 convolution_convert_fusion.7.refs_1_
  199.8 2.9 fusion.refs_0_
  202.7 189.9 %shard_map.218 = (bf16[192,2304]{1,0:T(8,128)(2,1)}, bf16[192,768]{1,0:T(8,128)(2,1)}, bf16[192,3072]{1,0:T(8,128)(2,1)}, bf16[768,768]{1,0:T(8,128)(2,1)}, bf16...) custom-call(bf16[768,2304]{1,0:T(8,128)(2,1)} %fusion.refs_0_, ...), custom_call_target="tpu_custom_call" | custom-call | tf_op jit(solution)/shard_map/pallas_call | solution.py:261
  392.5 1.0 maximum_convert_fusion.4
  396.4 4.3 %maximum_convert_fusion.1 = f32[2,768,768]{2,1,0:T(8,128)} fusion(bf16[1,768,768]{2,1,0:T(8,128)(2,1)} %bitcast.70, bf16[1,768,768]{2,1,0:T(8,128)(2,1)} %bitcast.69), kind=kLoop, calls=%fused_computation.8 | loop fusion | flops 2359296 | bytes 7077888 | tf_op jit(solution)/shard_map/convert_element_type | solution.py:286
  400.7 2.5 maximum_convert_fusion
  403.2 1.1 maximum_convert_fusion.3
  405.1 2.0 maximum_convert_fusion.2
  407.1 0.9 pad_maximum_fusion
  (86 shorter events, 9.1 us)
Async XLA Ops:
  106.5 19.5 %copy-start.23 = (s32[256]{0:T(256)S(1)}, s32[256]{0:T(256)}, u32[]{:S(2)}) copy-start(s32[256]{0:T(256)} %param.16) | copy-start | bytes 3076
  106.5 19.5 %copy-start.15 = (bf16[256,768]{1,0:T(8,128)(2,1)S(1)}, bf16[256,768]{1,0:T(8,128)(2,1)}, u32[]{:S(2)}) copy-start(bf16[256,768]{1,0:T(8,128)(2,1)} %param.15) | copy-start | bytes 1179652
  127.0 24.9 %copy-start.3 = (bf16[256,3072]{1,0:T(8,128)(2,1)S(1)}, bf16[256,3072]{1,0:T(8,128)(2,1)}, u32[]{:S(2)}) copy-start(bf16[256,3072]{1,0:T(8,128)(2,1)} %get-tuple-element.110) | copy-start | bytes 4718596
  151.9 4.8 %copy-start.5 = (bf16[256,3072]{1,0:T(8,128)(2,1)S(1)}, bf16[256,3072]{1,0:T(8,128)(2,1)}, u32[]{:S(2)}) copy-start(bf16[256,3072]{1,0:T(8,128)(2,1)} %get-tuple-element.109) | copy-start | bytes 4718596
  151.9 4.8 %copy-start.14 = (bf16[256,768]{1,0:T(8,128)(2,1)S(1)}, bf16[256,768]{1,0:T(8,128)(2,1)}, u32[]{:S(2)}) copy-start(bf16[256,768]{1,0:T(8,128)(2,1)} %get-tuple-element.108) | copy-start | bytes 1179652
  156.8 3.6 copy-start.18
  156.8 3.6 copy-start.20
  160.3 1.5 copy-start
  160.3 1.5 copy-start.10
  164.9 24.9 %copy-start.2 = (bf16[256,3072]{1,0:T(8,128)(2,1)S(1)}, bf16[256,3072]{1,0:T(8,128)(2,1)}, u32[]{:S(2)}) copy-start(bf16[256,3072]{1,0:T(8,128)(2,1)} %get-tuple-element.103) | copy-start | bytes 4718596
  189.8 4.8 %copy-start.6 = (bf16[256,3072]{1,0:T(8,128)(2,1)S(1)}, bf16[256,3072]{1,0:T(8,128)(2,1)}, u32[]{:S(2)}) copy-start(bf16[256,3072]{1,0:T(8,128)(2,1)} %get-tuple-element.102) | copy-start | bytes 4718596
  189.8 4.8 %copy-start.13 = (bf16[256,768]{1,0:T(8,128)(2,1)S(1)}, bf16[256,768]{1,0:T(8,128)(2,1)}, u32[]{:S(2)}) copy-start(bf16[256,768]{1,0:T(8,128)(2,1)} %get-tuple-element.101) | copy-start | bytes 1179652
  194.6 3.6 copy-start.17
  194.6 3.6 copy-start.19
  198.2 1.6 copy-start.4
  198.2 1.6 copy-start.7
  396.4 4.3 %copy-start.8 = (bf16[192,3072]{1,0:T(8,128)(2,1)S(1)}, bf16[192,3072]{1,0:T(8,128)(2,1)}, u32[]{:S(2)}) copy-start(bf16[192,3072]{1,0:T(8,128)(2,1)} %get-tuple-element.118) | copy-start | bytes 3538948
  396.4 4.3 %copy-start.9 = (bf16[192,3072]{1,0:T(8,128)(2,1)S(1)}, bf16[192,3072]{1,0:T(8,128)(2,1)}, u32[]{:S(2)}) copy-start(bf16[192,3072]{1,0:T(8,128)(2,1)} %get-tuple-element.119) | copy-start | bytes 3538948
  400.7 2.5 copy-start.21
  400.7 2.5 copy-start.22
  403.2 1.6 copy-start.11
  403.2 1.9 copy-start.12
  405.1 2.0 copy-start.1
  405.1 2.0 copy-start.16

commit v4 on v3

--- a/solution.py
+++ b/solution.py
@@ -16,7 +16,7 @@
 
 
 EPSILON = 1e-05
-LAG = 2
+LAG = 1
 
 
 def norm_forward(values, gain_row, shift_row):
@@ -298,11 +298,18 @@
     )
 
 
-def gather_kernel(items, *refs):
+def opening_kernel(items, *refs):
     total = len(items)
-    sources, targets = refs[:5], refs[5 : 5 + total]
-    stages = refs[5 + total : 5 + 2 * total]
-    load_sem, store_sem, send_sem, arrive = refs[5 + 2 * total :]
+    ready = 1 + 4
+    sources, forward_in = refs[:5], refs[5:9]
+    outs = refs[9 : 9 + total - 1 + 3 + 13]
+    vectors, up_shifts, table = outs[total - 1 : total + 2]
+    forward_out = outs[total + 2 :]
+    rest = refs[9 + len(outs) :]
+    stages, rest = rest[:total], rest[total:]
+    landing_small, load_sem, store_sem, send_sem, arrive = rest[:5]
+    forward_scratch = rest[5:]
+    targets = (landing_small,) + tuple(outs[: total - 1])
     dp = lax.axis_index("dp")
     shard = lax.axis_index("fsdp")
     x_at, core = lax.div(shard, 2), lax.rem(shard, 2)
@@ -333,9 +340,15 @@
         return stages[i].shape[0]
 
     def parts_of(i):
-        return 4 if depth_of(i) % 64 == 0 else 1
+        return 1 if i == 0 else 4
+
+    def small_lanes(at):
+        size = stages[0].shape[1]
+        return landing_small.at[:, pl.ds(pl.multiple_of(at * size, size), size)]
 
     def mine_out(i):
+        if i == 0:
+            return small_lanes(shard)
         n = depth_of(i)
         return targets[i].at[pl.ds(pl.multiple_of(shard * n, 16), n)]
 
@@ -345,6 +358,8 @@
         return targets[i].at[pl.ds(pl.multiple_of(other * n + quarter * part, 16), part)]
 
     def other_whole(i):
+        if i == 0:
+            return small_lanes(other)
         n = depth_of(i)
         return targets[i].at[pl.ds(pl.multiple_of(other * n, 16), n)]
 
@@ -358,6 +373,8 @@
         return now[1] * 2 + now[0]
 
     def x_send(i):
+        if i == 0:
+            return copy(shard_of(i), small_lanes(shard), i, 0, x_peer)
         n = depth_of(i)
         part = n // parts_of(i)
         start = pl.multiple_of(quarter_of(i, ()) * part, 16)
@@ -414,81 +431,133 @@
             relay_send(i).wait_recv()
         far_share(i).start()
 
-    for step in range(total + 4):
-        if step < total:
+    def arrived(i):
+        own_share(i).wait_recv()
+        far_share(i).wait_recv()
+        store(i).wait()
+
+    for step in range(ready + 3):
+        if step < ready:
             spread(step)
-        if 0 <= step - 1 < total:
+        elif step < total:
+            spread(step)
+        if 0 <= step - 1 < ready:
             relay(step - 1)
-        if 0 <= step - 3 < total:
+        if 0 <= step - 3 < ready:
             share(step - 3)
+    for i in range(ready):
+        arrived(i)
+    place_small(landing_small, vectors, up_shifts, table)
+
+    waiting = [functools.partial(spread, i) for i in range(ready + 3, total)]
+    waiting += [functools.partial(relay, i) for i in range(ready, total)]
+    waiting += [functools.partial(share, i) for i in range(ready, total)]
+    points = 4
+    per_point = -(-len(waiting) // points)
+
+    def service(point):
+        for act in waiting[point * per_point : (point + 1) * per_point]:
+            act()
+
+    forward_core(
+        0, service, *forward_in, vectors, up_shifts, table, *targets[1:5], *forward_out,
+        *forward_scratch,
+    )
+    for i in range(ready, total):
+        arrived(i)
     for i in range(total):
-        own_share(i).wait()
-        far_share(i).wait()
+        own_share(i).wait_send()
+        far_share(i).wait_send()
         x_send(i).wait_send()
         if parts_of(i) == 4:
             first_send(i).wait_send()
             second_send(i).wait_send()
             relay_send(i).wait_send()
-        store(i).wait()
-
-
-def gather_weights(sources, small, shards):
+
+
+def place_small(landing, vectors, up_shifts, table):
+    lanes = landing.shape[1]
+    each = 2 * WIN
+    shards = lanes // each
+
+    def selected(rows, own, width):
+        source = lax.broadcasted_iota(jnp.int32, (lanes, width), 0)
+        target = lax.broadcasted_iota(jnp.int32, (lanes, width), 1)
+        within = source % each
+        picked = (within < own) & (target == source // each * own + within)
+        return jnp.dot(
+            landing[rows, :], picked.astype(jnp.float32).astype(jnp.bfloat16),
+            preferred_element_type=jnp.float32,
+        )
+
+    layers = up_shifts.shape[0]
+    width = vectors.shape[1]
+    vectors[...] = selected(pl.ds(0, 16), width // shards, width)
+    shift_rows = landing[16:32, :].astype(jnp.float32)
+    runs = width // each
+    for layer in range(layers):
+        for shard in range(shards):
+            for run in range(runs):
+                start = shard * width + run * each
+                up_shifts[layer : layer + 1, start : start + each] = shift_rows[
+                    layer * runs + run : layer * runs + run + 1,
+                    shard * each : (shard + 1) * each,
+                ]
+    table[...] = selected(pl.ds(32, table.shape[0]), NB // shards, WIN)
+
+
+def small_rows(biases, ffn_in_bias, gains, tables):
+    layers = biases.shape[0]
+    each = 2 * WIN
+    vectors = jnp.concatenate([biases, gains], axis=1).reshape(layers * 8, -1)
+    vectors = jnp.pad(vectors, ((0, 16 - 8 * layers), (0, each - vectors.shape[1])))
+    shifts = ffn_in_bias.reshape(-1, each)
+    shifts = jnp.pad(shifts, ((0, 16 - shifts.shape[0]), (0, 0)))
+    entries = jnp.swapaxes(tables, 2, 3)
+    entries = jnp.pad(
+        entries, ((0, 0), (0, 0), (0, 16 - H), (0, each - entries.shape[3]))
+    ).reshape(layers * 48, each)
+    return jnp.concatenate([vectors, shifts, entries], axis=0)
+
+
+def open_layers(sources, small, shards, inputs, buckets, live, lengths):
     layers = sources[0].shape[0]
-    items = [(4, None)]
-    forms = [small.shape]
-    for layer in range(layers):
-        for member in range(4):
-            items.append((member, layer))
-            forms.append(sources[member].shape[1:])
-    hbm = pl.BlockSpec(memory_space=pltpu.MemorySpace.HBM)
+    rows, width = inputs.shape
+    items = [(4, None)] + [(member, layer) for layer in range(layers) for member in range(4)]
+    forms = [small.shape] + [sources[member].shape[1:] for member, _ in items[1:]]
     total = len(items)
-    return pl.pallas_call(
-        functools.partial(gather_kernel, tuple(items)),
+    hidden = sources[2].shape[2]
+    outs, scratch = forward_forms(rows, width, hidden)
+    vmem, hbm, smem = memory_specs()
+    shared = [
+        jax.ShapeDtypeStruct((16, width), jnp.float32),
+        jax.ShapeDtypeStruct((layers, hidden), jnp.float32),
+        jax.ShapeDtypeStruct((layers * 48, WIN), jnp.float32),
+    ]
+    results = pl.pallas_call(
+        functools.partial(opening_kernel, tuple(items)),
         out_shape=[
-            jax.ShapeDtypeStruct((form[0] * shards, form[1]), jnp.bfloat16) for form in forms
-        ],
-        in_specs=[hbm] * 5,
-        out_specs=[hbm] * total,
+            jax.ShapeDtypeStruct((form[0] * shards, form[1]), jnp.bfloat16) for form in forms[1:]
+        ]
+        + shared
+        + outs,
+        in_specs=[hbm] * 5 + [vmem, vmem, vmem, smem],
+        out_specs=[hbm] * (total - 1) + [vmem] * (3 + len(outs)),
         scratch_shapes=[pltpu.VMEM(form, jnp.bfloat16) for form in forms]
         + [
+            pltpu.VMEM((small.shape[0], small.shape[1] * shards), jnp.bfloat16),
             pltpu.SemaphoreType.DMA((total,)),
             pltpu.SemaphoreType.DMA((total,)),
             pltpu.SemaphoreType.DMA((total, 6)),
             pltpu.SemaphoreType.DMA((total, 6)),
-        ],
-        compiler_params=pltpu.CompilerParams(collective_id=0, has_side_effects=True),
-    )(*sources, small)
-
-
-def fetch_all(attn_in, attn_out, ffn_in, ffn_out, biases, ffn_in_bias, gains, tables, shards):
-    layers, depth = attn_in.shape[0], attn_in.shape[1]
-    width = depth * shards
-    flat = jnp.concatenate(
-        [member.reshape(-1) for member in (biases, ffn_in_bias, gains, tables)]
-    )
-    rows = -(-flat.shape[0] // (16 * width)) * 16
-    small = jnp.pad(flat, (0, rows * width - flat.shape[0])).reshape(rows, width)
-    gathered = gather_weights((attn_in, attn_out, ffn_in, ffn_out), small, shards)
-    small = gathered[0].reshape(shards, -1)
-    pieces = []
-    start = 0
-    for member, axis in ((biases, 2), (ffn_in_bias, 1), (gains, 2), (tables, 2)):
-        piece = small[:, start : start + member.size].reshape((shards,) + member.shape)
-        start += member.size
-        piece = jnp.moveaxis(piece, 0, axis)
-        pieces.append(
-            piece.reshape(member.shape[:axis] + (-1,) + member.shape[axis + 1 :])
-        )
-    shifts, up_shift, gain_rows, table = [piece.astype(jnp.float32) for piece in pieces]
-    vectors = jnp.concatenate([shifts, gain_rows], axis=1)
-    table = jnp.pad(
-        jnp.swapaxes(table, 2, 3), ((0, 0), (0, 0), (0, 16 - H), (0, WIN - NB))
-    )
-    return [
-        tuple(gathered[1 + 4 * layer : 5 + 4 * layer])
-        + (vectors[layer], up_shift[layer : layer + 1], table[layer])
-        for layer in range(layers)
-    ]
+        ]
+        + scratch,
+        compiler_params=pltpu.CompilerParams(
+            collective_id=0, has_side_effects=True, vmem_limit_bytes=58 * 1024 * 1024
+        ),
+    )(*sources, small, inputs, buckets, live, lengths)
+    weights = [results[4 * layer : 4 * layer + 4] for layer in range(layers)]
+    return weights, results[total - 1 : total + 2], results[total + 2 :]
 
 
 def contract(left, right, left_axis, right_axis):
@@ -512,9 +581,13 @@
     return first.astype(jnp.bfloat16), (1.0 - first).astype(jnp.bfloat16)
 
 
-def forward_kernel(
-    x_ref, buckets, live, lengths, vectors, up_shift, table, w_in_hbm, w_out_hbm, w_up_hbm,
-    w_down_hbm, out_ref, q_ref, k_ref, v_ref, o_ref, p_ref, low_ref, n1_ref, r1_ref, slope_ref,
+def forward_kernel(layer, *refs):
+    forward_core(layer, lambda point: None, *refs)
+
+
+def forward_core(
+    layer, service, x_ref, buckets, live, lengths, all_vectors, up_shifts, table, w_in_hbm,
+    w_out_hbm, w_up_hbm, w_down_hbm, out_ref, q_ref, k_ref, v_ref, o_ref, p_ref, low_ref, n1_ref, r1_ref, slope_ref,
     g_ref, n2_ref, r2_ref, w_in, w_out, w_up, w_down, allowed, y1, total, sem,
 ):
     loads = [
@@ -525,6 +598,8 @@
     ]
     for load in loads:
         load.start()
+    vectors = all_vectors.at[pl.ds(8 * layer, 8)]
+    up_shift = up_shifts.at[pl.ds(layer, 1)]
     rows, width = x_ref.shape
     windows = rows // WIN
     row, column = positions_of(0), positions_of(1)
@@ -554,6 +629,7 @@
         jnp.dot(inputs, w_in[:, 2 * width :], preferred_element_type=jnp.float32)
         + vectors[1:2, :]
     ).astype(jnp.bfloat16)
+    service(0)
 
     def attend(w, pair):
         span = pl.ds(w * WIN, WIN)
@@ -565,7 +641,8 @@
             scores = contract(queries * half, keys, 1, 1)
             bias = 0.0
             for kind, index in enumerate((offset, buckets[0, span, :], buckets[1, span, :])):
-                entries = jnp.broadcast_to(table[kind, pl.ds(head, 1), :], (WIN, WIN))
+                entry = table[pl.ds(48 * layer + 16 * kind + head, 1), :]
+                entries = jnp.broadcast_to(entry, (WIN, WIN))
                 bias = bias + jnp.take_along_axis(
                     entries, index, axis=1, mode="promise_in_bounds"
                 )
@@ -587,6 +664,8 @@
             attend(w, quad * 2)
             attend(w, quad * 2 + 1)
 
+        service(1 + w)
+
     loads[1].wait()
     attended = (
         jnp.dot(o_ref[...], w_out[...], preferred_element_type=jnp.float32) + vectors[2:3, :]
@@ -599,6 +678,7 @@
     y1[...] = first_norm
     low_ref[...] = first_norm.astype(jnp.bfloat16)
     total[...] = jnp.zeros_like(total)
+    service(1 + windows)
     loads[2].wait()
     loads[3].wait()
 
@@ -625,43 +705,55 @@
     out_ref[...] = result.astype(jnp.bfloat16)
 
 
-def forward_layer(inputs, weights, buckets, live, lengths):
-    w_in, w_out, w_up, w_down, vectors, up_shift, table = weights
-    rows, width = inputs.shape
-    hidden = w_up.shape[1]
+def forward_forms(rows, width, hidden):
     low, full = jnp.bfloat16, jnp.float32
     narrow = jax.ShapeDtypeStruct((rows, width), low)
     wide = jax.ShapeDtypeStruct((rows, width), full)
     column = jax.ShapeDtypeStruct((rows, WIN), full)
-    vmem = pl.BlockSpec(memory_space=pltpu.MemorySpace.VMEM)
-    hbm = pl.BlockSpec(memory_space=pltpu.MemorySpace.HBM)
-    smem = pl.BlockSpec(memory_space=pltpu.MemorySpace.SMEM)
+    outs = [
+        narrow, narrow, narrow, narrow, narrow,
+        jax.ShapeDtypeStruct((rows // WIN * H, WIN, WIN), full),
+        narrow, wide, column,
+        jax.ShapeDtypeStruct((rows, hidden), full),
+        jax.ShapeDtypeStruct((rows, hidden), low),
+        wide, column,
+    ]
+    scratch = [
+        pltpu.VMEM((width, 3 * width), low), pltpu.VMEM((width, width), low),
+        pltpu.VMEM((width, hidden), low), pltpu.VMEM((hidden, width), low),
+        pltpu.VMEM((rows // WIN, WIN, WIN), jnp.int32),
+        pltpu.VMEM((rows, width), full), pltpu.VMEM((rows, width), full),
+        pltpu.SemaphoreType.DMA((4,)),
+    ]
+    return outs, scratch
+
+
+def memory_specs():
+    return [
+        pl.BlockSpec(memory_space=space)
+        for space in (
+            pltpu.MemorySpace.VMEM, pltpu.MemorySpace.HBM, pltpu.MemorySpace.SMEM
+        )
+    ]
+
+
+def forward_layer(layer, inputs, weights, shared, buckets, live, lengths):
+    rows, width = inputs.shape
+    outs, scratch = forward_forms(rows, width, weights[2].shape[1])
+    vmem, hbm, smem = memory_specs()
     return pl.pallas_call(
-        forward_kernel,
-        out_shape=[
-            narrow, narrow, narrow, narrow, narrow,
-            jax.ShapeDtypeStruct((rows // WIN * H, WIN, WIN), full),
-            narrow, wide, column,
-            jax.ShapeDtypeStruct((rows, hidden), full),
-            jax.ShapeDtypeStruct((rows, hidden), low),
-            wide, column,
-        ],
+        functools.partial(forward_kernel, layer),
+        out_shape=outs,
         in_specs=[vmem, vmem, vmem, smem, vmem, vmem, vmem, hbm, hbm, hbm, hbm],
-        out_specs=[vmem] * 13,
-        scratch_shapes=[
-            pltpu.VMEM(w_in.shape, low), pltpu.VMEM(w_out.shape, low),
-            pltpu.VMEM(w_up.shape, low), pltpu.VMEM(w_down.shape, low),
-            pltpu.VMEM((rows // WIN, WIN, WIN), jnp.int32),
-            pltpu.VMEM((rows, width), full), pltpu.VMEM((rows, width), full),
-            pltpu.SemaphoreType.DMA((4,)),
-        ],
+        out_specs=[vmem] * len(outs),
+        scratch_shapes=scratch,
         compiler_params=pltpu.CompilerParams(vmem_limit_bytes=56 * 1024 * 1024),
-    )(inputs, buckets, live, lengths, vectors, up_shift, table, w_in, w_out, w_up, w_down)
+    )(inputs, buckets, live, lengths, *shared, *weights)
 
 
 def backward_kernel(
-    dz_ref, n2_ref, r2_ref, slope_ref, n1_ref, r1_ref, p_ref, q_ref, k_ref, v_ref, buckets,
-    vectors, w_down_hbm, w_up_hbm, w_out_hbm, w_in_hbm, dx_ref, df_ref, du_ref, da_ref, dqkv_ref,
+    layer, dz_ref, n2_ref, r2_ref, slope_ref, n1_ref, r1_ref, p_ref, q_ref, k_ref, v_ref, buckets,
+    all_vectors, w_down_hbm, w_up_hbm, w_out_hbm, w_in_hbm, dx_ref, df_ref, du_ref, da_ref, dqkv_ref,
     small_ref, w_down, w_up, w_out, w_in, small, grad, mixed, spread, sem,
 ):
     loads = [
@@ -672,6 +764,7 @@
     ]
     for load in loads:
         load.start()
+    vectors = all_vectors.at[pl.ds(8 * layer, 8)]
     rows, width = dz_ref.shape
     windows = rows // WIN
     first, second = lane_halves()
@@ -788,17 +881,16 @@
     small_ref[...] = small[...].astype(jnp.bfloat16)
 
 
-def backward_layer(incoming, weights, kept, buckets):
-    w_in, w_out, w_up, w_down, vectors, _, _ = weights
+def backward_layer(layer, incoming, weights, vectors, kept, buckets):
+    w_in, w_out, w_up, w_down = weights
     rows, width = incoming.shape
     hidden = w_up.shape[1]
     low, full = jnp.bfloat16, jnp.float32
     narrow = jax.ShapeDtypeStruct((rows, width), low)
-    vmem = pl.BlockSpec(memory_space=pltpu.MemorySpace.VMEM)
-    hbm = pl.BlockSpec(memory_space=pltpu.MemorySpace.HBM)
+    vmem, hbm, _ = memory_specs()
     q, k, v, _, p, _, n1, r1, slope, _, n2, r2 = kept
     return pl.pallas_call(
-        backward_kernel,
+        functools.partial(backward_kernel, layer),
         out_shape=[
             jax.ShapeDtypeStruct((rows, width), full),
             narrow,
@@ -837,15 +929,18 @@
     tables,
 ):
     shards = lax.axis_size("fsdp")
-    weights_list = fetch_all(
-        attn_in, attn_out, ffn_in, ffn_out, biases, ffn_in_bias, gains, tables, shards
+    live = live_mask.reshape(-1, WIN)
+    weights_list, shared, first = open_layers(
+        (attn_in, attn_out, ffn_in, ffn_out), small_rows(biases, ffn_in_bias, gains, tables),
+        shards, tokens, layout_buckets, live, doc_lengths,
     )
-    live = live_mask.reshape(-1, WIN)
-    current = tokens
-    layer_inputs, kept_list, outputs = [], [], []
-    for weights in weights_list:
+    current, *kept = first
+    layer_inputs, kept_list, outputs = [tokens], [kept], [current]
+    for layer in range(1, len(weights_list)):
         layer_inputs.append(current)
-        current, *kept = forward_layer(current, weights, layout_buckets, live, doc_lengths)
+        current, *kept = forward_layer(
+            layer, current, weights_list[layer], shared, layout_buckets, live, doc_lengths
+        )
         kept_list.append(kept)
         outputs.append(current)
     incoming = out_grad.astype(jnp.float32) * mlm_mask.astype(jnp.float32)[:, None]
@@ -853,7 +948,7 @@
     for layer in reversed(range(len(weights_list))):
         kept = kept_list[layer]
         incoming, df, du, da, dqkv, small = backward_layer(
-            incoming, weights_list[layer], kept, layout_buckets
+            layer, incoming, weights_list[layer], shared[0], kept, layout_buckets
         )
         pairs = ((layer_inputs[layer], dqkv), (kept[3], da), (kept[5], du), (kept[9], df))
         members = [

time: 408 us -> 391 us (0.958)
  Pallas kernels: 357 us -> 344 us
  local copies, waits for them, and re-layouts: 11.5 us -> 5.95 us
    pallas_call x5 -> x4, Pallas kernels: 167 us -> 153 us  [the longest x1 83.8 us: open_layers(): pl.pallas_call(functools.partial(opening_kernel, tuple(items)), out_shape...]
where the time goes in v4:
time: 391 us
  Pallas kernels  344 us (88%)
  matrix products  25.7 us (7%)
  other arithmetic  14.2 us (4%)
  local copies, waits for them, and re-layouts  5.95 us (2%)
    pallas_call x1, Pallas kernels, reduce_gradients(): pl.pallas_call(functools.partial(reduce_kernel, high, count, segments, le...  191 us
    pallas_call x1, Pallas kernels, open_layers(): pl.pallas_call(functools.partial(opening_kernel, tuple(items)), out_shape...  83.8 us
    pallas_call x2, Pallas kernels, backward_layer(): pl.pallas_call(functools.partial(backward_kernel, layer), out_shape=[jax....  49.7 us
    dot_general x8, matrix products, local(): jnp.einsum('nd,ne->de', left, right, preferred_element_type=jnp.float32)  25.7 us
    pallas_call x1, Pallas kernels, forward_layer(): pl.pallas_call(functools.partial(forward_kernel, layer), out_shape=outs,...  19.5 us
    convert_element_type x4, other arithmetic, sum_gradients(): jnp.stack([reduced[4 * layer + member] for layer in range(layers)])  9.87 us

profile of v4, /device:TPU:0, one launch (start us, length us, event | category | flops | bytes accessed | tf_op | source)
XLA Modules:
  0.0 390.6 jit_solution(12252005317784421881)
XLA Ops:
  0.6 0.8 copy.39
  2.2 0.7 pad_maximum_fusion.1
  2.9 0.7 reshape.37
  4.2 83.8 %shard_map.213 = (bf16[768,2304]{1,0:T(8,128)(2,1)}, bf16[768,768]{1,0:T(8,128)(2,1)}, bf16[768,3072]{1,0:T(8,128)(2,1)}, bf16[3072,768]{1,0:T(8,128)(2,1)}, bf1...) custom-call(bf16[2,192,2304]{2,1,0:T(8,128)(2,1)} %refs_0_.1, ...), custom_call_target="tpu_custom_call" | custom-call | tf_op jit(solution)/shard_map/pallas_call | solution.py:537
  88.1 19.5 %shard_map.214 = (bf16[256,768]{1,0:T(8,128)(2,1)}, bf16[256,768]{1,0:T(8,128)(2,1)}, bf16[256,768]{1,0:T(8,128)(2,1)}, bf16[256,768]{1,0:T(8,128)(2,1)}, bf16[2...) custom-call(bf16[256,768]{1,0:T(8,128)(2,1)} %get-tuple-element.69.r, ...), custom_call_target="tpu_custom_call" | custom-call | tf_op jit(solution)/shard_map/pallas_call | solution.py:744
  107.6 1.0 convert_multiply_fusion.dz_ref
  108.6 24.8 %shard_map.215 = (f32[256,768]{1,0:T(8,128)}, bf16[256,768]{1,0:T(8,128)(2,1)}, bf16[256,3072]{1,0:T(8,128)(2,1)}, bf16[256,768]{1,0:T(8,128)(2,1)}, bf16[256,2304]{1,0:T(8,128)(2,1)}, /*index=5*/bf16[64,768]{1,0:T(8,128)(2,1)}) custom-call(f32[256,768]{1,0:T(8,128)} %convert_multiply_fusion.dz_ref, f32[256,768]{1,0:T(8,128)} %get-tuple-element.78.n2_ref, ...), custom_call_target="tpu_custom_call" | custom-call | tf_op jit(solution)/shard_map/pallas_call | solution.py:892
  133.5 4.8 %convolution_convert_fusion.refs_7_ = bf16[3072,768]{1,0:T(8,128)(2,1)} fusion(bf16[256,3072]{1,0:T(8,128)(2,1)S(1)} %copy-done.3, bf16[256,768]{1,0:T(8,128)(2,1)} %get-tuple-element.115), kind=kOutput, calls=%fused_computation | convolution fusion | flops 1210318848 | bytes 6684672 | tf_op jit(solution)/shard_map/nd,ne->de/dot_general | solution.py:955
  138.3 3.5 convolution_convert_fusion.1.refs_6_
  141.9 1.5 convolution_convert_fusion.6.refs_5_
  143.4 3.0 convolution_convert_fusion.2.refs_4_
  146.4 24.8 %shard_map.216 = (f32[256,768]{1,0:T(8,128)}, bf16[256,768]{1,0:T(8,128)(2,1)}, bf16[256,3072]{1,0:T(8,128)(2,1)}, bf16[256,768]{1,0:T(8,128)(2,1)}, bf16[256,2304]{1,0:T(8,128)(2,1)}, /*index=5*/bf16[64,768]{1,0:T(8,128)(2,1)}) custom-call(f32[256,768]{1,0:T(8,128)} %get-tuple-element.87.dz_ref, f32[256,768]{1,0:T(8,128)} %get-tuple-element.88.n2_ref, ...), custom_call_target="tpu_custom_call" | custom-call | tf_op jit(solution)/shard_map/pallas_call | solution.py:892
  171.3 4.8 %convolution_convert_fusion.3.refs_3_ = bf16[3072,768]{1,0:T(8,128)(2,1)} fusion(bf16[256,3072]{1,0:T(8,128)(2,1)S(1)} %copy-done.2, bf16[256,768]{1,0:T(8,128)(2,1)} %get-tuple-element.108), kind=kOutput, calls=%fused_computation.3 | convolution fusion | flops 1210318848 | bytes 6684672 | tf_op jit(solution)/shard_map/nd,ne->de/dot_general | solution.py:955
  176.1 3.6 convolution_convert_fusion.4.refs_2_
  179.7 1.6 convolution_convert_fusion.7.refs_1_
  181.2 2.9 fusion.refs_0_
  184.2 190.9 %shard_map.217 = (bf16[192,2304]{1,0:T(8,128)(2,1)}, bf16[192,768]{1,0:T(8,128)(2,1)}, bf16[192,3072]{1,0:T(8,128)(2,1)}, bf16[768,768]{1,0:T(8,128)(2,1)}, bf16...) custom-call(bf16[768,2304]{1,0:T(8,128)(2,1)} %fusion.refs_0_, ...), custom_call_target="tpu_custom_call" | custom-call | tf_op jit(solution)/shard_map/pallas_call | solution.py:261
  375.1 1.0 maximum_convert_fusion.4
  376.3 0.7 copy.36
  378.9 4.3 %maximum_convert_fusion.1 = f32[2,768,768]{2,1,0:T(8,128)} fusion(bf16[1,768,768]{2,1,0:T(8,128)(2,1)} %bitcast.47, bf16[1,768,768]{2,1,0:T(8,128)(2,1)} %bitcast.46), kind=kLoop, calls=%fused_computation.8 | loop fusion | flops 2359296 | bytes 7077888 | tf_op jit(solution)/shard_map/convert_element_type | solution.py:286
  383.2 2.5 maximum_convert_fusion
  385.7 1.1 maximum_convert_fusion.3
  387.6 2.0 maximum_convert_fusion.2
  389.6 0.9 pad_maximum_fusion
  (63 shorter events, 4.4 us)
Async XLA Ops:
  88.1 19.6 %copy-start.23 = (s32[256]{0:T(256)S(1)}, s32[256]{0:T(256)}, u32[]{:S(2)}) copy-start(s32[256]{0:T(256)} %param.16) | copy-start | bytes 3076
  88.1 19.6 %copy-start.15 = (bf16[256,768]{1,0:T(8,128)(2,1)S(1)}, bf16[256,768]{1,0:T(8,128)(2,1)}, u32[]{:S(2)}) copy-start(bf16[256,768]{1,0:T(8,128)(2,1)} %param.15) | copy-start | bytes 1179652
  108.6 24.8 %copy-start.3 = (bf16[256,3072]{1,0:T(8,128)(2,1)S(1)}, bf16[256,3072]{1,0:T(8,128)(2,1)}, u32[]{:S(2)}) copy-start(bf16[256,3072]{1,0:T(8,128)(2,1)} %get-tuple-element.114) | copy-start | bytes 4718596
  133.5 4.8 %copy-start.7 = (bf16[256,3072]{1,0:T(8,128)(2,1)S(1)}, bf16[256,3072]{1,0:T(8,128)(2,1)}, u32[]{:S(2)}) copy-start(bf16[256,3072]{1,0:T(8,128)(2,1)} %get-tuple-element.113) | copy-start | bytes 4718596
  133.5 4.8 %copy-start.14 = (bf16[256,768]{1,0:T(8,128)(2,1)S(1)}, bf16[256,768]{1,0:T(8,128)(2,1)}, u32[]{:S(2)}) copy-start(bf16[256,768]{1,0:T(8,128)(2,1)} %get-tuple-element.112) | copy-start | bytes 1179652
  138.3 3.6 copy-start.18
  138.3 3.6 copy-start.20
  141.9 1.6 copy-start
  141.9 1.6 copy-start.10
  146.4 24.8 %copy-start.2 = (bf16[256,3072]{1,0:T(8,128)(2,1)S(1)}, bf16[256,3072]{1,0:T(8,128)(2,1)}, u32[]{:S(2)}) copy-start(bf16[256,3072]{1,0:T(8,128)(2,1)} %get-tuple-element.107) | copy-start | bytes 4718596
  171.3 4.8 %copy-start.6 = (bf16[256,3072]{1,0:T(8,128)(2,1)S(1)}, bf16[256,3072]{1,0:T(8,128)(2,1)}, u32[]{:S(2)}) copy-start(bf16[256,3072]{1,0:T(8,128)(2,1)} %get-tuple-element.106) | copy-start | bytes 4718596
  171.3 4.8 %copy-start.13 = (bf16[256,768]{1,0:T(8,128)(2,1)S(1)}, bf16[256,768]{1,0:T(8,128)(2,1)}, u32[]{:S(2)}) copy-start(bf16[256,768]{1,0:T(8,128)(2,1)} %get-tuple-element.105) | copy-start | bytes 1179652
  176.1 3.6 copy-start.17
  176.1 3.6 copy-start.19
  179.7 1.6 copy-start.4
  179.7 1.6 copy-start.5
  378.9 4.3 %copy-start.8 = (bf16[192,3072]{1,0:T(8,128)(2,1)S(1)}, bf16[192,3072]{1,0:T(8,128)(2,1)}, u32[]{:S(2)}) copy-start(bf16[192,3072]{1,0:T(8,128)(2,1)} %get-tuple-element.122) | copy-start | bytes 3538948
  378.9 4.3 %copy-start.9 = (bf16[192,3072]{1,0:T(8,128)(2,1)S(1)}, bf16[192,3072]{1,0:T(8,128)(2,1)}, u32[]{:S(2)}) copy-start(bf16[192,3072]{1,0:T(8,128)(2,1)} %get-tuple-element.123) | copy-start | bytes 3538948
  383.2 2.5 copy-start.21
  383.2 2.5 copy-start.22
  385.7 1.6 copy-start.11
  385.7 1.9 copy-start.12
  387.6 2.0 copy-start.1
  387.6 2.0 copy-start.16

commit v5 on v4

--- a/solution.py
+++ b/solution.py
@@ -17,6 +17,7 @@
 
 EPSILON = 1e-05
 LAG = 1
+LAG_OWN = 1
 
 
 def norm_forward(values, gain_row, shift_row):
@@ -37,10 +38,18 @@
     )
 
 
-def reduce_kernel(high, count, segments, members, *refs):
-    sources, targets = refs[:members], refs[members : 2 * members]
-    (own, core_in, x_in, y_in, z_in, full, load_sem, core_sem, x_sem, y_sem, z_sem, zg_sem,
-     yg_sem, sent, out_sem) = refs[2 * members :]
+RING = 4
+
+
+def reduce_kernel(high, chunk, segments, shards, layers, *refs):
+    each = 4 * layers
+    lefts, rights, smalls = refs[:each], refs[each : 2 * each], refs[2 * each : 2 * each + layers]
+    refs = refs[2 * each + layers :]
+    members = len(refs) - 19
+    targets = refs[:members]
+    (left, right, ring, total, x_in, y_in, z_in, full, load_sem, ring_sem, core_sem, small_sem,
+     x_sem, y_sem, z_sem, zg_sem, yg_sem, sent) = refs[members:][:18]
+    out_sem = refs[-1]
     dp = lax.axis_index("dp")
     shard = lax.axis_index("fsdp")
     y_at, z_at = lax.rem(dp, 2), lax.div(dp, 2)
@@ -51,9 +60,13 @@
     z_of = [lax.rem(z_at + step, high) for step in range(high)]
     z_from = [lax.rem(z_at + high - step, high) for step in range(high)]
     z_peers = [(z_of[step] * 2 + y_at, shard) for step in range(high)]
-    chunk = own.shape[2]
     half = chunk // 2
     piece = half // high
+    width = full.shape[2]
+    count = full.shape[0]
+    depth = width // shards
+    down = rights[2].shape[1] // width
+    blocks = layers * (8 + down)
 
     barrier = pltpu.get_barrier_semaphore()
     peers = [core_peer, x_peer, y_peer] + z_peers[1:]
@@ -67,37 +80,125 @@
             device_id=peer, device_id_type=MESH,
         )
 
-    def source_of(segment, wanted):
-        ref = sources[segment.member]
-        start = pl.multiple_of(wanted * segment.depth + segment.row, 16)
-        return ref.at[pl.ds(start, segment.rows), pl.ds(segment.column, own.shape[3])]
-
-    def slot_of(buffer, k, j, segment):
-        return buffer.at[k, j, pl.ds(segment.at, segment.rows)]
-
-    def load_arrival(k, j):
-        slot = own.at[k, j]
-        return pltpu.make_async_copy(slot, slot, load_sem.at[k, j])
-
-    def core_arrival(k, j):
-        return remote(core_in.at[k, j], core_in.at[k, j], 0, core_sem.at[k, j], core_peer)
+    loads, at_left, at_right, first_block = [], 0, 0, []
+    for layer in range(layers):
+        for kind in range(4):
+            member = 4 * layer + kind
+            rows = lefts[member].shape[0]
+            pairs = [(lefts[member], left.at[pl.ds(at_left, rows)])]
+            for column in range(0, rights[member].shape[1], width):
+                pairs.append((rights[member].at[:, pl.ds(column, width)], right.at[at_right]))
+                at_right += 1
+            at_left += rows
+            loads.append([
+                pltpu.make_async_copy(source, target, load_sem.at[member, at])
+                for at, (source, target) in enumerate(pairs)
+            ])
+            first_block.append(layer * (8 + down) + (0, 3, 4, 4 + down)[kind])
+    for load in loads:
+        for copy in load:
+            copy.start()
+
+    def gradient(block, wanted):
+        layer, b = lax.div(block, 8 + down), lax.rem(block, 8 + down)
+        deep = b - 4 - down
+        start = layer * (at_left // layers) + jnp.where(
+            b < 3, 0, jnp.where(b < 4, width, jnp.where(deep < 0, 2 * width, 3 * width))
+        )
+        start = start + jnp.where(deep < 0, depth * wanted, down * depth * wanted + depth * deep)
+        column = layer * (at_right // layers) + jnp.minimum(b, 4 + down)
+        return jnp.dot(
+            left[pl.ds(pl.multiple_of(start, 64), depth), :], right[column],
+            preferred_element_type=jnp.float32,
+        )
+
+    def block_rows(block):
+        return pl.ds(pl.multiple_of(block * depth, 64), depth)
+
+    def chunk_rows_of(k):
+        return pl.ds(pl.multiple_of(k * chunk, chunk), chunk)
+
+    def wanted_of(j, side):
+        return (x_at if j == 0 else 1 - x_at) * 2 + side
+
+    def core_send(block, j):
+        slot = lax.rem(block, RING)
+        return pltpu.make_async_remote_copy(
+            src_ref=ring.at[slot, j], dst_ref=total.at[j, block_rows(block)],
+            send_sem=ring_sem.at[slot, j], recv_sem=core_sem.at[block, j],
+            device_id=core_peer, device_id_type=MESH,
+        )
+
+    small_depth = smalls[0].shape[0]
+
+    def small_rows_of(layer):
+        return pl.ds(blocks * depth + layer * small_depth, small_depth)
+
+    def small_send(layer, j):
+        return pltpu.make_async_remote_copy(
+            src_ref=smalls[layer], dst_ref=total.at[j, small_rows_of(layer)],
+            send_sem=small_sem.at[0, layer, j], recv_sem=small_sem.at[1, layer, j],
+            device_id=core_peer, device_id_type=MESH,
+        )
+
+    for layer in range(layers):
+        for j in (1, 0):
+            small_send(layer, j).start()
+
+    def stage_make(block):
+        for member, first in enumerate(first_block):
+
+            @pl.when(block == first)
+            def _(member=member):
+                for copy in loads[member]:
+                    copy.wait()
+
+        for j in (1, 0):
+
+            @pl.when(block >= RING)
+            def _(j=j):
+                core_send(block, j).wait_send()
+
+            ring[lax.rem(block, RING), j] = gradient(block, wanted_of(j, 1 - core)).astype(
+                jnp.bfloat16
+            )
+            core_send(block, j).start()
+
+    def stage_own(block):
+        for j in (1, 0):
+            own = gradient(block, wanted_of(j, core))
+            core_send(block, j).wait_recv()
+            place = total.at[j, block_rows(block)]
+            place[...] = (place[...].astype(jnp.float32) + own).astype(jnp.bfloat16)
+
+    def add_smalls():
+        for layer in range(layers):
+            for j in (1, 0):
+                small_send(layer, j).wait_recv()
+                add_rows(total.at[j, small_rows_of(layer)], smalls[layer])
 
     def x_send(k):
-        return remote(own.at[k, 1], x_in.at[k], 1, x_sem.at[k], x_peer)
+        return remote(total.at[1, chunk_rows_of(k)], x_in.at[k], 1, x_sem.at[k], x_peer)
 
     def y_rows(side):
         return pl.ds(pl.multiple_of(side * half, half), half)
 
+    def y_part(k, side):
+        return total.at[0, pl.ds(pl.multiple_of(k * chunk + side * half, half), half)]
+
     def y_send(k):
-        return remote(own.at[k, 0, y_rows(1 - y_at)], y_in.at[k], 2, y_sem.at[k], y_peer)
+        return remote(y_part(k, 1 - y_at), y_in.at[k], 2, y_sem.at[k], y_peer)
 
     def z_rows(at):
         return pl.ds(pl.multiple_of(y_at * half + at * piece, piece), piece)
 
+    def z_part(k, at):
+        start = k * chunk + y_at * half + at * piece
+        return total.at[0, pl.ds(pl.multiple_of(start, piece), piece)]
+
     def z_send(k, step):
         return remote(
-            own.at[k, 0, z_rows(z_of[step])], z_in.at[k, step - 1], 3,
-            z_sem.at[k, step - 1], z_peers[step],
+            z_part(k, z_of[step]), z_in.at[k, step - 1], 3, z_sem.at[k, step - 1], z_peers[step]
         )
 
     def zg_send(k, step):
@@ -115,44 +216,26 @@
     def store_end(k):
         return pltpu.make_async_copy(full.at[k], full.at[k], out_sem.at[k])
 
-    for segment in segments:
-        k = segment.chunk
-        for j in (1, 0):
-            x_wanted = x_at if j == 0 else 1 - x_at
-            remote(
-                source_of(segment, x_wanted * 2 + 1 - core), slot_of(core_in, k, j, segment),
-                0, core_sem.at[k, j], core_peer,
-            ).start()
-            pltpu.make_async_copy(
-                source_of(segment, x_wanted * 2 + core), slot_of(own, k, j, segment),
-                load_sem.at[k, j],
-            ).start()
-
     def stage_core(k):
-        for j in (1, 0):
-            load_arrival(k, j).wait()
-            core_arrival(k, j).wait_recv()
-            add_rows(own.at[k, j], core_in.at[k, j])
-            if j == 1:
-                x_send(k).start()
+        x_send(k).start()
 
     def stage_x(k):
         x_send(k).wait_recv()
-        add_rows(own.at[k, 0], x_in.at[k])
+        add_rows(total.at[0, chunk_rows_of(k)], x_in.at[k])
         y_send(k).start()
 
     def stage_y(k):
         y_send(k).wait_recv()
-        add_rows(own.at[k, 0, y_rows(y_at)], y_in.at[k])
+        add_rows(y_part(k, y_at), y_in.at[k])
         for step in range(1, high):
             z_send(k, step).start()
 
     def stage_z(k):
-        total = own[k, 0, z_rows(z_at), :].astype(jnp.float32)
+        summed = z_part(k, z_at)[...].astype(jnp.float32)
         for step in range(1, high):
             z_send(k, step).wait_recv()
-            total = total + z_in[k, step - 1].astype(jnp.float32)
-        full[k, z_rows(z_at), :] = total.astype(jnp.bfloat16)
+            summed = summed + z_in[k, step - 1].astype(jnp.float32)
+        full[k, z_rows(z_at), :] = summed.astype(jnp.bfloat16)
         for step in range(1, high):
             zg_send(k, step).start()
 
@@ -168,29 +251,43 @@
             @pl.when(k == segment.chunk)
             def _(segment=segment):
                 target = targets[segment.member].at[
-                    pl.ds(segment.row, segment.rows), pl.ds(segment.column, own.shape[3])
+                    pl.ds(segment.row, segment.rows), pl.ds(segment.column, width)
                 ]
                 pltpu.make_async_copy(
                     full.at[segment.chunk, pl.ds(segment.at, segment.rows)], target,
                     out_sem.at[segment.chunk],
                 ).start()
 
+    def done(block):
+        return jnp.where(
+            block >= blocks, count, lax.div(jnp.maximum(block, 0) * depth, chunk)
+        )
+
     stages = (stage_core, stage_x, stage_y, stage_z, stage_spread, stage_store)
-    lags = (0, LAG, 2 * LAG, 3 * LAG, 4 * LAG, 5 * LAG)
-
-    @pl.loop(0, count + lags[-1])
+
+    @pl.loop(0, blocks + LAG_OWN + 5 * LAG)
     def _(t):
-        for stage, lag in zip(stages, lags):
-            k = t - lag
-
-            @pl.when((k >= 0) & (k < count))
-            def _():
+        pl.when(t < blocks)(lambda: stage_make(t))
+        own_at = t - LAG_OWN
+        pl.when((own_at >= 0) & (own_at < blocks))(lambda: stage_own(own_at))
+        pl.when(own_at == blocks - 1)(add_smalls)
+        for at, stage in enumerate(stages):
+            last = own_at - at * LAG + 1
+
+            @pl.loop(done(last - 1), done(last))
+            def _(k, stage=stage):
                 stage(k)
+
+    for block in range(max(0, blocks - RING), blocks):
+        for j in (1, 0):
+            core_send(block, j).wait_send()
+    for layer in range(layers):
+        for j in (1, 0):
+            small_send(layer, j).wait_send()
 
     def all_sent(source, target, send_at, peer):
         remote(source, target, send_at, x_sem.at[0], peer).wait_send()
 
-    all_sent(own, core_in, 0, core_peer)
     all_sent(x_in, x_in, 1, x_peer)
     all_sent(y_in, y_in, 2, y_peer)
     all_sent(z_in, z_in, 3, z_peers[1])
@@ -204,7 +301,6 @@
 
 class Segment(NamedTuple):
     member: int
-    depth: int
     row: int
     column: int
     rows: int
@@ -212,76 +308,68 @@
     at: int
 
 
-def plan_segments(members, depths, strides, width, chunk):
+def plan_segments(forms, width, chunk):
     segments, place = [], 0
-    for member, array in enumerate(members):
-        depth = depths[member]
-        for column in range(0, array.shape[1], width):
+    for member, (depth, columns) in enumerate(forms):
+        for column in range(0, columns, width):
             row = 0
             while row < depth:
                 rows = min(depth - row, chunk - place % chunk)
                 segments.append(
-                    Segment(
-                        member, strides[member], row, column, rows, place // chunk, place % chunk
-                    )
+                    Segment(member, row, column, rows, place // chunk, place % chunk)
                 )
                 row, place = row + rows, place + rows
     return tuple(segments), place
 
 
-def reduce_gradients(members, smalls, shards, group, width):
+def reduce_gradients(lefts, rights, smalls, shards, group, width):
     high = group // 2
     chunk = chunk_rows(group)
-    depths = [array.shape[0] // shards for array in members]
-    strides = depths + [0] * len(smalls)
-    depths += [array.shape[0] for array in smalls]
-    filled = sum(
-        array.shape[1] // width * depth for array, depth in zip(members + smalls, depths)
-    )
-    rest = -filled % chunk
-    members = members + smalls
-    if rest:
-        members = members + [jnp.zeros((rest, width), jnp.bfloat16)]
-        depths.append(rest)
-        strides.append(0)
-    segments, rows = plan_segments(members, depths, strides, width, chunk)
-    count = rows // chunk
+    layers = len(smalls)
+    forms = [
+        (left.shape[0] // shards, right.shape[1]) for left, right in zip(lefts, rights)
+    ] + [small.shape for small in smalls]
+    segments, used = plan_segments(forms, width, chunk)
+    count = -(-used // chunk)
     piece = chunk // group
+    depth = width // shards
+    blocks = sum(rows * columns for rows, columns in forms[: 4 * layers]) // (depth * width)
+    tokens = rights[0].shape[0]
     buffers = [
-        (count, 2, chunk, width),
-        (count, 2, chunk, width),
+        (sum(left.shape[0] for left in lefts), tokens),
+        (sum(right.shape[1] for right in rights) // width, tokens, width),
+        (RING, 2, depth, width),
+        (2, count * chunk, width),
         (count, chunk, width),
         (count, chunk // 2, width),
         (count, high - 1, piece, width),
         (count, chunk, width),
     ]
-    semaphores = [(count, 2), (count, 2), (count,), (count,), (count, high - 1),
-                  (count, high - 1), (count,), (6,), (count,)]
-    hbm = pl.BlockSpec(memory_space=pltpu.MemorySpace.HBM)
+    semaphores = [(4 * layers, 1 + rights[2].shape[1] // width), (RING, 2), (blocks, 2),
+                  (2, layers, 2), (count,), (count,), (count, high - 1), (count, high - 1),
+                  (count,), (6,), (count,)]
+    vmem, hbm, _ = memory_specs()
     return pl.pallas_call(
-        functools.partial(reduce_kernel, high, count, segments, len(members)),
-        out_shape=[
-            jax.ShapeDtypeStruct((depth, array.shape[1]), jnp.bfloat16)
-            for array, depth in zip(members, depths)
-        ],
-        in_specs=[hbm] * len(members),
-        out_specs=[hbm] * len(members),
+        functools.partial(reduce_kernel, high, chunk, segments, shards, layers),
+        out_shape=[jax.ShapeDtypeStruct(form, jnp.bfloat16) for form in forms],
+        in_specs=[hbm] * (8 * layers) + [vmem] * layers,
+        out_specs=[hbm] * len(forms),
         scratch_shapes=[pltpu.VMEM(shape, jnp.bfloat16) for shape in buffers]
         + [pltpu.SemaphoreType.DMA(shape) for shape in semaphores],
         compiler_params=pltpu.CompilerParams(
             collective_id=1, has_side_effects=True, vmem_limit_bytes=64 * 1024 * 1024 - 65536
         ),
-    )(*members)
+    )(*lefts, *rights, *smalls)
 
 
 def chunk_rows(group):
     return 16 * CHUNK_TILES * group
 
 
-def sum_gradients(members, smalls, shards, group):
+def sum_gradients(lefts, rights, smalls, shards, group):
     width = smalls[0].shape[1]
     layers = len(smalls)
-    reduced = reduce_gradients(members, smalls, shards, group, width)
+    reduced = reduce_gradients(lefts, rights, smalls, shards, group, width)
     spans = [
         jnp.stack([reduced[4 * layer + member] for layer in range(layers)]).astype(jnp.float32)
         for member in range(4)
@@ -302,7 +390,7 @@
     total = len(items)
     ready = 1 + 4
     sources, forward_in = refs[:5], refs[5:9]
-    outs = refs[9 : 9 + total - 1 + 3 + 13]
+    outs = refs[9 : 9 + total - 1 + 3 + 14]
     vectors, up_shifts, table = outs[total - 1 : total + 2]
     forward_out = outs[total + 2 :]
     rest = refs[9 + len(outs) :]
@@ -587,8 +675,9 @@
 
 def forward_core(
     layer, service, x_ref, buckets, live, lengths, all_vectors, up_shifts, table, w_in_hbm,
-    w_out_hbm, w_up_hbm, w_down_hbm, out_ref, q_ref, k_ref, v_ref, o_ref, p_ref, low_ref, n1_ref, r1_ref, slope_ref,
-    g_ref, n2_ref, r2_ref, w_in, w_out, w_up, w_down, allowed, y1, total, sem,
+    w_out_hbm, w_up_hbm, w_down_hbm, out_ref, q_ref, k_ref, v_ref, o_turned, p_ref, low_turned, n1_ref, r1_ref,
+    slope_ref, g_turned, n2_ref, r2_ref, x_turned, w_in, w_out, w_up, w_down, allowed, y1, total,
+    o_ref, low_ref, sem,
 ):
     loads = [
         pltpu.make_async_copy(source, target, sem.at[at])
@@ -666,6 +755,8 @@
 
         service(1 + w)
 
+    x_turned[...] = jnp.transpose(inputs)
+    o_turned[...] = jnp.transpose(o_ref[...])
     loads[1].wait()
     attended = (
         jnp.dot(o_ref[...], w_out[...], preferred_element_type=jnp.float32) + vectors[2:3, :]
@@ -676,7 +767,9 @@
     n1_ref[...] = normed
     r1_ref[...] = jnp.broadcast_to(inverse, r1_ref.shape)
     y1[...] = first_norm
-    low_ref[...] = first_norm.astype(jnp.bfloat16)
+    low = first_norm.astype(jnp.bfloat16)
+    low_ref[...] = low
+    low_turned[...] = jnp.transpose(low)
     total[...] = jnp.zeros_like(total)
     service(1 + windows)
     loads[2].wait()
@@ -694,7 +787,7 @@
             0.5 / math.pi
         ) ** 0.5
         active = (hidden * mass).astype(jnp.bfloat16)
-        g_ref[:, lanes] = active
+        g_turned[lanes, :] = jnp.transpose(active)
         total[...] += jnp.dot(active, w_down[lanes, :], preferred_element_type=jnp.float32)
 
     result, normed, inverse = norm_forward(
@@ -710,19 +803,21 @@
     narrow = jax.ShapeDtypeStruct((rows, width), low)
     wide = jax.ShapeDtypeStruct((rows, width), full)
     column = jax.ShapeDtypeStruct((rows, WIN), full)
+    turned = jax.ShapeDtypeStruct((width, rows), low)
     outs = [
-        narrow, narrow, narrow, narrow, narrow,
+        narrow, narrow, narrow, narrow, turned,
         jax.ShapeDtypeStruct((rows // WIN * H, WIN, WIN), full),
-        narrow, wide, column,
+        turned, wide, column,
         jax.ShapeDtypeStruct((rows, hidden), full),
-        jax.ShapeDtypeStruct((rows, hidden), low),
-        wide, column,
+        jax.ShapeDtypeStruct((hidden, rows), low),
+        wide, column, turned,
     ]
     scratch = [
         pltpu.VMEM((width, 3 * width), low), pltpu.VMEM((width, width), low),
         pltpu.VMEM((width, hidden), low), pltpu.VMEM((hidden, width), low),
         pltpu.VMEM((rows // WIN, WIN, WIN), jnp.int32),
         pltpu.VMEM((rows, width), full), pltpu.VMEM((rows, width), full),
+        pltpu.VMEM((rows, width), low), pltpu.VMEM((rows, width), low),
         pltpu.SemaphoreType.DMA((4,)),
     ]
     return outs, scratch
@@ -888,7 +983,7 @@
     low, full = jnp.bfloat16, jnp.float32
     narrow = jax.ShapeDtypeStruct((rows, width), low)
     vmem, hbm, _ = memory_specs()
-    q, k, v, _, p, _, n1, r1, slope, _, n2, r2 = kept
+    q, k, v, _, p, _, n1, r1, slope, _, n2, r2, _ = kept
     return pl.pallas_call(
         functools.partial(backward_kernel, layer),
         out_shape=[
@@ -935,30 +1030,24 @@
         shards, tokens, layout_buckets, live, doc_lengths,
     )
     current, *kept = first
-    layer_inputs, kept_list, outputs = [tokens], [kept], [current]
+    kept_list, outputs = [kept], [current]
     for layer in range(1, len(weights_list)):
-        layer_inputs.append(current)
         current, *kept = forward_layer(
             layer, current, weights_list[layer], shared, layout_buckets, live, doc_lengths
         )
         kept_list.append(kept)
         outputs.append(current)
     incoming = out_grad.astype(jnp.float32) * mlm_mask.astype(jnp.float32)[:, None]
-    members, smalls = [], []
+    lefts, rights, smalls = [], [], []
     for layer in reversed(range(len(weights_list))):
         kept = kept_list[layer]
         incoming, df, du, da, dqkv, small = backward_layer(
             layer, incoming, weights_list[layer], shared[0], kept, layout_buckets
         )
-        pairs = ((layer_inputs[layer], dqkv), (kept[3], da), (kept[5], du), (kept[9], df))
-        members = [
-            jnp.einsum("nd,ne->de", left, right, preferred_element_type=jnp.float32).astype(
-                jnp.bfloat16
-            )
-            for left, right in pairs
-        ] + members
+        lefts = [kept[12], kept[3], kept[5], kept[9]] + lefts
+        rights = [dqkv, da, du, df] + rights
         smalls = [small] + smalls
-    summed = sum_gradients(members, smalls, shards, lax.axis_size("dp"))
+    summed = sum_gradients(lefts, rights, smalls, shards, lax.axis_size("dp"))
     return (jnp.stack(outputs), incoming) + summed
 
 

time: 391 us -> 372 us (0.951)
  matrix products: 25.7 us -> 0 us
  Pallas kernels: 344 us -> 349 us
    dot_general x8 -> x0, matrix products: 25.7 us -> none  [local(): jnp.einsum('nd,ne->de', left, right, preferred_element_type=jnp.float32)]
    pallas_call x1, Pallas kernels: 191 us -> 195 us  [reduce_gradients(): pl.pallas_call(functools.partial(reduce_kernel, high, chunk, segments, sh...]
where the time goes in v5:
time: 372 us; the launch traced here: 370 us
  Pallas kernels  349 us (94%)
  other arithmetic  14.2 us (4%)
  local copies, waits for them, and re-layouts  5.89 us (2%)
    pallas_call x1, Pallas kernels, reduce_gradients(): pl.pallas_call(functools.partial(reduce_kernel, high, chunk, segments, sh...  195 us
    pallas_call x1, Pallas kernels, open_layers(): pl.pallas_call(functools.partial(opening_kernel, tuple(items)), out_shape...  84.5 us
    pallas_call x2, Pallas kernels, backward_layer(): pl.pallas_call(functools.partial(backward_kernel, layer), out_shape=[jax....  49.5 us
    pallas_call x1, Pallas kernels, forward_layer(): pl.pallas_call(functools.partial(forward_kernel, layer), out_shape=outs,...  20.4 us
    convert_element_type x4, other arithmetic, sum_gradients(): jnp.stack([reduced[4 * layer + member] for layer in range(layers)])  9.87 us

profile of v5, /device:TPU:0, one launch (start us, length us, event | category | flops | bytes accessed | tf_op | source)
XLA Modules:
  0.0 370.3 jit_solution(1265471692154171544)
XLA Ops:
  0.6 0.8 copy.36
  1.5 0.7 copy.29
  2.2 0.7 pad_maximum_fusion.1
  2.9 0.7 reshape.37
  3.6 0.6 fusion.4.refs_4_
  4.2 84.5 %shard_map.213 = (bf16[768,2304]{1,0:T(8,128)(2,1)}, bf16[768,768]{1,0:T(8,128)(2,1)}, bf16[768,3072]{1,0:T(8,128)(2,1)}, bf16[3072,768]{1,0:T(8,128)(2,1)}, bf1...) custom-call(bf16[2,192,2304]{2,1,0:T(8,128)(2,1)} %refs_0_.1, ...), custom_call_target="tpu_custom_call" | custom-call | tf_op jit(solution)/shard_map/pallas_call | solution.py:625
  88.8 20.4 %shard_map.214 = (bf16[256,768]{1,0:T(8,128)(2,1)}, bf16[256,768]{1,0:T(8,128)(2,1)}, bf16[256,768]{1,0:T(8,128)(2,1)}, bf16[256,768]{1,0:T(8,128)(2,1)}, bf16[7...) custom-call(bf16[256,768]{1,0:T(8,128)(2,1)} %get-tuple-element.71.r, ...), custom_call_target="tpu_custom_call" | custom-call | tf_op jit(solution)/shard_map/pallas_call | solution.py:839
  109.2 1.0 convert_multiply_fusion.dz_ref
  110.2 24.8 %shard_map.215 = (f32[256,768]{1,0:T(8,128)}, bf16[256,768]{1,0:T(8,128)(2,1)}, bf16[256,3072]{1,0:T(8,128)(2,1)}, bf16[256,768]{1,0:T(8,128)(2,1)}, bf16[256,2304]{1,0:T(8,128)(2,1)}, /*index=5*/bf16[64,768]{1,0:T(8,128)(2,1)}) custom-call(f32[256,768]{1,0:T(8,128)} %convert_multiply_fusion.dz_ref, f32[256,768]{1,0:T(8,128)} %get-tuple-element.80.n2_ref, ...), custom_call_target="tpu_custom_call" | custom-call | tf_op jit(solution)/shard_map/pallas_call | solution.py:987
  135.0 24.6 %shard_map.216 = (f32[256,768]{1,0:T(8,128)}, bf16[256,768]{1,0:T(8,128)(2,1)}, bf16[256,3072]{1,0:T(8,128)(2,1)}, bf16[256,768]{1,0:T(8,128)(2,1)}, bf16[256,2304]{1,0:T(8,128)(2,1)}, /*index=5*/bf16[64,768]{1,0:T(8,128)(2,1)}) custom-call(f32[256,768]{1,0:T(8,128)} %get-tuple-element.89.dz_ref, f32[256,768]{1,0:T(8,128)} %get-tuple-element.90.n2_ref, ...), custom_call_target="tpu_custom_call" | custom-call | tf_op jit(solution)/shard_map/pallas_call | solution.py:987
  159.7 195.1 %shard_map.217 = (bf16[192,2304]{1,0:T(8,128)(2,1)}, bf16[192,768]{1,0:T(8,128)(2,1)}, bf16[192,3072]{1,0:T(8,128)(2,1)}, bf16[768,768]{1,0:T(8,128)(2,1)}, bf16...) custom-call(bf16[768,256]{1,0:T(8,128)(2,1)} %get-tuple-element.104., ...), custom_call_target="tpu_custom_call" | custom-call | tf_op jit(solution)/shard_map/pallas_call | solution.py:352
  354.8 1.0 maximum_convert_fusion.4
  355.8 0.1 reshape.40
  356.0 0.7 copy.34
  356.8 0.6 copy.33
  357.4 0.7 constant_dynamic-slice_fusion.2
  358.1 0.6 copy.40
  358.7 4.3 %maximum_convert_fusion.1 = f32[2,768,768]{2,1,0:T(8,128)} fusion(bf16[1,768,768]{2,1,0:T(8,128)(2,1)} %bitcast.29, bf16[1,768,768]{2,1,0:T(8,128)(2,1)} %bitcast.28), kind=kLoop, calls=%fused_computation.1 | loop fusion | flops 2359296 | bytes 7077888 | tf_op jit(solution)/shard_map/convert_element_type | solution.py:374
  363.0 2.5 maximum_convert_fusion
  365.5 1.1 maximum_convert_fusion.3
  366.6 0.5 copy-done.3
  367.1 0.3 copy-done.4
  367.4 2.0 maximum_convert_fusion.2
  369.4 0.9 pad_maximum_fusion
  (27 shorter events, 0.2 us)
Async XLA Ops:
  88.7 20.4 %copy-start.9 = (s32[256]{0:T(256)S(1)}, s32[256]{0:T(256)}, u32[]{:S(2)}) copy-start(s32[256]{0:T(256)} %param.16) | copy-start | bytes 3076
  88.7 20.4 %copy-start.5 = (bf16[256,768]{1,0:T(8,128)(2,1)S(1)}, bf16[256,768]{1,0:T(8,128)(2,1)}, u32[]{:S(2)}) copy-start(bf16[256,768]{1,0:T(8,128)(2,1)} %param.15) | copy-start | bytes 1179652
  358.7 4.3 %copy-start.1 = (bf16[192,3072]{1,0:T(8,128)(2,1)S(1)}, bf16[192,3072]{1,0:T(8,128)(2,1)}, u32[]{:S(2)}) copy-start(bf16[192,3072]{1,0:T(8,128)(2,1)} %get-tuple-element.126) | copy-start | bytes 3538948
  358.7 4.3 %copy-start.2 = (bf16[192,3072]{1,0:T(8,128)(2,1)S(1)}, bf16[192,3072]{1,0:T(8,128)(2,1)}, u32[]{:S(2)}) copy-start(bf16[192,3072]{1,0:T(8,128)(2,1)} %get-tuple-element.127) | copy-start | bytes 3538948
  363.0 2.5 copy-start.7
  363.0 2.5 copy-start.8
  365.5 1.6 copy-start.3
  365.5 1.9 copy-start.4
  367.4 2.0 copy-start
  367.4 2.0 copy-start.6

commit v6 on v5

--- a/solution.py
+++ b/solution.py
@@ -17,7 +17,7 @@
 
 EPSILON = 1e-05
 LAG = 1
-LAG_OWN = 1
+LAG_OWN = 2
 
 
 def norm_forward(values, gain_row, shift_row):
@@ -46,7 +46,9 @@
     lefts, rights, smalls = refs[:each], refs[each : 2 * each], refs[2 * each : 2 * each + layers]
     refs = refs[2 * each + layers :]
     members = len(refs) - 19
-    targets = refs[:members]
+    targets = [
+        refs[kind].at[layer] for layer in range(layers) for kind in range(4)
+    ] + [refs[4].at[layer] for layer in range(layers)]
     (left, right, ring, total, x_in, y_in, z_in, full, load_sem, ring_sem, core_sem, small_sem,
      x_sem, y_sem, z_sem, zg_sem, yg_sem, sent) = refs[members:][:18]
     out_sem = refs[-1]
@@ -351,9 +353,12 @@
     vmem, hbm, _ = memory_specs()
     return pl.pallas_call(
         functools.partial(reduce_kernel, high, chunk, segments, shards, layers),
-        out_shape=[jax.ShapeDtypeStruct(form, jnp.bfloat16) for form in forms],
+        out_shape=[
+            jax.ShapeDtypeStruct((layers,) + tuple(form), jnp.bfloat16)
+            for form in forms[:4] + forms[-1:]
+        ],
         in_specs=[hbm] * (8 * layers) + [vmem] * layers,
-        out_specs=[hbm] * len(forms),
+        out_specs=[hbm] * 5,
         scratch_shapes=[pltpu.VMEM(shape, jnp.bfloat16) for shape in buffers]
         + [pltpu.SemaphoreType.DMA(shape) for shape in semaphores],
         compiler_params=pltpu.CompilerParams(
@@ -366,15 +371,34 @@
     return 16 * CHUNK_TILES * group
 
 
+def widen_kernel(*refs):
+    total = len(refs) // 2
+    for source, target in zip(refs[:total], refs[total:]):
+        target[...] = source[...].astype(jnp.float32)
+
+
+def widen(arrays):
+    steps = 4
+    specs = [
+        pl.BlockSpec((1, array.shape[1] // steps, array.shape[2]), lambda i, j: (i, j, 0))
+        for array in arrays
+    ]
+    return pl.pallas_call(
+        widen_kernel,
+        grid=(arrays[0].shape[0], steps),
+        out_shape=[jax.ShapeDtypeStruct(array.shape, jnp.float32) for array in arrays],
+        in_specs=specs,
+        out_specs=specs,
+        compiler_params=pltpu.CompilerParams(vmem_limit_bytes=32 * 1024 * 1024),
+    )(*arrays)
+
+
 def sum_gradients(lefts, rights, smalls, shards, group):
     width = smalls[0].shape[1]
     layers = len(smalls)
     reduced = reduce_gradients(lefts, rights, smalls, shards, group, width)
-    spans = [
-        jnp.stack([reduced[4 * layer + member] for layer in range(layers)]).astype(jnp.float32)
-        for member in range(4)
-    ]
-    small = jnp.stack(reduced[4 * layers : 5 * layers]).astype(jnp.float32)
+    spans = widen(reduced[:4])
+    small = reduced[4].astype(jnp.float32)
     depth = width // shards
     shard = lax.axis_index("fsdp")
     rows = lax.dynamic_slice_in_dim(small[:, :8], shard * depth, depth, axis=2)
@@ -795,7 +819,11 @@
     )
     n2_ref[...] = normed
     r2_ref[...] = jnp.broadcast_to(inverse, r2_ref.shape)
-    out_ref[...] = result.astype(jnp.bfloat16)
+    if len(out_ref.shape) == 3:
+        out_ref[0] = inputs
+        out_ref[1] = result.astype(jnp.bfloat16)
+    else:
+        out_ref[...] = result.astype(jnp.bfloat16)
 
 
 def forward_forms(rows, width, hidden):
@@ -835,6 +863,7 @@
 def forward_layer(layer, inputs, weights, shared, buckets, live, lengths):
     rows, width = inputs.shape
     outs, scratch = forward_forms(rows, width, weights[2].shape[1])
+    outs[0] = jax.ShapeDtypeStruct((layer + 1, rows, width), jnp.bfloat16)
     vmem, hbm, smem = memory_specs()
     return pl.pallas_call(
         functools.partial(forward_kernel, layer),
@@ -1030,13 +1059,10 @@
         shards, tokens, layout_buckets, live, doc_lengths,
     )
     current, *kept = first
-    kept_list, outputs = [kept], [current]
-    for layer in range(1, len(weights_list)):
-        current, *kept = forward_layer(
-            layer, current, weights_list[layer], shared, layout_buckets, live, doc_lengths
-        )
-        kept_list.append(kept)
-        outputs.append(current)
+    outputs, *kept_next = forward_layer(
+        1, current, weights_list[1], shared, layout_buckets, live, doc_lengths
+    )
+    kept_list = [kept, kept_next]
     incoming = out_grad.astype(jnp.float32) * mlm_mask.astype(jnp.float32)[:, None]
     lefts, rights, smalls = [], [], []
     for layer in reversed(range(len(weights_list))):
@@ -1048,7 +1074,7 @@
         rights = [dqkv, da, du, df] + rights
         smalls = [small] + smalls
     summed = sum_gradients(lefts, rights, smalls, shards, lax.axis_size("dp"))
-    return (jnp.stack(outputs), incoming) + summed
+    return (outputs, incoming) + summed
 
 
 def solution(mesh):

time: 372 us -> 370 us (level)
  other arithmetic: 14.2 us -> 2.41 us
  Pallas kernels: 349 us -> 355 us
  local copies, waits for them, and re-layouts: 5.89 us -> 11 us
    convert_element_type x5 -> x1, other arithmetic: 10.8 us -> 0.03 us  [sum_gradients(): small = reduced[4].astype(jnp.float32)]
    pallas_call x0 -> x1, Pallas kernels: none -> 5.59 us  [widen(): pl.pallas_call(widen_kernel, grid=(arrays[0].shape[0], steps), out_shape=...]
    unnamed x25 -> x19, local copies, waits for them, and re-layouts: 4.22 us -> 9.31 us
where the time goes in v6:
time: 370 us
  Pallas kernels  355 us (96%)
  local copies, waits for them, and re-layouts  11 us (3%)
    pallas_call x1, Pallas kernels, reduce_gradients(): pl.pallas_call(functools.partial(reduce_kernel, high, chunk, segments, sh...  195 us
    pallas_call x1, Pallas kernels, open_layers(): pl.pallas_call(functools.partial(opening_kernel, tuple(items)), out_shape...  84.5 us
    pallas_call x2, Pallas kernels, backward_layer(): pl.pallas_call(functools.partial(backward_kernel, layer), out_shape=[jax....  49.5 us
    pallas_call x1, Pallas kernels, forward_layer(): pl.pallas_call(functools.partial(forward_kernel, layer), out_shape=outs,...  20.5 us
    unnamed x19, local copies, waits for them, and re-layouts  9.31 us

profile of v6, /device:TPU:0, one launch (start us, length us, event | category | flops | bytes accessed | tf_op | source)
XLA Modules:
  0.0 369.6 jit_solution(1429540055559696733)
XLA Ops:
  0.6 0.8 copy.36
  1.5 0.7 copy.29
  2.2 0.7 pad_maximum_fusion
  2.9 0.7 reshape.37
  3.6 0.6 fusion.4.refs_4_
  4.2 84.5 %shard_map.213 = (bf16[768,2304]{1,0:T(8,128)(2,1)}, bf16[768,768]{1,0:T(8,128)(2,1)}, bf16[768,3072]{1,0:T(8,128)(2,1)}, bf16[3072,768]{1,0:T(8,128)(2,1)}, bf1...) custom-call(bf16[2,192,2304]{2,1,0:T(8,128)(2,1)} %refs_0_.1, ...), custom_call_target="tpu_custom_call" | custom-call | tf_op jit(solution)/shard_map/pallas_call | solution.py:649
  88.7 0.0 copy-start.6
  88.7 20.5 %shard_map.214 = (bf16[2,256,768]{2,1,0:T(8,128)(2,1)}, bf16[256,768]{1,0:T(8,128)(2,1)}, bf16[256,768]{1,0:T(8,128)(2,1)}, bf16[256,768]{1,0:T(8,128)(2,1)}, bf...) custom-call(bf16[256,768]{1,0:T(8,128)(2,1)} %get-tuple-element.70.r, ...), custom_call_target="tpu_custom_call" | custom-call | tf_op jit(solution)/shard_map/pallas_call | solution.py:868
  109.3 1.0 convert_multiply_fusion.dz_ref
  110.3 24.8 %shard_map.215 = (f32[256,768]{1,0:T(8,128)}, bf16[256,768]{1,0:T(8,128)(2,1)}, bf16[256,3072]{1,0:T(8,128)(2,1)}, bf16[256,768]{1,0:T(8,128)(2,1)}, bf16[256,2304]{1,0:T(8,128)(2,1)}, /*index=5*/bf16[64,768]{1,0:T(8,128)(2,1)}) custom-call(f32[256,768]{1,0:T(8,128)} %convert_multiply_fusion.dz_ref, f32[256,768]{1,0:T(8,128)} %get-tuple-element.79.n2_ref, ...), custom_call_target="tpu_custom_call" | custom-call | tf_op jit(solution)/shard_map/pallas_call | solution.py:1016
  135.1 24.7 %shard_map.216 = (f32[256,768]{1,0:T(8,128)}, bf16[256,768]{1,0:T(8,128)(2,1)}, bf16[256,3072]{1,0:T(8,128)(2,1)}, bf16[256,768]{1,0:T(8,128)(2,1)}, bf16[256,2304]{1,0:T(8,128)(2,1)}, /*index=5*/bf16[64,768]{1,0:T(8,128)(2,1)}) custom-call(f32[256,768]{1,0:T(8,128)} %get-tuple-element.88.dz_ref, f32[256,768]{1,0:T(8,128)} %get-tuple-element.89.n2_ref, ...), custom_call_target="tpu_custom_call" | custom-call | tf_op jit(solution)/shard_map/pallas_call | solution.py:1016
  159.8 195.4 %shard_map.217 = (bf16[2,192,2304]{2,1,0:T(8,128)(2,1)}, bf16[2,192,768]{2,1,0:T(8,128)(2,1)}, bf16[2,192,3072]{2,1,0:T(8,128)(2,1)}, bf16[2,768,768]{2,1,0:T(8,128)(2,1)}, bf16[2,64,768]{2,1,0:T(8,128)(2,1)}) custom-call(bf16[768,256]{1,0:T(8,128)(2,1)} %get-tuple-element.103.refs_0_, bf16[768,256]{1,0:T(8,128)(2,1)} %get-tuple-element.104.refs_1_, ...), custom_call_target="tpu_custom_call" | custom-call | tf_op jit(solution)/shard_map/pallas_call | solution.py:354
  355.2 1.7 copy-done
  356.8 1.7 copy-done.1
  358.5 1.5 copy-done.2
  360.0 1.1 copy-done.3
  361.0 5.6 %shard_map.218 = (f32[2,192,2304]{2,1,0:T(8,128)}, f32[2,192,768]{2,1,0:T(8,128)}, f32[2,192,3072]{2,1,0:T(8,128)}, f32[2,768,768]{2,1,0:T(8,128)}) custom-call(bf16[2,192,2304]{2,1,0:T(8,128)(2,1)S(1)} %copy-done.2, bf16[2,192,768]{2,1,0:T(8,128)(2,1)S(1)} %copy-done.3, bf16[2,192,3072]{2,1,0:T(8,128)(2,1)S(1)} %copy-done, bf16[2,768,768]{2,1,0:T(8,128)(2,1)S(1)} %copy-done.1), custom_call_target="tpu_custom_call" | custom-call | tf_op jit(solution)/shard_map/pallas_call | solution.py:386
  366.7 0.6 copy.40
  367.3 0.1 reshape.40
  367.4 0.1 dynamic-slice_bitcast_fusion
  367.5 0.7 copy.34
  368.2 0.1 constant_dynamic-slice_fusion
  368.3 0.6 copy.33
  368.9 0.7 constant_dynamic-slice_fusion.2
  (17 shorter events, 0.1 us)
Async XLA Ops:
  88.7 20.5 %copy-start.6 = (s32[256]{0:T(256)S(1)}, s32[256]{0:T(256)}, u32[]{:S(2)}) copy-start(s32[256]{0:T(256)} %param.16) | copy-start | bytes 3076
  88.7 20.5 %copy-start.4 = (bf16[256,768]{1,0:T(8,128)(2,1)S(1)}, bf16[256,768]{1,0:T(8,128)(2,1)}, u32[]{:S(2)}) copy-start(bf16[256,768]{1,0:T(8,128)(2,1)} %param.15) | copy-start | bytes 1179652
  355.1 1.7 copy-start
  356.8 1.7 copy-start.1
  358.5 1.5 copy-start.2
  360.0 1.1 copy-start.3
  361.0 5.6 %copy-start.5 = (bf16[2,64,768]{2,1,0:T(8,128)(2,1)S(1)}, bf16[2,64,768]{2,1,0:T(8,128)(2,1)}, u32[]{:S(2)}) copy-start(bf16[2,64,768]{2,1,0:T(8,128)(2,1)} %get-tuple-element.129) | copy-start | bytes 589828

commit v7 on v6

--- a/solution.py
+++ b/solution.py
@@ -44,14 +44,14 @@
 def reduce_kernel(high, chunk, segments, shards, layers, *refs):
     each = 4 * layers
     lefts, rights, smalls = refs[:each], refs[each : 2 * each], refs[2 * each : 2 * each + layers]
-    refs = refs[2 * each + layers :]
-    members = len(refs) - 19
+    spreads, buckets = refs[2 * each + layers : 2 * each + 2 * layers], refs[2 * each + 2 * layers]
+    refs = refs[2 * each + 2 * layers + 1 :]
+    members = len(refs) - 21
     targets = [
         refs[kind].at[layer] for layer in range(layers) for kind in range(4)
     ] + [refs[4].at[layer] for layer in range(layers)]
-    (left, right, ring, total, x_in, y_in, z_in, full, load_sem, ring_sem, core_sem, small_sem,
-     x_sem, y_sem, z_sem, zg_sem, yg_sem, sent) = refs[members:][:18]
-    out_sem = refs[-1]
+    (counts, small_all, left, right, ring, total, x_in, y_in, z_in, full, load_sem, ring_sem,
+     core_sem, small_sem, x_sem, y_sem, z_sem, zg_sem, yg_sem, sent, out_sem) = refs[members:]
     dp = lax.axis_index("dp")
     shard = lax.axis_index("fsdp")
     y_at, z_at = lax.rem(dp, 2), lax.div(dp, 2)
@@ -138,14 +138,48 @@
 
     def small_send(layer, j):
         return pltpu.make_async_remote_copy(
-            src_ref=smalls[layer], dst_ref=total.at[j, small_rows_of(layer)],
+            src_ref=small_all.at[layer], dst_ref=total.at[j, small_rows_of(layer)],
             send_sem=small_sem.at[0, layer, j], recv_sem=small_sem.at[1, layer, j],
             device_id=core_peer, device_id_type=MESH,
         )
 
-    for layer in range(layers):
-        for j in (1, 0):
-            small_send(layer, j).start()
+    bucket = lax.broadcasted_iota(jnp.int32, (NB, WIN), 0)
+    lane = lax.broadcasted_iota(jnp.int32, (1, WIN), 1)
+    together = 8
+    counting = WIN // together
+    counts[...] = jnp.zeros_like(counts)
+
+    def count_group(w, at):
+        hits, terms = [], [[] for _ in range(layers)]
+        for step in range(together):
+            i = at * together + step
+            indices = (
+                linear_bucket(lane - i),
+                buckets[0, pl.ds(w * WIN + i, 1), :],
+                buckets[1, pl.ds(w * WIN + i, 1), :],
+            )
+            found = [(index == bucket).astype(jnp.float32) for index in indices]
+            found.append(jnp.zeros((WIN - 3 * NB, WIN), jnp.float32))
+            hits.append(jnp.concatenate(found, axis=0).astype(jnp.bfloat16))
+            for layer in range(layers):
+                terms[layer].append(spreads[layer][w, pl.ds(pl.multiple_of(i * 16, 16), 16), :])
+        hits = jnp.concatenate(hits, axis=1)
+        for layer in range(layers):
+            counts[layer] += lax.dot_general(
+                jnp.concatenate(terms[layer], axis=1), hits, (((1,), (1,)), ((), ())),
+                preferred_element_type=jnp.float32,
+            )
+
+    def count_step(at):
+        for w in range(spreads[0].shape[0]):
+            count_group(w, at)
+
+    def finish_smalls():
+        for layer in range(layers):
+            small_all[layer] = smalls[layer][...]
+            small_all[layer, 16:32, 0:WIN] = counts[layer].astype(jnp.bfloat16)
+            for j in (1, 0):
+                small_send(layer, j).start()
 
     def stage_make(block):
         for member, first in enumerate(first_block):
@@ -177,7 +211,7 @@
         for layer in range(layers):
             for j in (1, 0):
                 small_send(layer, j).wait_recv()
-                add_rows(total.at[j, small_rows_of(layer)], smalls[layer])
+                add_rows(total.at[j, small_rows_of(layer)], small_all.at[layer])
 
     def x_send(k):
         return remote(total.at[1, chunk_rows_of(k)], x_in.at[k], 1, x_sem.at[k], x_peer)
@@ -272,6 +306,8 @@
         pl.when(t < blocks)(lambda: stage_make(t))
         own_at = t - LAG_OWN
         pl.when((own_at >= 0) & (own_at < blocks))(lambda: stage_own(own_at))
+        pl.when((t >= 1) & (t <= counting))(lambda: count_step(t - 1))
+        pl.when(t == counting + 1)(finish_smalls)
         pl.when(own_at == blocks - 1)(add_smalls)
         for at, stage in enumerate(stages):
             last = own_at - at * LAG + 1
@@ -324,7 +360,7 @@
     return tuple(segments), place
 
 
-def reduce_gradients(lefts, rights, smalls, shards, group, width):
+def reduce_gradients(lefts, rights, smalls, spreads, buckets, shards, group, width):
     high = group // 2
     chunk = chunk_rows(group)
     layers = len(smalls)
@@ -357,14 +393,18 @@
             jax.ShapeDtypeStruct((layers,) + tuple(form), jnp.bfloat16)
             for form in forms[:4] + forms[-1:]
         ],
-        in_specs=[hbm] * (8 * layers) + [vmem] * layers,
+        in_specs=[hbm] * (8 * layers) + [vmem] * (2 * layers + 1),
         out_specs=[hbm] * 5,
-        scratch_shapes=[pltpu.VMEM(shape, jnp.bfloat16) for shape in buffers]
+        scratch_shapes=[
+            pltpu.VMEM((layers, 16, WIN), jnp.float32),
+            pltpu.VMEM((layers,) + smalls[0].shape, jnp.bfloat16),
+        ]
+        + [pltpu.VMEM(shape, jnp.bfloat16) for shape in buffers]
         + [pltpu.SemaphoreType.DMA(shape) for shape in semaphores],
         compiler_params=pltpu.CompilerParams(
             collective_id=1, has_side_effects=True, vmem_limit_bytes=64 * 1024 * 1024 - 65536
         ),
-    )(*lefts, *rights, *smalls)
+    )(*lefts, *rights, *smalls, *spreads, buckets)
 
 
 def chunk_rows(group):
@@ -389,14 +429,16 @@
         out_shape=[jax.ShapeDtypeStruct(array.shape, jnp.float32) for array in arrays],
         in_specs=specs,
         out_specs=specs,
-        compiler_params=pltpu.CompilerParams(vmem_limit_bytes=32 * 1024 * 1024),
+        compiler_params=pltpu.CompilerParams(vmem_limit_bytes=64 * 1024 * 1024 - 65536),
     )(*arrays)
 
 
-def sum_gradients(lefts, rights, smalls, shards, group):
+def sum_gradients(lefts, rights, smalls, spreads, buckets, shards, group):
     width = smalls[0].shape[1]
     layers = len(smalls)
-    reduced = reduce_gradients(lefts, rights, smalls, shards, group, width)
+    reduced = reduce_gradients(
+        lefts, rights, smalls, spreads, buckets, shards, group, width
+    )
     spans = widen(reduced[:4])
     small = reduced[4].astype(jnp.float32)
     depth = width // shards
@@ -876,9 +918,9 @@
 
 
 def backward_kernel(
-    layer, dz_ref, n2_ref, r2_ref, slope_ref, n1_ref, r1_ref, p_ref, q_ref, k_ref, v_ref, buckets,
+    layer, dz_ref, n2_ref, r2_ref, slope_ref, n1_ref, r1_ref, p_ref, q_ref, k_ref, v_ref,
     all_vectors, w_down_hbm, w_up_hbm, w_out_hbm, w_in_hbm, dx_ref, df_ref, du_ref, da_ref, dqkv_ref,
-    small_ref, w_down, w_up, w_out, w_in, small, grad, mixed, spread, sem,
+    small_ref, spread_ref, w_down, w_up, w_out, w_in, small, grad, mixed, spread, sem,
 ):
     loads = [
         pltpu.make_async_copy(source, target, sem.at[at])
@@ -965,9 +1007,6 @@
             jnp.bfloat16
         )
 
-    bucket = lax.broadcasted_iota(jnp.int32, (NB, WIN), 0)
-    column = lax.broadcasted_iota(jnp.int32, (1, WIN), 1)
-    group = 8
     for w in range(windows):
 
         @pl.loop(0, H // 4)
@@ -975,28 +1014,7 @@
             attend(w, quad * 2)
             attend(w, quad * 2 + 1)
 
-        def count_group(at, w=w):
-            hits, terms = [], []
-            for step in range(group):
-                i = at * group + step
-                indices = (
-                    linear_bucket(column - i),
-                    buckets[0, pl.ds(w * WIN + i, 1), :],
-                    buckets[1, pl.ds(w * WIN + i, 1), :],
-                )
-                hits.append(
-                    jnp.concatenate(
-                        [(index == bucket).astype(jnp.float32) for index in indices], axis=0
-                    ).astype(jnp.bfloat16)
-                )
-                terms.append(
-                    spread[pl.ds(pl.multiple_of(i * 16, 16), 16), :].astype(jnp.bfloat16)
-                )
-            return contract(jnp.concatenate(terms, axis=1), jnp.concatenate(hits, axis=1), 1, 1)
-
-        @pl.loop(0, WIN // group)
-        def _(at):
-            small[16:32, 0 : 3 * NB] += count_group(at)
+        spread_ref[w] = spread[...].astype(jnp.bfloat16)
 
     loads[3].wait()
     add_row(0, dqkv_ref[:, :width].astype(jnp.float32))
@@ -1005,7 +1023,7 @@
     small_ref[...] = small[...].astype(jnp.bfloat16)
 
 
-def backward_layer(layer, incoming, weights, vectors, kept, buckets):
+def backward_layer(layer, incoming, weights, vectors, kept):
     w_in, w_out, w_up, w_down = weights
     rows, width = incoming.shape
     hidden = w_up.shape[1]
@@ -1022,9 +1040,10 @@
             narrow,
             jax.ShapeDtypeStruct((rows, 3 * width), low),
             jax.ShapeDtypeStruct((64, width), low),
+            jax.ShapeDtypeStruct((rows // WIN, WIN * 16, WIN), low),
         ],
-        in_specs=[vmem] * 12 + [hbm] * 4,
-        out_specs=[vmem] * 6,
+        in_specs=[vmem] * 11 + [hbm] * 4,
+        out_specs=[vmem] * 7,
         scratch_shapes=[
             pltpu.VMEM(w_down.shape, low), pltpu.VMEM(w_up.shape, low),
             pltpu.VMEM(w_out.shape, low), pltpu.VMEM(w_in.shape, low),
@@ -1033,7 +1052,7 @@
             pltpu.SemaphoreType.DMA((4,)),
         ],
         compiler_params=pltpu.CompilerParams(vmem_limit_bytes=56 * 1024 * 1024),
-    )(incoming, n2, r2, slope, n1, r1, p, q, k, v, buckets, vectors, w_down, w_up, w_out, w_in)
+    )(incoming, n2, r2, slope, n1, r1, p, q, k, v, vectors, w_down, w_up, w_out, w_in)
 
 
 def local(
@@ -1064,16 +1083,19 @@
     )
     kept_list = [kept, kept_next]
     incoming = out_grad.astype(jnp.float32) * mlm_mask.astype(jnp.float32)[:, None]
-    lefts, rights, smalls = [], [], []
+    lefts, rights, smalls, spreads = [], [], [], []
     for layer in reversed(range(len(weights_list))):
         kept = kept_list[layer]
-        incoming, df, du, da, dqkv, small = backward_layer(
-            layer, incoming, weights_list[layer], shared[0], kept, layout_buckets
+        incoming, df, du, da, dqkv, small, spread = backward_layer(
+            layer, incoming, weights_list[layer], shared[0], kept
         )
         lefts = [kept[12], kept[3], kept[5], kept[9]] + lefts
         rights = [dqkv, da, du, df] + rights
         smalls = [small] + smalls
-    summed = sum_gradients(lefts, rights, smalls, shards, lax.axis_size("dp"))
+        spreads = [spread] + spreads
+    summed = sum_gradients(
+        lefts, rights, smalls, spreads, layout_buckets, shards, lax.axis_size("dp")
+    )
     return (outputs, incoming) + summed
 
 

time: 370 us -> 361 us (0.976)
  Pallas kernels: 355 us -> 350 us
  local copies, waits for them, and re-layouts: 11 us -> 6.55 us
    pallas_call x2, Pallas kernels: 49.5 us -> 38.9 us  [backward_layer(): pl.pallas_call(functools.partial(backward_kernel, layer), out_shape=[jax....]
    unnamed x19 -> x9, local copies, waits for them, and re-layouts: 9.31 us -> 3.44 us
where the time goes in v7:
time: 361 us; the launch traced here: 360 us
  Pallas kernels  350 us (97%)
  local copies, waits for them, and re-layouts  6.55 us (2%)
    pallas_call x1, Pallas kernels, reduce_gradients(): pl.pallas_call(functools.partial(reduce_kernel, high, chunk, segments, sh...  196 us
    pallas_call x1, Pallas kernels, open_layers(): pl.pallas_call(functools.partial(opening_kernel, tuple(items)), out_shape...  84.5 us
    pallas_call x2, Pallas kernels, backward_layer(): pl.pallas_call(functools.partial(backward_kernel, layer), out_shape=[jax....  38.9 us
    pallas_call x1, Pallas kernels, forward_layer(): pl.pallas_call(functools.partial(forward_kernel, layer), out_shape=outs,...  20.5 us
    pallas_call x1, Pallas kernels, widen(): pl.pallas_call(widen_kernel, grid=(arrays[0].shape[0], steps), out_shape=...  9.23 us

profile of v7, /device:TPU:0, one launch (start us, length us, event | category | flops | bytes accessed | tf_op | source)
XLA Modules:
  0.0 360.2 jit_solution(10241554501168421834)
XLA Ops:
  0.6 0.8 copy.36
  1.5 0.7 copy.29
  2.2 0.7 pad_maximum_fusion
  2.9 0.7 reshape.37
  3.6 0.6 fusion.4.refs_4_
  4.2 84.5 %shard_map.213 = (bf16[768,2304]{1,0:T(8,128)(2,1)}, bf16[768,768]{1,0:T(8,128)(2,1)}, bf16[768,3072]{1,0:T(8,128)(2,1)}, bf16[3072,768]{1,0:T(8,128)(2,1)}, bf1...) custom-call(bf16[2,192,2304]{2,1,0:T(8,128)(2,1)} %refs_0_.1, ...), custom_call_target="tpu_custom_call" | custom-call | tf_op jit(solution)/shard_map/pallas_call | solution.py:691
  88.7 0.0 copy-start.1
  88.7 0.0 copy-start
  88.8 20.5 %shard_map.214 = (bf16[2,256,768]{2,1,0:T(8,128)(2,1)}, bf16[256,768]{1,0:T(8,128)(2,1)}, bf16[256,768]{1,0:T(8,128)(2,1)}, bf16[256,768]{1,0:T(8,128)(2,1)}, bf...) custom-call(bf16[256,768]{1,0:T(8,128)(2,1)} %get-tuple-element.72.r, ...), custom_call_target="tpu_custom_call" | custom-call | tf_op jit(solution)/shard_map/pallas_call | solution.py:910
  109.3 1.0 convert_multiply_fusion.dz_ref
  110.3 19.6 %shard_map.215 = (f32[256,768]{1,0:T(8,128)}, bf16[256,768]{1,0:T(8,128)(2,1)}, bf16[256,3072]{1,0:T(8,128)(2,1)}, bf16[256,768]{1,0:T(8,128)(2,1)}, bf16[256,23...) custom-call(f32[256,768]{1,0:T(8,128)} %convert_multiply_fusion.dz_ref, ...), custom_call_target="tpu_custom_call" | custom-call | tf_op jit(solution)/shard_map/pallas_call | solution.py:1034
  129.8 19.4 %shard_map.216 = (f32[256,768]{1,0:T(8,128)}, bf16[256,768]{1,0:T(8,128)(2,1)}, bf16[256,3072]{1,0:T(8,128)(2,1)}, bf16[256,768]{1,0:T(8,128)(2,1)}, bf16[256,23...) custom-call(f32[256,768]{1,0:T(8,128)} %get-tuple-element.90.dz_ref, ...), custom_call_target="tpu_custom_call" | custom-call | tf_op jit(solution)/shard_map/pallas_call | solution.py:1034
  149.2 196.4 %shard_map.217 = (bf16[2,192,2304]{2,1,0:T(8,128)(2,1)}, bf16[2,192,768]{2,1,0:T(8,128)(2,1)}, bf16[2,192,3072]{2,1,0:T(8,128)(2,1)}, bf16[2,768,768]{2,1,0:T(8,128)(2,1)}, bf16[2,64,768]{2,1,0:T(8,128)(2,1)}) custom-call(bf16[768,256]{1,0:T(8,128)(2,1)} %get-tuple-element.105.refs_0_, bf16[768,256]{1,0:T(8,128)(2,1)} %get-tuple-element.106.refs_1_, ...), custom_call_target="tpu_custom_call" | custom-call | tf_op jit(solution)/shard_map/pallas_call | solution.py:390
  345.6 9.2 %shard_map.218 = (f32[2,192,2304]{2,1,0:T(8,128)}, f32[2,192,768]{2,1,0:T(8,128)}, f32[2,192,3072]{2,1,0:T(8,128)}, f32[2,768,768]{2,1,0:T(8,128)}) custom-call(bf16[2,192,2304]{2,1,0:T(8,128)(2,1)} %get-tuple-element.125.refs_0_, bf16[2,192,768]{2,1,0:T(8,128)(2,1)} %get-tuple-element.126.refs_1_, bf16[2,192,3072]{2,1,0:T(8,128)(2,1)} %get-tuple-element.127.refs_2_, ...), custom_call_target="tpu_custom_call" | custom-call | tf_op jit(solution)/shard_map/pallas_call | solution.py:426
  354.9 1.0 convert_element_type.17
  355.9 0.6 copy.40
  356.5 0.7 slice.17
  357.2 0.1 reshape.40
  357.3 0.1 dynamic-slice_bitcast_fusion
  357.4 0.7 copy.34
  358.1 0.7 slice.16
  358.8 0.1 constant_dynamic-slice_fusion
  358.9 0.6 copy.33
  359.5 0.7 constant_dynamic-slice_fusion.2
  (7 shorter events, 0.1 us)
Async XLA Ops:
  88.7 20.5 %copy-start.1 = (s32[256]{0:T(256)S(1)}, s32[256]{0:T(256)}, u32[]{:S(2)}) copy-start(s32[256]{0:T(256)} %param.16) | copy-start | bytes 3076
  88.7 20.5 %copy-start = (bf16[256,768]{1,0:T(8,128)(2,1)S(1)}, bf16[256,768]{1,0:T(8,128)(2,1)}, u32[]{:S(2)}) copy-start(bf16[256,768]{1,0:T(8,128)(2,1)} %param.15) | copy-start | bytes 1179652
